TPU v7x, 256 devices: a 4x2x16 block of a 4x16x16 slice. The times are simulated.
256 devices in a mesh: rep: 2 (over y), seq: 128 (over x, z, core).
Axes of the slice: x: 4, y: 2, z: 16, core: 2. Of those that a mesh axis runs over, the one named last changes fastest.
The devices are a block of a 4x16x16 slice.
Arguments:
- tokens: bfloat16 [131072, 768], P(('rep', 'seq')), parts along dimension 0, may hold values from -60 to 60
- w_qkv: bfloat16 [768, 2304], replicated, may hold values from -0.21875 to 0.21875
- w_gate: bfloat16 [768, 36], replicated, may hold values from -0.21875 to 0.21875
- w_out: bfloat16 [768, 768], replicated, may hold values from -0.21875 to 0.21875
- cmp_med: bfloat16 [2, 12, 16], replicated, may hold values from -1.5 to 1.5
- cmp_coarse: bfloat16 [2, 12, 256], replicated, may hold values from -0.375 to 0.375
- group_id: int32 [8192], P('rep'), parts along dimension 0, may hold values from 0 to 63, never falling along the last dimension, each value on 1 to 96 neighbouring positions
Outputs:
- layer_out: bfloat16 [131072, 768], P(('rep', 'seq')), parts along dimension 0
There are 2 independent parts, one for each index of `rep`. A program takes and returns all parts, laid end to end along the dimension named above; an argument that names none is the same for every part. Nothing has to cross between parts.
Inputs may be any that keep to these rules, and one draw needn't show every extreme that they name: `group_id`: never falling along the blocks; each sub-group holds 1 to 96 consecutive blocks, and one holds exactly that many.
All inputs are finite; a program needn't handle non-finite values.
Results may differ from a plain program's by a relative error of at most 0.012.
The roundings to bfloat16 on the way count: a program that leaves them out, or rounds other values in their place, can miss the bound.
Values may be sent and summed in bfloat16 or wider, within the bound.
No kernel may reach another device: no remote copies, remote signals or barrier semaphores. Data moves between devices by JAX's collectives and lax.ppermute only.
A program may use at most 128 MiB of HBM per device.

v0:
```python
import jax
import jax.numpy as jnp
from jax import lax
from jax.sharding import Mesh
from jax.sharding import PartitionSpec as P

WINDOW = 128
REACH = 3
SEQ = ("seq_0", "seq_1", "seq_2")
REP_SEQ = ("rep", "seq_0", "seq_1", "seq_2")


def shifted(block, axis, distance):
    devices = range(lax.axis_size(axis))
    route = [(i - distance, i) for i in devices if i - distance in devices]
    return lax.ppermute(block, axis, route)


def from_everyone(value, axis):
    size = lax.axis_size(axis)
    return lax.all_to_all(
        jnp.broadcast_to(value[None], (size, *value.shape)), axis, 0, 0, tiled=True
    )


def in_order(blocks, dim):
    shape = list(blocks.shape[1:])
    shape[dim] *= blocks.shape[0]
    return jnp.moveaxis(blocks, 0, dim).reshape(shape)


def whole_of(value, axes, dim):
    far, near = axes
    blocks = from_everyone(from_everyone(value, far), near)
    return in_order(blocks.swapaxes(0, 1).reshape(-1, *value.shape), dim)


def sent_together(arrays, axis, dim, along):
    both = jnp.concatenate(arrays, axis=along)
    result, at, finished = (whole_of(both, axis, dim), 0, [])
    for a in arrays:
        finished.append(lax.slice_in_dim(result, at, at + a.shape[along], axis=along))
        at += a.shape[along]
    return tuple(finished)


def compress(row_data, weights, head_count):
    block_len = weights.shape[1]
    blocks = row_data.shape[0] // block_len
    head_dim = row_data.shape[1] // head_count
    shaped = row_data.reshape(blocks, block_len, head_count, head_dim)
    packed = jnp.einsum("bjhd,hj->bhd", shaped, weights, preferred_element_type=jnp.float32)
    return packed.reshape(blocks, head_count * head_dim).astype(jnp.bfloat16)


def sink_attend(scores, visible, value_rows):
    masked = jnp.where(visible[:, None, :], scores, -1e30)
    row_peak = jnp.maximum(jnp.max(masked, axis=-1, keepdims=True), 0.0)
    exp_terms = jnp.where(visible[:, None, :], jnp.exp(masked - row_peak), 0.0)
    denominator = jnp.exp(-row_peak) + jnp.sum(exp_terms, axis=-1, keepdims=True)
    weights = (exp_terms / denominator).astype(jnp.bfloat16)
    return jnp.einsum("qhk,khd->qhd", weights, value_rows, preferred_element_type=jnp.float32)


def shards(tokens, w_qkv, w_gate, w_out, cmp_med, cmp_coarse, group_id):
    tok_rows = tokens.shape[0]
    head_count = cmp_med.shape[1]
    med_len = cmp_med.shape[2]
    coarse_len = cmp_coarse.shape[2]
    inner = w_out.shape[0]
    head_dim = inner // head_count
    scale = head_dim ** (-0.5)
    block_rows = min(512, tok_rows)
    med_blocks = tok_rows // med_len
    device_pos = lax.axis_index(SEQ)
    row_start = device_pos * tok_rows
    projected = jnp.dot(tokens, w_qkv, preferred_element_type=jnp.float32).astype(jnp.bfloat16)
    queries = projected[:, :inner]
    key_rows = projected[:, inner : 2 * inner]
    value_rows = projected[:, 2 * inner :]
    gate_values = jax.nn.sigmoid(jnp.dot(tokens, w_gate, preferred_element_type=jnp.float32))
    med_keys = compress(key_rows, cmp_med[0], head_count)
    med_values = compress(value_rows, cmp_med[1], head_count)
    coarse_keys = compress(key_rows, cmp_coarse[0], head_count)
    coarse_values = compress(value_rows, cmp_coarse[1], head_count)
    key_tail = key_rows[tok_rows - WINDOW :]
    value_tail = value_rows[tok_rows - WINDOW :]
    arrived = shifted((med_keys, med_values, key_tail, value_tail), SEQ, 1)
    nearest = (arrived[0], arrived[1])
    rim_keys, rim_values = (arrived[2], arrived[3])
    reached = [(med_keys, med_values), (nearest[0], nearest[1])]
    while len(reached) < REACH + 1:
        count_now = len(reached)
        stacked = (
            jnp.concatenate([pair_kv[0] for pair_kv in reached], 0),
            jnp.concatenate([pair_kv[1] for pair_kv in reached], 0),
        )
        landed = shifted((stacked[0], stacked[1]), SEQ, count_now)
        for offset in range(count_now):
            reached.append(
                (
                    landed[0][offset * med_blocks : (offset + 1) * med_blocks],
                    landed[1][offset * med_blocks : (offset + 1) * med_blocks],
                )
            )
    reached = reached[: REACH + 1]
    near_keys = jnp.concatenate(
        [reached[distance][0] for distance in range(REACH, -1, -1)], 0
    ).reshape(-1, head_count, head_dim)
    near_values = jnp.concatenate(
        [reached[distance][1] for distance in range(REACH, -1, -1)], 0
    ).reshape(-1, head_count, head_dim)
    padded_groups = jnp.concatenate([jnp.full((REACH * med_blocks,), -1, jnp.int32), group_id], 0)
    key_groups = lax.dynamic_slice_in_dim(
        padded_groups, device_pos * med_blocks, (REACH + 1) * med_blocks, 0
    )
    key_blocks = (device_pos - REACH) * med_blocks + jnp.arange(
        (REACH + 1) * med_blocks, dtype=jnp.int32
    )
    token_groups = jnp.repeat(
        lax.dynamic_slice_in_dim(group_id, device_pos * med_blocks, med_blocks, 0), med_len
    )
    ext_keys = jnp.concatenate([rim_keys, key_rows], 0)
    ext_values = jnp.concatenate([rim_values, value_rows], 0)
    all_keys, all_values = sent_together(
        (coarse_keys, coarse_values), (("seq_0", "seq_1"), "seq_2"), 0, 1
    )
    all_keys = all_keys.reshape(-1, head_count, head_dim)
    all_values = all_values.reshape(-1, head_count, head_dim)
    coarse_index = jnp.arange(all_keys.shape[0], dtype=jnp.int32)
    block_index = 0
    low_row = block_index * block_rows
    positions = row_start + low_row + jnp.arange(block_rows, dtype=jnp.int32)
    query_block = queries.reshape(block_rows, head_count, head_dim)
    scores = (
        jnp.einsum("qhd,khd->qhk", query_block, all_keys, preferred_element_type=jnp.float32)
        * scale
    )
    visible = coarse_index[None, :] * coarse_len + coarse_len - 1 <= positions[:, None]
    coarse_parts = sink_attend(scores, visible, all_values)
    block_index = 0
    low_row = block_index * block_rows
    positions = row_start + low_row + jnp.arange(block_rows, dtype=jnp.int32)
    query_block = queries.reshape(block_rows, head_count, head_dim)
    win_keys = ext_keys.reshape(-1, head_count, head_dim)
    win_values = ext_values.reshape(-1, head_count, head_dim)
    key_pos = row_start + low_row - WINDOW + jnp.arange(block_rows + WINDOW, dtype=jnp.int32)
    visible = (
        (key_pos[None, :] <= positions[:, None])
        & (key_pos[None, :] > positions[:, None] - WINDOW)
        & (key_pos[None, :] >= 0)
    )
    scores = (
        jnp.einsum("qhd,khd->qhk", query_block, win_keys, preferred_element_type=jnp.float32)
        * scale
    )
    masked = jnp.where(visible[:, None, :], scores, -1e30)
    row_peak = jnp.max(masked, axis=-1, keepdims=True)
    exp_terms = jnp.where(visible[:, None, :], jnp.exp(masked - row_peak), 0.0)
    weights_low = (exp_terms / jnp.sum(exp_terms, axis=-1, keepdims=True)).astype(jnp.bfloat16)
    window_out = jnp.einsum(
        "qhk,khd->qhd", weights_low, win_values, preferred_element_type=jnp.float32
    )
    visible_med = (key_groups[None, :] == token_groups[:, None]) & (
        key_blocks[None, :] * med_len + med_len - 1 <= positions[:, None]
    )
    med_scores = (
        jnp.einsum("qhd,khd->qhk", query_block, near_keys, preferred_element_type=jnp.float32)
        * scale
    )
    medium_out = sink_attend(med_scores, visible_med, near_values)
    mixed_heads = (
        gate_values[:, :head_count, None] * window_out
        + gate_values[:, head_count : 2 * head_count, None] * medium_out
        + gate_values[:, 2 * head_count :, None] * coarse_parts
    )
    mixed_parts = mixed_heads.reshape(block_rows, inner).astype(jnp.bfloat16)
    return jnp.dot(mixed_parts, w_out, preferred_element_type=jnp.float32).astype(jnp.bfloat16)


def solution(mesh):
    torus = Mesh(
        mesh.devices.reshape(mesh.shape["rep"], 4, 16, 2), ("rep", "seq_0", "seq_1", "seq_2")
    )
    return jax.shard_map(
        shards,
        mesh=torus,
        in_specs=(P(REP_SEQ, None), P(), P(), P(), P(), P(), P("rep")),
        out_specs=P(REP_SEQ, None),
        check_vma=False,
    )
```

profile of v0, /device:TPU:33, one launch (start us, length us, event | category | flops | bytes accessed | tf_op | source)
XLA Modules:
  0.0 169.6 jit_solution(12995888847905951643)
XLA Ops:
  0.0 2.0 %copy-done = bf16[768,2304]{1,0:T(8,128)(2,1)S(1)} copy-done((bf16[768,2304]{1,0:T(8,128)(2,1)S(1)}, bf16[768,2304]{1,0:T(8,128)(2,1)}, u32[]{:S(2)}) %copy-start) | copy-done | bytes 3538968
  2.0 3.1 %convolution_convert_fusion = bf16[512,2304]{1,0:T(8,128)(2,1)S(1)} fusion(bf16[512,768]{1,0:T(8,128)(2,1)} %param.7, bf16[768,2304]{1,0:T(8,128)(2,1)S(1)} %copy-done), kind=kOutput, calls=%fused_computation.13 | convolution fusion | flops 1813118976 | bytes 6684672 | tf_op jit(solution)/shard_map/dot_general | solution.py:77
  5.2 1.4 copy-done.6
  6.6 1.5 fusion.43
  8.0 2.3 %copy.53 = bf16[512,768]{0,1:T(8,128)(2,1)} copy(bf16[512,768]{1,0:T(8,128)(2,1)} %get-tuple-element.9) | data formatting | bytes 1572864 | tf_op jit(solution)/shard_map/slice | solution.py:80
  10.4 2.9 %reshape.252 = bf16[2,256,12,64]{1,0,3,2:T(2,128)(2,1)} reshape(bf16[512,768]{0,1:T(8,128)(2,1)} %copy.53) | data formatting | bytes 1572864 | tf_op jit(solution)/shard_map/reshape | solution.py:51
  13.9 1.5 fusion.22
  16.1 2.3 %copy.51 = bf16[512,768]{0,1:T(8,128)(2,1)} copy(bf16[512,768]{1,0:T(8,128)(2,1)} %get-tuple-element.8) | data formatting | bytes 1572864 | tf_op jit(solution)/shard_map/slice | solution.py:79
  18.5 2.9 %reshape.251 = bf16[2,256,12,64]{1,0,3,2:T(2,128)(2,1)} reshape(bf16[512,768]{0,1:T(8,128)(2,1)} %copy.51) | data formatting | bytes 1572864 | tf_op jit(solution)/shard_map/reshape | solution.py:51
  21.4 1.5 fusion.24
  25.3 29.6 %all-to-all-start = ((bf16[64,2,1536]{2,1,0:T(2,128)(2,1)}), bf16[64,2,1536]{2,1,0:T(2,128)(2,1)}, u32[]{:S(2)}, u32[]{:S(2)}) async-start(bf16[64,2,1536]{2,1,0:T(2,128)(2,1)} %broadcast_in_dim.102), calls=%async_computation | async-start | bytes 786432 | tf_op jit(solution)/shard_map/all_to_all | solution.py:21
  54.9 1.8 %fusion.42 = (bf16[128,768]{1,0:T(8,128)(2,1)}, bf16[128,768]{1,0:T(8,128)(2,1)}) fusion(bf16[512,2304]{1,0:T(8,128)(2,1)} %copy-done.6), kind=kLoop, calls=%fused_computation.85 | loop fusion | bytes 786432 | tf_op jit(solution)/shard_map/slice | solution.py:86
  56.8 3.1 %collective-permute-start = (bf16[128,768]{1,0:T(8,128)(2,1)}, bf16[128,768]{1,0:T(8,128)(2,1)}, u32[]{:S(2)}, u32[]{:S(2)}) collective-permute-start(bf16[128,768]{1,0:T(8,128)(2,1)} %get-tuple-element.6), channel_id=1, source_target_pairs={{0,1},{1,2},{2,3},{3,4},{4,5},{5,6},{6,7},{7,8},{8,9},{9,10},{10,1... | collective-permute-start | bytes 589832 | tf_op jit(solution)/shard_map/ppermute | solution.py:16
  59.9 2.0 %collective-permute-start.1 = (bf16[128,768]{1,0:T(8,128)(2,1)}, bf16[128,768]{1,0:T(8,128)(2,1)}, u32[]{:S(2)}, u32[]{:S(2)}) collective-permute-start(bf16[128,768]{1,0:T(8,128)(2,1)} %get-tuple-element.5), channel_id=1, source_target_pairs={{0,1},{1,2},{2,3},{3,4},{4,5},{5,6},{6,7},{7,8},{8,9},{9,10},{10,1... | collective-permute-start | bytes 589832 | tf_op jit(solution)/shard_map/ppermute | solution.py:16
  61.8 3.8 %reshape.247 = bf16[32,16,12,64]{3,2,1,0:T(8,128)(2,1)} reshape(bf16[512,768]{1,0:T(8,128)(2,1)} %get-tuple-element.9) | data formatting | bytes 1572864 | tf_op jit(solution)/shard_map/reshape | solution.py:51
  65.6 2.8 %fusion.16 = bf16[12,1,32,64]{3,1,2,0:T(2,128)(2,1)} fusion(bf16[32,16,12,64]{3,2,1,0:T(8,128)(2,1)} %reshape.247, bf16[12,16,1,1]{1,0,2,3:T(8,128)(2,1)S(1)} %get-tuple-element.32), kind=kOutput, calls=%fused_computation.29 | convolution fusion | flops 786432 | bytes 835968 | tf_op jit(solution)/shard_map/bjhd,hj->bhd/dot_general | solution.py:52
  68.5 1.8 %copy.62 = bf16[12,1,32,64]{2,3,0,1:T(8,128)(2,1)} copy(bf16[12,1,32,64]{3,1,2,0:T(2,128)(2,1)} %fusion.16) | data formatting | bytes 98304 | tf_op jit(solution)/shard_map/bjhd,hj->bhd/dot_general | solution.py:52
  70.2 3.5 %collective-permute-start.2 = (bf16[32,768]{0,1:T(8,128)(2,1)}, bf16[32,768]{0,1:T(8,128)(2,1)}, u32[]{:S(2)}, u32[]{:S(2)}) collective-permute-start(bf16[32,768]{0,1:T(8,128)(2,1)} %bitcast.129), channel_id=1, source_target_pairs={{0,1},{1,2},{2,3},{3,4},{4,5},{5,6},{6,7},{7,8},{8,9},{9,10},{10,1... | collective-permute-start | bytes 147464 | tf_op jit(solution)/shard_map/ppermute | solution.py:16
  73.7 3.8 %reshape.249 = bf16[32,16,12,64]{3,2,1,0:T(8,128)(2,1)} reshape(bf16[512,768]{1,0:T(8,128)(2,1)} %get-tuple-element.8) | data formatting | bytes 1572864 | tf_op jit(solution)/shard_map/reshape | solution.py:51
  77.5 2.8 %fusion.14 = bf16[12,1,32,64]{3,1,2,0:T(2,128)(2,1)} fusion(bf16[32,16,12,64]{3,2,1,0:T(8,128)(2,1)} %reshape.249, bf16[12,16,1,1]{1,0,2,3:T(8,128)(2,1)S(1)} %get-tuple-element.31), kind=kOutput, calls=%fused_computation.27 | convolution fusion | flops 786432 | bytes 835968 | tf_op jit(solution)/shard_map/bjhd,hj->bhd/dot_general | solution.py:52
  80.3 1.7 %copy.65 = bf16[12,1,32,64]{2,3,0,1:T(8,128)(2,1)} copy(bf16[12,1,32,64]{3,1,2,0:T(2,128)(2,1)} %fusion.14) | data formatting | bytes 98304 | tf_op jit(solution)/shard_map/bjhd,hj->bhd/dot_general | solution.py:52
  82.1 2.1 %collective-permute-start.4 = (bf16[32,768]{0,1:T(8,128)(2,1)}, bf16[32,768]{0,1:T(8,128)(2,1)}, u32[]{:S(2)}, u32[]{:S(2)}) collective-permute-start(bf16[32,768]{0,1:T(8,128)(2,1)} %bitcast.132), channel_id=1, source_target_pairs={{0,1},{1,2},{2,3},{3,4},{4,5},{5,6},{6,7},{7,8},{8,9},{9,10},{10,1... | collective-permute-start | bytes 147464 | tf_op jit(solution)/shard_map/ppermute | solution.py:16
  88.6 1.5 fusion.21
  90.8 1.5 broadcast_compare_fusion
  93.0 1.8 %and_and_fusion = pred[512,640]{0,1:T(8,128)(4,1)} fusion(s32[512]{0:T(512)} %broadcast_add_fusion, s32[512]{0:T(512)} %iota_add_fusion.1, s32[640]{0:T(1024)} %iota_add_fusion, pred[640]{0:T(1024)(128)(4,1)} %broadcast_compare_fusion.1), kind=kLoop, calls=%fused_computation.33 | loop fusion | flops 1310720 | bytes 334976 | tf_op jit(solution)/shard_map/and | solution.py:149
  94.8 1.4 compare_and_fusion
  96.3 2.3 %copy.46 = bf16[512,768]{0,1:T(8,128)(2,1)} copy(bf16[512,768]{1,0:T(8,128)(2,1)} %get-tuple-element.7) | data formatting | bytes 1572864 | tf_op jit(solution)/shard_map/slice | solution.py:78
  99.8 3.1 %collective-permute-start.5 = (bf16[64,768]{0,1:T(8,128)(2,1)S(1)}, bf16[64,768]{0,1:T(8,128)(2,1)S(1)}, u32[]{:S(2)}, u32[]{:S(2)}) collective-permute-start(bf16[64,768]{0,1:T(8,128)(2,1)S(1)} %pad_maximum_fusion.4), channel_id=1, source_target_pairs={{0,2},{1,3},{2,4},{3,5},{4,6},{5,7},{6,8},{7,9},{8,10},{9,11},{10,... | collective-permute-start | bytes 294920 | tf_op jit(solution)/shard_map/ppermute | solution.py:16
  104.1 4.5 %collective-permute-start.3 = (bf16[64,768]{0,1:T(8,128)(2,1)S(1)}, bf16[64,768]{0,1:T(8,128)(2,1)S(1)}, u32[]{:S(2)}, u32[]{:S(2)}) collective-permute-start(bf16[64,768]{0,1:T(8,128)(2,1)S(1)} %pad_maximum_fusion.2), channel_id=1, source_target_pairs={{0,2},{1,3},{2,4},{3,5},{4,6},{5,7},{6,8},{7,9},{8,10},{9,11},{10,... | collective-permute-start | bytes 294920 | tf_op jit(solution)/shard_map/ppermute | solution.py:16
  110.0 1.6 fusion.9
  112.6 2.5 %pad_maximum_fusion.3 = bf16[128,768]{0,1:T(8,128)(2,1)} fusion(bf16[32,768]{0,1:T(8,128)(2,1)S(1)} %bitcast.131, bf16[32,768]{0,1:T(8,128)(2,1)} %collective-permute-done.2, bf16[32,768]{0,1:T(8,128)(2,1)S(1)} %get-tuple-element.15, bf16[32,768]{0,1:T(8,128)(2,1)S(1)} %get-tuple-element.14), kind=kLoop, calls=%fused_computation.49 | loop fusion | flops 786432 | bytes 393216 | tf_op jit(solution)/shard_map/concatenate | solution.py:110
  115.7 2.4 %pad_maximum_fusion = (bf16[640,768]{1,0:T(8,128)(2,1)}, bf16[640,768]{1,0:T(8,128)(2,1)}) fusion(bf16[512,768]{1,0:T(8,128)(2,1)S(1)} %copy-done.4, bf16[128,768]{1,0:T(8,128)(2,1)} %collective-permute-done, bf16[512,768]{1,0:T(8,128)(2,1)S(1)} %copy-done.3, bf16[128,768]{1,0:T(8,128)(2,1)} %collective-permute-done.1), kind=kLoop, calls=%fused_computation.38 | loop fusion | flops 3932160 | bytes 3932160 | tf_op jit(solution)/shard_map/concatenate | solution.py:124
  118.2 2.2 %copy.44 = bf16[640,768]{0,1:T(8,128)(2,1)} copy(bf16[640,768]{1,0:T(8,128)(2,1)} %get-tuple-element.29) | data formatting | bytes 1966080 | tf_op jit(solution)/shard_map/concatenate | solution.py:124
  120.4 2.2 %copy.45 = bf16[640,768]{0,1:T(8,128)(2,1)} copy(bf16[640,768]{1,0:T(8,128)(2,1)} %get-tuple-element.30) | data formatting | bytes 1966080 | tf_op jit(solution)/shard_map/concatenate | solution.py:123
  122.7 12.1 %fusion.50 = (f32[512,12]{0,1:T(8,128)}, f32[512,12,640]{0,2,1:T(8,128)}) fusion(pred[512,640]{0,1:T(8,128)(4,1)} %and_and_fusion, bf16[640,12,64]{0,2,1:T(8,128)(2,1)} %bitcast.137, bf16[512,12,64]{0,2,1:T(8,128)(2,1)} %bitcast.125), kind=kOutput, calls=%fused_computation.93 | convolution fusion | flops 522977920 | bytes 17850368 | tf_op jit(solution)/shard_map/sub | solution.py:159
  134.8 8.3 %fusion.5 = f32[12,64,512]{2,1,0:T(8,128)} fusion(bf16[640,12,64]{0,2,1:T(8,128)(2,1)} %bitcast.136, f32[512,12,640]{0,2,1:T(8,128)} %get-tuple-element.26, f32[512,12]{0,1:T(8,128)} %get-tuple-element.25), kind=kOutput, calls=%fused_computation.8 | convolution fusion | flops 511180800 | bytes 18309120 | tf_op jit(solution)/shard_map/qhk,khd->qhd/dot_general | solution.py:161
  143.1 1.4 broadcast_in_dim.103
  144.5 5.2 %all_to_all.10 = bf16[2,64,2,1536]{3,2,1,0:T(2,128)(2,1)S(1)} all-to-all(bf16[2,64,2,1536]{3,2,1,0:T(2,128)(2,1)S(1)} %broadcast_in_dim.103), channel_id=1, replica_groups=mesh['rep'=2,'seq_0'=4,'seq_1'=16,'seq_2'=2] {'seq_2'}, dimensions={0} | all-to-all | bytes 1572864 | tf_op jit(solution)/shard_map/all_to_all | solution.py:21
  149.7 1.4 copy.55
  151.1 3.0 %reshape_reshape.3 = bf16[256,1536]{1,0:T(8,128)(2,1)} reshape(bf16[64,2,2,1536]{3,2,1,0:T(2,128)(2,1)} %copy.55) | data formatting | bytes 1572864 | tf_op jit(solution)/shard_map/reshape;reshape | solution.py:29
  154.0 2.0 %fusion.44 = (bf16[256,768]{1,0:T(8,128)(2,1)}, bf16[256,768]{1,0:T(8,128)(2,1)}) fusion(bf16[256,1536]{1,0:T(8,128)(2,1)} %reshape_reshape.3), kind=kLoop, calls=%fused_computation.87 | loop fusion | bytes 1572864 | tf_op jit(solution)/shard_map/slice | solution.py:42
  156.1 1.9 %copy.56 = bf16[256,768]{0,1:T(8,128)(2,1)} copy(bf16[256,768]{1,0:T(8,128)(2,1)} %get-tuple-element.11) | data formatting | bytes 786432 | tf_op jit(solution)/shard_map/slice | solution.py:42
  158.0 1.9 %copy.57 = bf16[256,768]{0,1:T(8,128)(2,1)} copy(bf16[256,768]{1,0:T(8,128)(2,1)} %get-tuple-element.10) | data formatting | bytes 786432 | tf_op jit(solution)/shard_map/slice | solution.py:42
  159.9 2.4 %fusion.6 = (f32[512,12]{0,1:T(8,128)S(1)}, f32[12,256,512]{2,1,0:T(8,128)S(1)}) fusion(pred[512,256]{0,1:T(8,128)(4,1)} %broadcast_compare_fusion, bf16[256,12,64]{0,2,1:T(8,128)(2,1)} %bitcast.135, bf16[512,12,64]{0,2,1:T(8,128)(2,1)} %bitcast.126), kind=kOutput, calls=%fused_computation.12 | convolution fusion | flops 206039040 | bytes 7626752 | tf_op jit(solution)/shard_map/qhd,khd->qhk/dot_general | solution.py:136
  162.4 1.5 fusion.7
  164.0 2.1 %fusion.8 = f32[12,64,512]{2,1,0:T(8,128)S(1)} fusion(bf16[256,12,64]{0,2,1:T(8,128)(2,1)S(1)} %bitcast.139, f32[12,256,512]{2,1,0:T(8,128)S(1)} %get-tuple-element.24, f32[512,12]{0,1:T(8,128)S(1)} %exponential_add_fusion, f32[512,12]{0,1:T(8,128)S(1)} %broadcast_maximum_fusion, pred[512,256]{0,1:T(8,128)(4,1)S(1)} %copy-done.8), kind=kOutput, calls=%fused_computation.18 | convolution fusion | flops 210763776 | bytes 8437760 | tf_op jit(solution)/shard_map/qhk,khd->qhd/dot_general | solution.py:62
  166.5 1.4 fusion.12
  167.9 1.7 %convolution_convert_fusion.1 = bf16[512,768]{1,0:T(8,128)(2,1)} fusion(bf16[512,768]{0,1:T(8,128)(2,1)S(1)} %bitcast.143, bf16[768,768]{1,0:T(8,128)(2,1)S(1)} %copy-done.22), kind=kOutput, calls=%fused_computation.32 | convolution fusion | flops 604372992 | bytes 2752512 | tf_op jit(solution)/shard_map/dot_general | solution.py:178
  (83 shorter events, 15.3 us)
Async XLA Ops:
  0.0 2.0 %copy-start = (bf16[768,2304]{1,0:T(8,128)(2,1)S(1)}, bf16[768,2304]{1,0:T(8,128)(2,1)}, u32[]{:S(2)}) copy-start(bf16[768,2304]{1,0:T(8,128)(2,1)} %param.8) | copy-start | bytes 10616836
  5.1 1.4 copy-start.6
  6.6 6.7 %copy-start.15 = (bf16[2,12,256]{2,0,1:T(2,128)(2,1)S(1)}, bf16[2,12,256]{2,0,1:T(2,128)(2,1)}, u32[]{:S(2)}) copy-start(bf16[2,12,256]{2,0,1:T(2,128)(2,1)} %param.12) | copy-start | bytes 36868
  16.1 5.3 %copy-start.21 = (bf16[12,256,1,1]{1,0,2,3:T(8,128)(2,1)S(1)}, bf16[12,256,1,1]{1,0,2,3:T(8,128)(2,1)}, u32[]{:S(2)}) copy-start(bf16[12,256,1,1]{1,0,2,3:T(8,128)(2,1)} %get-tuple-element.34) | copy-start | bytes 18436
  21.4 44.2 %copy-start.20 = (bf16[2,12,16]{2,0,1:T(2,128)(2,1)S(1)}, bf16[2,12,16]{2,0,1:T(2,128)(2,1)}, u32[]{:S(2)}) copy-start(bf16[2,12,16]{2,0,1:T(2,128)(2,1)} %param.11) | copy-start | bytes 2308
  25.3 117.8 %all-to-all-start = ((bf16[64,2,1536]{2,1,0:T(2,128)(2,1)}), bf16[64,2,1536]{2,1,0:T(2,128)(2,1)}, u32[]{:S(2)}, u32[]{:S(2)}) async-start(bf16[64,2,1536]{2,1,0:T(2,128)(2,1)} %broadcast_in_dim.102), calls=%async_computation | async-start | bytes 786432 | tf_op jit(solution)/shard_map/all_to_all | solution.py:21
  56.8 59.0 %collective-permute-start = (bf16[128,768]{1,0:T(8,128)(2,1)}, bf16[128,768]{1,0:T(8,128)(2,1)}, u32[]{:S(2)}, u32[]{:S(2)}) collective-permute-start(bf16[128,768]{1,0:T(8,128)(2,1)} %get-tuple-element.6), channel_id=1, source_target_pairs={{0,1},{1,2},{2,3},{3,4},{4,5},{5,6},{6,7},{7,8},{8,9},{9,10},{10,1... | collective-permute-start | bytes 589832 | tf_op jit(solution)/shard_map/ppermute | solution.py:16
  59.9 55.9 %collective-permute-start.1 = (bf16[128,768]{1,0:T(8,128)(2,1)}, bf16[128,768]{1,0:T(8,128)(2,1)}, u32[]{:S(2)}, u32[]{:S(2)}) collective-permute-start(bf16[128,768]{1,0:T(8,128)(2,1)} %get-tuple-element.5), channel_id=1, source_target_pairs={{0,1},{1,2},{2,3},{3,4},{4,5},{5,6},{6,7},{7,8},{8,9},{9,10},{10,1... | collective-permute-start | bytes 589832 | tf_op jit(solution)/shard_map/ppermute | solution.py:16
  70.2 32.7 %collective-permute-start.2 = (bf16[32,768]{0,1:T(8,128)(2,1)}, bf16[32,768]{0,1:T(8,128)(2,1)}, u32[]{:S(2)}, u32[]{:S(2)}) collective-permute-start(bf16[32,768]{0,1:T(8,128)(2,1)} %bitcast.129), channel_id=1, source_target_pairs={{0,1},{1,2},{2,3},{3,4},{4,5},{5,6},{6,7},{7,8},{8,9},{9,10},{10,1... | collective-permute-start | bytes 147464 | tf_op jit(solution)/shard_map/ppermute | solution.py:16
  82.1 16.5 %collective-permute-start.4 = (bf16[32,768]{0,1:T(8,128)(2,1)}, bf16[32,768]{0,1:T(8,128)(2,1)}, u32[]{:S(2)}, u32[]{:S(2)}) collective-permute-start(bf16[32,768]{0,1:T(8,128)(2,1)} %bitcast.132), channel_id=1, source_target_pairs={{0,1},{1,2},{2,3},{3,4},{4,5},{5,6},{6,7},{7,8},{8,9},{9,10},{10,1... | collective-permute-start | bytes 147464 | tf_op jit(solution)/shard_map/ppermute | solution.py:16
  98.6 11.5 %copy-start.5 = (bf16[512,768]{0,1:T(8,128)(2,1)S(1)}, bf16[512,768]{0,1:T(8,128)(2,1)}, u32[]{:S(2)}) copy-start(bf16[512,768]{0,1:T(8,128)(2,1)} %copy.46) | copy-start | bytes 2359300
  99.8 8.8 %collective-permute-start.5 = (bf16[64,768]{0,1:T(8,128)(2,1)S(1)}, bf16[64,768]{0,1:T(8,128)(2,1)S(1)}, u32[]{:S(2)}, u32[]{:S(2)}) collective-permute-start(bf16[64,768]{0,1:T(8,128)(2,1)S(1)} %pad_maximum_fusion.4), channel_id=1, source_target_pairs={{0,2},{1,3},{2,4},{3,5},{4,6},{5,7},{6,8},{7,9},{8,10},{9,11},{10,... | collective-permute-start | bytes 294920 | tf_op jit(solution)/shard_map/ppermute | solution.py:16
  104.1 7.6 %copy-start.9 = (pred[512,128]{0,1:T(8,128)(4,1)S(1)}, pred[512,128]{0,1:T(8,128)(4,1)}, u32[]{:S(2)}) copy-start(pred[512,128]{0,1:T(8,128)(4,1)} %compare_and_fusion) | copy-start | bytes 196612
  104.1 8.4 %collective-permute-start.3 = (bf16[64,768]{0,1:T(8,128)(2,1)S(1)}, bf16[64,768]{0,1:T(8,128)(2,1)S(1)}, u32[]{:S(2)}, u32[]{:S(2)}) collective-permute-start(bf16[64,768]{0,1:T(8,128)(2,1)S(1)} %pad_maximum_fusion.2), channel_id=1, source_target_pairs={{0,2},{1,3},{2,4},{3,5},{4,6},{5,7},{6,8},{7,9},{8,10},{9,11},{10,... | collective-permute-start | bytes 294920 | tf_op jit(solution)/shard_map/ppermute | solution.py:16
  110.0 2.6 %copy-start.7 = (bf16[12,1,32,64]{2,3,0,1:T(8,128)(2,1)S(1)}, bf16[12,1,32,64]{2,3,0,1:T(8,128)(2,1)}, u32[]{:S(2)}) copy-start(bf16[12,1,32,64]{2,3,0,1:T(8,128)(2,1)} %copy.62) | copy-start | bytes 147460
  111.6 6.6 %copy-start.1 = (f32[12,128,512]{2,1,0:T(8,128)}, f32[12,128,512]{2,1,0:T(8,128)S(1)}, u32[]{:S(2)}) copy-start(f32[12,128,512]{2,1,0:T(8,128)S(1)} %get-tuple-element.28) | copy-start | bytes 9437188
  111.6 4.1 %copy-start.3 = (bf16[512,768]{1,0:T(8,128)(2,1)S(1)}, bf16[512,768]{1,0:T(8,128)(2,1)}, u32[]{:S(2)}) copy-start(bf16[512,768]{1,0:T(8,128)(2,1)} %get-tuple-element.8) | copy-start | bytes 2359300
  111.6 4.1 %copy-start.4 = (bf16[512,768]{1,0:T(8,128)(2,1)S(1)}, bf16[512,768]{1,0:T(8,128)(2,1)}, u32[]{:S(2)}) copy-start(bf16[512,768]{1,0:T(8,128)(2,1)} %get-tuple-element.9) | copy-start | bytes 2359300
  111.7 6.5 %copy-start.13 = (f32[512,12]{0,1:T(8,128)}, f32[512,12]{0,1:T(8,128)S(1)}, u32[]{:S(2)}) copy-start(f32[512,12]{0,1:T(8,128)S(1)} %broadcast_maximum_fusion.1) | copy-start | bytes 73732
  159.9 2.5 %copy-start.8 = (pred[512,256]{0,1:T(8,128)(4,1)S(1)}, pred[512,256]{0,1:T(8,128)(4,1)}, u32[]{:S(2)}) copy-start(pred[512,256]{0,1:T(8,128)(4,1)} %broadcast_compare_fusion) | copy-start | bytes 393220
  162.4 1.5 copy-start.11
  163.9 2.2 %copy-start.2 = (f32[12,128,512]{2,1,0:T(8,128)S(1)}, f32[12,128,512]{2,1,0:T(8,128)}, u32[]{:S(2)}) copy-start(f32[12,128,512]{2,1,0:T(8,128)} %copy-done.1) | copy-start | bytes 9437188
  163.9 2.2 %copy-start.10 = (pred[512,128]{0,1:T(8,128)(4,1)S(1)}, pred[512,128]{0,1:T(8,128)(4,1)}, u32[]{:S(2)}) copy-start(pred[512,128]{0,1:T(8,128)(4,1)} %compare_and_fusion) | copy-start | bytes 196612
  164.0 2.2 %copy-start.12 = (bf16[128,768]{0,1:T(8,128)(2,1)S(1)}, bf16[128,768]{0,1:T(8,128)(2,1)}, u32[]{:S(2)}) copy-start(bf16[128,768]{0,1:T(8,128)(2,1)} %pad_maximum_fusion.3) | copy-start | bytes 589828
  164.0 2.2 %copy-start.14 = (f32[512,12]{0,1:T(8,128)S(1)}, f32[512,12]{0,1:T(8,128)}, u32[]{:S(2)}) copy-start(f32[512,12]{0,1:T(8,128)} %copy-done.13) | copy-start | bytes 73732
  164.0 2.2 %copy-start.16 = (f32[512,12]{0,1:T(8,128)S(1)}, f32[512,12]{0,1:T(8,128)}, u32[]{:S(2)}) copy-start(f32[512,12]{0,1:T(8,128)} %exponential_add_fusion.1) | copy-start | bytes 73732
  164.0 2.2 %copy-start.17 = (f32[512,12]{0,1:T(8,128)S(1)}, f32[512,12]{0,1:T(8,128)}, u32[]{:S(2)}) copy-start(f32[512,12]{0,1:T(8,128)} %get-tuple-element.16) | copy-start | bytes 73732
  164.0 2.2 %copy-start.18 = (f32[512,12]{0,1:T(8,128)S(1)}, f32[512,12]{0,1:T(8,128)}, u32[]{:S(2)}) copy-start(f32[512,12]{0,1:T(8,128)} %get-tuple-element.17) | copy-start | bytes 73732
  164.0 2.2 %copy-start.19 = (f32[512,12]{0,1:T(8,128)S(1)}, f32[512,12]{0,1:T(8,128)}, u32[]{:S(2)}) copy-start(f32[512,12]{0,1:T(8,128)} %get-tuple-element.18) | copy-start | bytes 73732
  164.0 2.5 %copy-start.23 = (f32[12,64,512]{2,1,0:T(8,128)S(1)}, f32[12,64,512]{2,1,0:T(8,128)}, u32[]{:S(2)}) copy-start(f32[12,64,512]{2,1,0:T(8,128)} %fusion.5) | copy-start | bytes 4718596
  166.5 1.5 copy-start.22
where the time goes:
time: 172 us; the launch traced here: 170 us
  local copies, waits for them, and re-layouts  52.4 us (30%)
  starting transfers between devices  47.9 us (28%)
  matrix products  43 us (25%)
  other arithmetic  20.6 us (12%)
  blocking collectives  5.17 us (3%)
    all_to_all x1, starting transfers between devices, from_everyone(): lax.all_to_all(jnp.broadcast_to(value[None], (size, *value.shape)), axis,...  29.6 us
    ppermute x6, starting transfers between devices, shifted(): return lax.ppermute(block, axis, route)  18.3 us
    reshape x4, local copies, waits for them, and re-layouts, compress(): shaped = row_data.reshape(blocks, block_len, head_count, head_dim)  13.4 us
    sub x1, matrix products, shards(): exp_terms = jnp.where(visible[:, None, :], jnp.exp(masked - row_peak), 0.0)  12.1 us
    dot_general x4, matrix products, compress(): jnp.einsum('bjhd,hj->bhd', shaped, weights, preferred_element_type=jnp.fl...  8.74 us
    dot_general x1, matrix products, shards(): jnp.einsum('qhk,khd->qhd', weights_low, win_values, preferred_element_typ...  8.33 us
    slice x3, local copies, waits for them, and re-layouts, sent_together(): lax.slice_in_dim(result, at, at + a.shape[along], axis=along)  5.87 us
    all_to_all x1, blocking collectives, from_everyone(): lax.all_to_all(jnp.broadcast_to(value[None], (size, *value.shape)), axis,...  5.17 us
  transfers between devices with their start and end apart: 7, of which 0 were waited for; matrix products, arithmetic and copies ran while one was open for 41% of the time, Pallas kernels for 0%

commit v1 on v0

v1 whole, which is shorter than its diff:
```python
import jax
import jax.numpy as jnp
from jax import lax
from jax.experimental import pallas as pl
from jax.experimental.pallas import tpu as pltpu
from jax.sharding import Mesh
from jax.sharding import PartitionSpec as P

WINDOW = 128
REACH = 3
AX_X, AX_Z, AX_C = "seq_0", "seq_1", "seq_2"
SEQ = (AX_X, AX_Z, AX_C)
REP_SEQ = ("rep", AX_X, AX_Z, AX_C)
LANES = 128
NEG = -1e30
F32, BF16, I32 = jnp.float32, jnp.bfloat16, jnp.int32
NT = (((1,), (1,)), ((), ()))
TN = (((0,), (0,)), ((), ()))


def dot(a, b):
    return jnp.dot(a, b, preferred_element_type=F32)


def dot_nt(a, b):
    return lax.dot_general(a, b, NT, preferred_element_type=F32)


def iota(shape, dim):
    return lax.broadcasted_iota(I32, shape, dim)


def one_hot(condition):
    return jnp.where(condition, 1.0, 0.0).astype(BF16)


def half_lanes(rows):
    return iota((rows, LANES), 1) < LANES // 2


def token_classes(tok_rows, med_len):
    row, lane = iota((tok_rows, LANES), 0), iota((tok_rows, LANES), 1)
    wanted = 2 * (row // med_len) + jnp.where(row % med_len == med_len - 1, 1, 0)
    return one_hot(lane % (LANES // 2) == wanted)


def project_kernel(tok_ref, w_ref, cm_ref, cc_ref, kv_ref, med_ref, pay_ref, w_buf, c_buf, sems):
    tok_rows = tok_ref.shape[0]
    heads, _, med_len = cm_ref.shape
    coarse_len = cc_ref.shape[2]
    inner = kv_ref.shape[1] // 2
    width = w_buf.shape[2]
    steps = w_buf.shape[0]
    copies = []
    for g in range(steps):
        columns = pl.ds(inner + g * width, width)
        copies.append(pltpu.make_async_copy(w_ref.at[:, columns], w_buf.at[g], sems.at[g]))
        copies[-1].start()
    med_blocks = tok_rows // med_len
    coarse_blocks = tok_rows // coarse_len
    per = width // 64
    tile_up = one_hot(iota((med_len, tok_rows), 1) % med_len == iota((med_len, tok_rows), 0))
    own_block = iota((per * med_blocks, tok_rows), 0) % med_blocks == (
        iota((per * med_blocks, tok_rows), 1) // med_len
    )
    own_coarse = iota((8, tok_rows), 0) == iota((8, tok_rows), 1) // coarse_len
    mixes = []
    for g in range(steps):
        side, first = (2 * g) // steps, (g % (steps // 2)) * per
        med_rows, coarse_rows = [], []
        for i in range(per):
            med_w = cm_ref[first + i].astype(F32)[side : side + 1, :]
            med_rows.append(jnp.broadcast_to(med_w, (med_blocks, med_len)))
            coarse_w = cc_ref[first + i].astype(F32)[side : side + 1, :]
            coarse_w = jnp.concatenate([coarse_w] * coarse_blocks, axis=1)
            coarse_rows.append(jnp.where(own_coarse, jnp.broadcast_to(coarse_w, (8, tok_rows)), 0.0))
        med_mix = dot(jnp.concatenate(med_rows, 0).astype(BF16), tile_up)
        med_mix = jnp.where(own_block, med_mix, 0.0)
        mixes.append(jnp.concatenate([med_mix] + coarse_rows, 0).astype(BF16))
    for g in range(steps):
        copies[g].wait()
        rows = dot(tok_ref[...], w_buf[g]).astype(BF16)
        kv_ref[:, g * width : (g + 1) * width] = rows
        packed = dot(mixes[g], rows)
        med_head = iota((med_blocks, width), 1) // 64
        coarse_head = iota((8, width), 1) // 64
        med = jnp.zeros((med_blocks, width), F32)
        coarse = jnp.zeros((8, width), F32)
        for i in range(per):
            med = jnp.where(med_head == i, packed[i * med_blocks : (i + 1) * med_blocks], med)
            at = per * med_blocks + 8 * i
            coarse = jnp.where(coarse_head == i, packed[at : at + 8], coarse)
        med_ref[:, g * width : (g + 1) * width] = med.astype(BF16)
        for i in range(width // LANES):
            tile = g * (width // LANES) + i
            c_buf[tile * coarse_blocks : (tile + 1) * coarse_blocks, :] = coarse[
                :coarse_blocks, i * LANES : (i + 1) * LANES
            ]
    count = c_buf.shape[0]
    total = pay_ref.shape[0]
    repeat = one_hot(iota((total, count), 0) % count == iota((total, count), 1))
    pay_ref[...] = dot(repeat, c_buf[...].astype(BF16)).astype(BF16)


def values_up(tile, odd):
    eye = one_hot(iota((LANES, LANES), 0) == iota((LANES, LANES), 1))
    turned = dot_nt(eye, tile).astype(BF16)
    half = LANES // 2
    ones = jnp.ones((16, tile.shape[0]), BF16)
    return jnp.concatenate([turned[half * odd : half * (odd + 1)], ones], 0)


def near_kernel(
    tok_ref, tail_ref, w_ref, wg_ref, kv_ref, far3_ref, far2_ref, far1_ref, med_ref, gid_ref,
    q_ref, gate_ref, mix_ref, w_buf, tail_buf, bias_buf, hot_buf, sems,
):
    tok_rows, depth = tok_ref.shape
    inner = kv_ref.shape[1] // 2
    width = w_buf.shape[2]
    steps = w_buf.shape[0]
    heads = gate_ref.shape[0] // 3
    med_blocks = med_ref.shape[0]
    med_len = tok_rows // med_blocks
    near = (REACH + 1) * med_blocks
    half = LANES // 2
    copies = []
    for g in range(steps):
        copies.append(
            pltpu.make_async_copy(w_ref.at[:, pl.ds(g * width, width)], w_buf.at[g], sems.at[g])
        )
        copies[-1].start()
    position = (lax.axis_index(AX_X) * lax.axis_size(AX_Z) + lax.axis_index(AX_Z)) * lax.axis_size(
        AX_C
    ) + lax.axis_index(AX_C)
    gate_ref[...] = 1.0 / (1.0 + jnp.exp(-dot_nt(wg_ref[...], tok_ref[...])))
    hot_buf[...] = token_classes(tok_rows, med_len)

    first = (position - REACH) * med_blocks
    padded = first + near
    row = padded // LANES - 1
    offset = padded % LANES
    low = gid_ref[pl.ds(jnp.maximum(row, 0), 1), :]
    high = gid_ref[pl.ds(jnp.minimum(row + 1, gid_ref.shape[0] - 1), 1), :]
    lane = iota((1, LANES), 1)
    both = jnp.where(lane >= offset, low, high)
    near_groups = pltpu.roll(jnp.broadcast_to(both, (8, LANES)), (LANES - offset) % LANES, 1)[:1]
    near_groups = jnp.where(lane + first >= 0, near_groups, -1).astype(F32).astype(BF16)
    spread = jnp.broadcast_to(near_groups.astype(F32), (near, LANES)).astype(BF16)
    i0, i1 = iota((near, LANES), 0), iota((near, LANES), 1)
    key_group = dot_nt(one_hot(i0 == i1), spread)
    own = (i1 % half) // 2 + REACH * med_blocks
    pick = one_hot(i0 == own)
    token_group = dot(spread, pick)
    visible = (key_group == token_group) & ((i0 < own) | ((i0 == own) & (i1 % 2 == 1)))
    bias_buf[...] = jnp.where(visible, 0.0, NEG).astype(BF16)

    for g in range(steps):
        copies[g].wait()
        lo = g * width
        if lo < inner:
            rows = dot(tok_ref[...], w_buf[g]).astype(BF16).astype(F32)
            q_ref[:, lo : lo + width] = (rows * (half**-0.5)).astype(BF16)
        else:
            tail_buf[:, lo - inner : lo - inner + width] = dot(tail_ref[...], w_buf[g]).astype(BF16)

    below = iota((WINDOW, WINDOW), 0) <= iota((WINDOW, WINDOW), 1)
    chunks = tok_rows // WINDOW
    first_bias = jnp.where(position == 0, NEG, 0.0)

    @pl.loop(0, heads // 2)
    def _(pair):
        at = pl.multiple_of(pair * LANES, LANES)
        at_v = pl.multiple_of(inner + pair * LANES, LANES)
        q_tile = q_ref[:, pl.ds(at, LANES)]
        keys = jnp.concatenate([tail_buf[:, pl.ds(at, LANES)], kv_ref[:, pl.ds(at, LANES)]], 0)
        values = jnp.concatenate([tail_buf[:, pl.ds(at_v, LANES)], kv_ref[:, pl.ds(at_v, LANES)]], 0)
        blocks = (far3_ref, far2_ref, far1_ref, med_ref)
        med_k = jnp.concatenate([b[:, pl.ds(at, LANES)] for b in blocks], 0)
        med_v = jnp.concatenate([b[:, pl.ds(at_v, LANES)] for b in blocks], 0)
        for odd in range(2):
            head = 2 * pair + odd
            mine = half_lanes(tok_rows) if odd == 0 else ~half_lanes(tok_rows)
            q_ext = jnp.where(mine, q_tile, hot_buf[...])
            mine_k = half_lanes(keys.shape[0]) if odd == 0 else ~half_lanes(keys.shape[0])
            k_ext = jnp.where(mine_k, keys, jnp.zeros_like(keys))
            merged = []
            for c in range(chunks):
                s = dot_nt(
                    k_ext[c * WINDOW : (c + 2) * WINDOW], q_ext[c * WINDOW : (c + 1) * WINDOW]
                )
                left, right = s[:WINDOW], s[WINDOW:]
                if c == 0:
                    left = left + first_bias
                merged.append(jnp.where(below, right, left))
            scores = jnp.concatenate(merged, 1)
            peak = jnp.max(scores, axis=0, keepdims=True)
            terms = jnp.exp(scores - peak).astype(BF16)
            v_up = values_up(values, odd)
            outs = []
            for c in range(chunks):
                part = terms[:, c * WINDOW : (c + 1) * WINDOW]
                zero = jnp.zeros_like(part)
                both_parts = jnp.concatenate(
                    [jnp.where(below, zero, part), jnp.where(below, part, zero)], 0
                )
                outs.append(dot(v_up[:, c * WINDOW : (c + 2) * WINDOW], both_parts))
            out = jnp.concatenate(outs, 1)
            factor = gate_ref[pl.ds(head, 1), :] / out[half : half + 1]
            mixed = out[:half] * factor

            mine_m = half_lanes(near) if odd == 0 else ~half_lanes(near)
            scores = dot_nt(jnp.where(mine_m, med_k, bias_buf[...]), q_ext)
            peak = jnp.maximum(jnp.max(scores, axis=0, keepdims=True), 0.0)
            terms = jnp.exp(scores - peak).astype(BF16)
            out = dot(values_up(med_v, odd), terms)
            factor = gate_ref[pl.ds(heads + head, 1), :] / (jnp.exp(-peak) + out[half : half + 1])
            mixed = mixed + out[:half] * factor
            mix_ref[pl.ds(pl.multiple_of(head * half, half), half), :] = mixed


def far_kernel(
    q_ref, gate_ref, mix_ref, w_ref, *refs
):
    pieces, (out_ref, keys_buf, values_buf, bias_buf, hot_buf, mixed_buf) = refs[:-6], refs[-6:]
    tok_rows, inner = q_ref.shape
    heads = gate_ref.shape[0] // 3
    half = LANES // 2
    tiles = inner // LANES
    total = pieces[0].shape[0]
    zs = lax.axis_size(AX_Z)
    count = total // zs
    each = total // (2 * tiles)
    per = each // zs
    pos_x, pos_z, pos_c = lax.axis_index(AX_X), lax.axis_index(AX_Z), lax.axis_index(AX_C)
    xs, cs = lax.axis_size(AX_X), lax.axis_size(AX_C)
    hot_buf[...] = token_classes(tok_rows, 16)

    r0, r1 = iota((total, total), 0), iota((total, total), 1)
    source = ((r0 % each) // per) * count + (r0 // each) * per + r0 % per
    turn = one_hot(source == r1)
    sorted_rows = dot(turn, jnp.concatenate([p[...] for p in pieces], 1)).astype(BF16)
    lane = iota((each, LANES), 1) % half
    row = iota((each, LANES), 0)
    position = (pos_x * zs + pos_z) * cs + pos_c
    seen = per * position + jnp.where(lane >= half // per - 1, 1, 0) + jnp.where(lane == half - 1, 1, 0)
    for n in range(len(pieces)):
        for t in range(tiles):
            block = sorted_rows[t * each : (t + 1) * each, n * LANES : (n + 1) * LANES]
            keys_buf[n * each : (n + 1) * each, t * LANES : (t + 1) * LANES] = block
            block = sorted_rows[(tiles + t) * each : (tiles + t + 1) * each, n * LANES : (n + 1) * LANES]
            values_buf[n * each : (n + 1) * each, t * LANES : (t + 1) * LANES] = block
        from_x = lax.rem(pos_x + xs - n % xs, xs)
        from_c = lax.rem(pos_c + n // xs, cs)
        index = ((from_x * zs + row // per) * cs + from_c) * per + row % per
        bias_buf[n * each : (n + 1) * each, :] = jnp.where(index < seen, 0.0, NEG).astype(BF16)

    keys_count = keys_buf.shape[0]

    @pl.loop(0, tiles)
    def _(pair):
        at = pl.multiple_of(pair * LANES, LANES)
        q_tile = q_ref[:, pl.ds(at, LANES)]
        keys = keys_buf[:, pl.ds(at, LANES)]
        values = values_buf[:, pl.ds(at, LANES)]
        for odd in range(2):
            head = 2 * pair + odd
            mine = half_lanes(tok_rows) if odd == 0 else ~half_lanes(tok_rows)
            q_ext = jnp.where(mine, q_tile, hot_buf[...])
            mine_k = half_lanes(keys_count) if odd == 0 else ~half_lanes(keys_count)
            scores = dot_nt(jnp.where(mine_k, keys, bias_buf[...]), q_ext)
            peak = jnp.maximum(jnp.max(scores, axis=0, keepdims=True), 0.0)
            terms = jnp.exp(scores - peak).astype(BF16)
            out = dot(values_up(values, odd), terms)
            factor = gate_ref[pl.ds(2 * heads + head, 1), :] / (jnp.exp(-peak) + out[half : half + 1])
            rows = pl.ds(pl.multiple_of(head * half, half), half)
            mixed_buf[rows, :] = (mix_ref[rows, :] + out[:half] * factor).astype(BF16)

    out_ref[...] = lax.dot_general(
        mixed_buf[...], w_ref[...], TN, preferred_element_type=F32
    ).astype(BF16)


def shifted(block, axis, distance):
    size = lax.axis_size(axis)
    return lax.ppermute(block, axis, [(i - distance, i) for i in range(distance, size)])


def turned(block, axis, distance):
    size = lax.axis_size(axis)
    return lax.ppermute(block, axis, [(i, (i + distance) % size) for i in range(size)])


VMEM = pl.BlockSpec(memory_space=pltpu.VMEM)
HBM = pl.BlockSpec(memory_space=pl.ANY)


def params(mib):
    return pltpu.CompilerParams(vmem_limit_bytes=mib << 20)


def shards(tokens, w_qkv, w_gate, w_out, cmp_med, cmp_coarse, group_id):
    tok_rows, depth = tokens.shape
    heads, med_len, coarse_len = cmp_med.shape[1], cmp_med.shape[2], cmp_coarse.shape[2]
    inner = w_out.shape[0]
    width = 256
    med_blocks = tok_rows // med_len
    coarse_blocks = tok_rows // coarse_len
    zs = lax.axis_size(AX_Z)
    count = coarse_blocks * 2 * inner // LANES
    tail = shifted(tokens[tok_rows - WINDOW :], SEQ, 1)

    kv_steps = 2 * inner // width
    kv, med, payload = pl.pallas_call(
        project_kernel,
        out_shape=(
            jax.ShapeDtypeStruct((tok_rows, 2 * inner), BF16),
            jax.ShapeDtypeStruct((med_blocks, 2 * inner), BF16),
            jax.ShapeDtypeStruct((zs * count, LANES), BF16),
        ),
        in_specs=[VMEM, HBM, VMEM, VMEM],
        out_specs=(VMEM, VMEM, VMEM),
        scratch_shapes=[
            pltpu.VMEM((kv_steps, depth, width), BF16),
            pltpu.VMEM((count, LANES), F32),
            pltpu.SemaphoreType.DMA((kv_steps,)),
        ],
        compiler_params=params(24),
        cost_estimate=pl.CostEstimate(flops=2 * tok_rows * depth * 2 * inner, bytes_accessed=4 << 20, transcendentals=0),
        name="project",
    )(tokens, w_qkv, cmp_med.transpose(1, 0, 2), cmp_coarse.transpose(1, 0, 2))

    column = lax.all_to_all(payload, AX_Z, 0, 0, tiled=True)
    far1, far2, far3 = (shifted(med, SEQ, k) for k in (1, 2, 3))

    all_steps = 3 * inner // width
    q, gates, mixed = pl.pallas_call(
        near_kernel,
        out_shape=(
            jax.ShapeDtypeStruct((tok_rows, inner), BF16),
            jax.ShapeDtypeStruct((3 * heads, tok_rows), F32),
            jax.ShapeDtypeStruct((inner, tok_rows), F32),
        ),
        in_specs=[VMEM, VMEM, HBM] + [VMEM] * 7,
        out_specs=(VMEM, VMEM, VMEM),
        scratch_shapes=[
            pltpu.VMEM((all_steps, depth, width), BF16),
            pltpu.VMEM((WINDOW, 2 * inner), BF16),
            pltpu.VMEM(((REACH + 1) * med_blocks, LANES), BF16),
            pltpu.VMEM((tok_rows, LANES), BF16),
            pltpu.SemaphoreType.DMA((all_steps,)),
        ],
        compiler_params=params(30),
        cost_estimate=pl.CostEstimate(flops=4 << 30, bytes_accessed=8 << 20, transcendentals=0),
        name="near",
    )(tokens, tail, w_qkv, w_gate.T, kv, far3, far2, far1, med, group_id.reshape(-1, LANES))

    columns = [column] + [turned(column, AX_X, k) for k in range(1, lax.axis_size(AX_X))]
    columns += [turned(c, AX_C, 1) for c in columns]
    keys_count = coarse_blocks * lax.axis_size(SEQ)
    return pl.pallas_call(
        far_kernel,
        out_shape=jax.ShapeDtypeStruct((tok_rows, inner), BF16),
        in_specs=[VMEM] * (4 + len(columns)),
        out_specs=VMEM,
        scratch_shapes=[
            pltpu.VMEM((keys_count, inner), BF16),
            pltpu.VMEM((keys_count, inner), BF16),
            pltpu.VMEM((keys_count, LANES), BF16),
            pltpu.VMEM((tok_rows, LANES), BF16),
            pltpu.VMEM((inner, tok_rows), BF16),
        ],
        compiler_params=params(24),
        cost_estimate=pl.CostEstimate(flops=2 << 30, bytes_accessed=4 << 20, transcendentals=0),
        name="far",
    )(q, gates, mixed, w_out, *columns)


def solution(mesh):
    torus = Mesh(mesh.devices.reshape(mesh.shape["rep"], 4, 16, 2), REP_SEQ)
    return jax.shard_map(
        shards,
        mesh=torus,
        in_specs=(P(REP_SEQ, None), P(), P(), P(), P(), P(), P("rep")),
        out_specs=P(REP_SEQ, None),
        check_vma=False,
    )
```

time: 172 us -> 82.7 us (0.48); the launches traced: 170 us -> 82.2 us
  local copies, waits for them, and re-layouts: 52.4 us -> 6.56 us
  matrix products: 43 us -> 0 us
  Pallas kernels: 0 us -> 24.6 us
  other arithmetic: 20.6 us -> 0 us
  waiting for transfers between devices: 0.02 us -> 5.54 us
  blocking collectives: 5.17 us -> 0 us
  starting transfers between devices: 47.9 us -> 45.4 us
    dot_general x12 -> x0, matrix products: 30.9 us -> none  [the longest x4 8.74 us: compress(): jnp.einsum('bjhd,hj->bhd', shaped, weights, preferred_element_type=jnp.fl...]
    pallas_call x0 -> x3, Pallas kernels: none -> 24.6 us  [the longest x1 11.4 us: shards(): pl.pallas_call(near_kernel, out_shape=(jax.ShapeDtypeStruct((tok_rows, in...]
    slice x13 -> x1, local copies, waits for them, and re-layouts: 17 us -> 0.01 us  [shards(): tail = shifted(tokens[tok_rows - WINDOW:], SEQ, 1)]
    reshape x4 -> x0, local copies, waits for them, and re-layouts: 13.4 us -> none  [compress(): shaped = row_data.reshape(blocks, block_len, head_count, head_dim)]
    sub x1 -> x0, matrix products: 12.1 us -> none  [shards(): exp_terms = jnp.where(visible[:, None, :], jnp.exp(masked - row_peak), 0.0)]
    concatenate x6 -> x0, other arithmetic: 9.31 us -> none  [the longest x1 2.5 us: shards(): jnp.concatenate([reached[distance][1] for distance in range(REACH, -1, -1...]
    ppermute x6 -> x11, waiting for transfers between devices: 0.02 us -> 5.54 us  [the longest x7 5.53 us: turned(): lax.ppermute(block, axis, [(i, (i + distance) % size) for i in range(size)])]
    all_to_all x1 -> x0, blocking collectives: 5.17 us -> none  [from_everyone(): lax.all_to_all(jnp.broadcast_to(value[None], (size, *value.shape)), axis,...]
  transfers between devices with their start and end apart: 7 -> 12, of which waited for: 0 -> 2; matrix products, arithmetic and copies ran while one was open for 41% -> 0% of each run, Pallas kernels for 0% -> 14%
where the time goes in v1:
time: 82.7 us; the launch traced here: 82.2 us
  starting transfers between devices  45.4 us (55%)
  Pallas kernels  24.6 us (30%)
  local copies, waits for them, and re-layouts  6.56 us (8%)
  waiting for transfers between devices  5.54 us (7%)
    all_to_all x1, starting transfers between devices, shards(): column = lax.all_to_all(payload, AX_Z, 0, 0, tiled=True)  24.5 us
    ppermute x4, starting transfers between devices, shifted(): lax.ppermute(block, axis, [(i - distance, i) for i in range(distance, siz...  14.8 us
    pallas_call x1, Pallas kernels, shards(): pl.pallas_call(near_kernel, out_shape=(jax.ShapeDtypeStruct((tok_rows, in...  11.4 us
    pallas_call x1, Pallas kernels, shards(): pl.pallas_call(far_kernel, out_shape=jax.ShapeDtypeStruct((tok_rows, inne...  7.49 us
    unnamed x18, local copies, waits for them, and re-layouts  6.54 us
    ppermute x7, starting transfers between devices, turned(): lax.ppermute(block, axis, [(i, (i + distance) % size) for i in range(size)])  6 us
    pallas_call x1, Pallas kernels, shards(): pl.pallas_call(project_kernel, out_shape=(jax.ShapeDtypeStruct((tok_rows,...  5.69 us
    ppermute x7, waiting for transfers between devices, turned(): lax.ppermute(block, axis, [(i, (i + distance) % size) for i in range(size)])  5.53 us
  transfers between devices with their start and end apart: 12, of which 2 were waited for; matrix products, arithmetic and copies ran while one was open for 0% of the time, Pallas kernels for 14%

profile of v1, /device:TPU:33, one launch (start us, length us, event | category | flops | bytes accessed | tf_op | source)
XLA Modules:
  0.0 82.2 jit_solution(17022024776455911792)
XLA Ops:
  0.0 0.0 copy-start
  0.0 1.1 %copy-done = bf16[512,768]{1,0:T(8,128)(2,1)S(1)} copy-done((bf16[512,768]{1,0:T(8,128)(2,1)S(1)}, bf16[512,768]{1,0:T(8,128)(2,1)}, u32[]{:S(2)}) %copy-start) | copy-done | bytes 786456
  1.1 0.0 copy-start.2
  1.1 2.0 %copy-done.2 = bf16[768,2304]{1,0:T(8,128)(2,1)S(1)} copy-done((bf16[768,2304]{1,0:T(8,128)(2,1)S(1)}, bf16[768,2304]{1,0:T(8,128)(2,1)}, u32[]{:S(2)}) %copy-start.2) | copy-done | bytes 3538968
  3.1 0.0 copy-start.7
  3.1 0.7 copy-done.7
  3.8 0.0 copy-start.8
  3.8 0.7 copy-done.8
  4.5 0.0 copy-start.1
  4.5 0.0 copy-start.5
  4.5 0.0 copy-start.6
  4.5 5.7 %project.1 = (bf16[512,1536]{1,0:T(8,128)(2,1)S(1)}, bf16[32,1536]{1,0:T(8,128)(2,1)S(1)}, bf16[384,128]{1,0:T(8,128)(2,1)}) custom-call(bf16[512,768]{1,0:T(8,128)(2,1)S(1)} %copy-done, bf16[768,2304]{1,0:T(8,128)(2,1)S(1)} %copy-done.2, bf16[12,2,16]{2,1,0:T(2,128)(2,1)S(1)} %bitcast.14, bf16[12,2,256]{2,1,0:T(2,128)(2,1)S(1)} %bitcast.13), custom_call_target="tpu_custom_call" | custom-call | flops 1207959552 | bytes 4194304 | tf_op jit(solution)/shard_map/project/pallas_call | solution.py:313
  10.2 24.5 %all-to-all-start = ((bf16[16,24,128]{2,1,0:T(8,128)(2,1)}), bf16[16,24,128]{2,1,0:T(8,128)(2,1)S(1)}, u32[]{:S(2)}, u32[]{:S(2)}) async-start(bf16[16,24,128]{2,1,0:T(8,128)(2,1)} %bitcast.4), calls=%async_computation | async-start | bytes 196608 | tf_op jit(solution)/shard_map/all_to_all | solution.py:332
  34.8 5.0 %collective-permute-start.1 = (bf16[32,1536]{1,0:T(8,128)(2,1)S(1)}, bf16[32,1536]{1,0:T(8,128)(2,1)S(1)}, u32[]{:S(2)}, u32[]{:S(2)}) collective-permute-start(bf16[32,1536]{1,0:T(8,128)(2,1)S(1)} %get-tuple-element.12.med_ref), channel_id=1, source_target_pairs={{0,3},{1,4},{2,5},{3,6},{4,7},{5,8},{6,9},{7,10},{8,11},{9,12},{10... | collective-permute-start | bytes 294920 | tf_op jit(solution)/shard_map/ppermute | solution.py:285
  39.8 3.1 %collective-permute-start.2 = (bf16[32,1536]{1,0:T(8,128)(2,1)S(1)}, bf16[32,1536]{1,0:T(8,128)(2,1)S(1)}, u32[]{:S(2)}, u32[]{:S(2)}) collective-permute-start(bf16[32,1536]{1,0:T(8,128)(2,1)S(1)} %get-tuple-element.12.med_ref), channel_id=1, source_target_pairs={{0,2},{1,3},{2,4},{3,5},{4,6},{5,7},{6,8},{7,9},{8,10},{9,11},{10,... | collective-permute-start | bytes 294920 | tf_op jit(solution)/shard_map/ppermute | solution.py:285
  43.0 0.0 copy-done.1
  43.0 2.0 %collective-permute-start = (bf16[128,768]{1,0:T(8,128)(2,1)S(1)}, bf16[128,768]{1,0:T(8,128)(2,1)S(1)}, u32[]{:S(2)}, u32[]{:S(2)}) collective-permute-start(bf16[128,768]{1,0:T(8,128)(2,1)S(1)} %slice.3), channel_id=1, source_target_pairs={{0,1},{1,2},{2,3},{3,4},{4,5},{5,6},{6,7},{7,8},{8,9},{9,10},{10,1... | collective-permute-start | bytes 589832 | tf_op jit(solution)/shard_map/ppermute | solution.py:285
  44.9 4.7 %collective-permute-start.3 = (bf16[32,1536]{1,0:T(8,128)(2,1)S(1)}, bf16[32,1536]{1,0:T(8,128)(2,1)S(1)}, u32[]{:S(2)}, u32[]{:S(2)}) collective-permute-start(bf16[32,1536]{1,0:T(8,128)(2,1)S(1)} %get-tuple-element.12.med_ref), channel_id=1, source_target_pairs={{0,1},{1,2},{2,3},{3,4},{4,5},{5,6},{6,7},{7,8},{8,9},{9,10},{10,1... | collective-permute-start | bytes 294920 | tf_op jit(solution)/shard_map/ppermute | solution.py:285
  49.7 0.0 all-to-all-done
  49.7 3.0 %collective-permute-start.6 = (bf16[384,128]{1,0:T(8,128)(2,1)S(1)}, bf16[384,128]{1,0:T(8,128)(2,1)S(1)}, u32[]{:S(2)}, u32[]{:S(2)}) collective-permute-start(bf16[384,128]{1,0:T(8,128)(2,1)S(1)} %bitcast.6), channel_id=1, source_target_pairs={{0,96},{32,0},{64,32},{96,64},{1,97},{33,1},{65,33},{97,65},{2,98}... | collective-permute-start | bytes 294920 | tf_op jit(solution)/shard_map/ppermute | solution.py:290
  52.7 0.0 collective-permute-done.1.far3_ref
  52.7 0.0 collective-permute-start.4
  52.7 0.0 collective-permute-done.2.far2_ref
  52.7 1.6 %collective-permute-start.5 = (bf16[384,128]{1,0:T(8,128)(2,1)S(1)}, bf16[384,128]{1,0:T(8,128)(2,1)S(1)}, u32[]{:S(2)}, u32[]{:S(2)}) collective-permute-start(bf16[384,128]{1,0:T(8,128)(2,1)S(1)} %bitcast.8), channel_id=1, source_target_pairs={{0,64},{32,96},{64,0},{96,32},{1,65},{33,97},{65,1},{97,33},{2,66}... | collective-permute-start | bytes 294920 | tf_op jit(solution)/shard_map/ppermute | solution.py:290
  54.3 0.0 collective-permute-done.3.far1_ref
  54.3 0.4 collective-permute-start.7
  54.7 0.6 collective-permute-done.6.refs_3_
  55.3 0.4 collective-permute-start.10
  55.7 4.9 %collective-permute-done.4.refs_1_ = bf16[384,128]{1,0:T(8,128)(2,1)S(1)} collective-permute-done((bf16[384,128]{1,0:T(8,128)(2,1)S(1)}, bf16[384,128]{1,0:T(8,128)(2,1)S(1)}, u32[]{:S(2)}, u32[]{:S(2)}) %collective-permute-start.4) | collective-permute-done | bytes 98336 | tf_op jit(solution)/shard_map/ppermute | solution.py:290
  60.5 0.7 collective-permute-start.8
  61.2 0.0 collective-permute-done.5.refs_2_
  61.2 0.0 collective-permute-start.9
  61.2 0.0 collective-permute-done.tail_ref
  61.2 0.0 copy-done.5
  61.2 0.0 copy-done.6
  61.2 0.0 copy-start.3
  61.3 2.0 %copy-done.3 = bf16[768,2304]{1,0:T(8,128)(2,1)S(1)} copy-done((bf16[768,2304]{1,0:T(8,128)(2,1)S(1)}, bf16[768,2304]{1,0:T(8,128)(2,1)}, u32[]{:S(2)}) %copy-start.3) | copy-done | bytes 3538968
  63.2 0.0 copy-start.4
  63.2 11.4 %near.1 = (bf16[512,768]{1,0:T(8,128)(2,1)S(1)}, f32[36,512]{1,0:T(8,128)S(1)}, f32[768,512]{1,0:T(8,128)S(1)}) custom-call(bf16[512,768]{1,0:T(8,128)(2,1)S(1)} %copy-done.1, bf16[128,768]{1,0:T(8,128)(2,1)S(1)} %collective-permute-done.tail_ref, bf16[768,2304]{1,0:T(8,128)(2,1)S(1)} %copy-done.3, bf16[36,768]{1,0:T(8,128)(2,1)S(1)} %bitcast.11, ...), custom_call_target="tpu_custom_call" | custom-call | flops 4294967296 | bytes 8388608 | tf_op jit(solution)/shard_map/near/pallas_call | solution.py:336
  74.7 0.0 collective-permute-done.7.refs_4_
  74.7 0.0 collective-permute-done.10.refs_7_
  74.7 0.0 collective-permute-done.8.refs_5_
  74.7 0.0 collective-permute-done.9.refs_6_
  74.7 0.0 copy-done.4
  74.7 7.5 %far.1 = bf16[512,768]{1,0:T(8,128)(2,1)} custom-call(bf16[512,768]{1,0:T(8,128)(2,1)S(1)} %get-tuple-element.13.q_ref, f32[36,512]{1,0:T(8,128)S(1)} %get-tuple-element.14.gate_ref, f32[768,512]{1,0:T(8,128)S(1)} %get-tuple-element.15.mix_ref, bf16[768,768]{1,0:T(8,128)(2,1)S(1)} %copy-done.4, bf16[384,128]{1,0:T(8,128)(2,1)S(1)} %bitcast.10, ...), custom_call_target="tpu_custom_call" | custom-call | flops 2147483648 | bytes 4194304 | tf_op jit(solution)/shard_map/far/pallas_call | solution.py:360
  (1 shorter events, 0.0 us)
Async XLA Ops:
  0.0 1.1 %copy-start = (bf16[512,768]{1,0:T(8,128)(2,1)S(1)}, bf16[512,768]{1,0:T(8,128)(2,1)}, u32[]{:S(2)}) copy-start(bf16[512,768]{1,0:T(8,128)(2,1)} %tok_ref.3) | copy-start | bytes 2359300
  1.1 2.0 %copy-start.2 = (bf16[768,2304]{1,0:T(8,128)(2,1)S(1)}, bf16[768,2304]{1,0:T(8,128)(2,1)}, u32[]{:S(2)}) copy-start(bf16[768,2304]{1,0:T(8,128)(2,1)} %w_ref.4) | copy-start | bytes 10616836
  3.1 0.7 copy-start.7
  3.8 0.7 copy-start.8
  4.5 38.4 %copy-start.1 = (bf16[512,768]{1,0:T(8,128)(2,1)S(1)}, bf16[512,768]{1,0:T(8,128)(2,1)}, u32[]{:S(2)}) copy-start(bf16[512,768]{1,0:T(8,128)(2,1)} %tok_ref.3) | copy-start | bytes 2359300
  4.5 56.7 %copy-start.5 = (bf16[768,36]{0,1:T(8,128)(2,1)S(1)}, bf16[768,36]{0,1:T(8,128)(2,1)}, u32[]{:S(2)}) copy-start(bf16[768,36]{0,1:T(8,128)(2,1)} %param.9) | copy-start | bytes 165892
  4.5 56.7 %copy-start.6 = (s32[4096]{0:T(1024)S(1)}, s32[4096]{0:T(1024)}, u32[]{:S(2)}) copy-start(s32[4096]{0:T(1024)} %param.13) | copy-start | bytes 49156
  10.2 39.4 %all-to-all-start = ((bf16[16,24,128]{2,1,0:T(8,128)(2,1)}), bf16[16,24,128]{2,1,0:T(8,128)(2,1)S(1)}, u32[]{:S(2)}, u32[]{:S(2)}) async-start(bf16[16,24,128]{2,1,0:T(8,128)(2,1)} %bitcast.4), calls=%async_computation | async-start | bytes 196608 | tf_op jit(solution)/shard_map/all_to_all | solution.py:332
  34.8 17.9 %collective-permute-start.1 = (bf16[32,1536]{1,0:T(8,128)(2,1)S(1)}, bf16[32,1536]{1,0:T(8,128)(2,1)S(1)}, u32[]{:S(2)}, u32[]{:S(2)}) collective-permute-start(bf16[32,1536]{1,0:T(8,128)(2,1)S(1)} %get-tuple-element.12.med_ref), channel_id=1, source_target_pairs={{0,3},{1,4},{2,5},{3,6},{4,7},{5,8},{6,9},{7,10},{8,11},{9,12},{10... | collective-permute-start | bytes 294920 | tf_op jit(solution)/shard_map/ppermute | solution.py:285
  39.8 12.9 %collective-permute-start.2 = (bf16[32,1536]{1,0:T(8,128)(2,1)S(1)}, bf16[32,1536]{1,0:T(8,128)(2,1)S(1)}, u32[]{:S(2)}, u32[]{:S(2)}) collective-permute-start(bf16[32,1536]{1,0:T(8,128)(2,1)S(1)} %get-tuple-element.12.med_ref), channel_id=1, source_target_pairs={{0,2},{1,3},{2,4},{3,5},{4,6},{5,7},{6,8},{7,9},{8,10},{9,11},{10,... | collective-permute-start | bytes 294920 | tf_op jit(solution)/shard_map/ppermute | solution.py:285
  43.0 18.2 %collective-permute-start = (bf16[128,768]{1,0:T(8,128)(2,1)S(1)}, bf16[128,768]{1,0:T(8,128)(2,1)S(1)}, u32[]{:S(2)}, u32[]{:S(2)}) collective-permute-start(bf16[128,768]{1,0:T(8,128)(2,1)S(1)} %slice.3), channel_id=1, source_target_pairs={{0,1},{1,2},{2,3},{3,4},{4,5},{5,6},{6,7},{7,8},{8,9},{9,10},{10,1... | collective-permute-start | bytes 589832 | tf_op jit(solution)/shard_map/ppermute | solution.py:285
  44.9 9.3 %collective-permute-start.3 = (bf16[32,1536]{1,0:T(8,128)(2,1)S(1)}, bf16[32,1536]{1,0:T(8,128)(2,1)S(1)}, u32[]{:S(2)}, u32[]{:S(2)}) collective-permute-start(bf16[32,1536]{1,0:T(8,128)(2,1)S(1)} %get-tuple-element.12.med_ref), channel_id=1, source_target_pairs={{0,1},{1,2},{2,3},{3,4},{4,5},{5,6},{6,7},{7,8},{8,9},{9,10},{10,1... | collective-permute-start | bytes 294920 | tf_op jit(solution)/shard_map/ppermute | solution.py:285
  49.7 5.6 %collective-permute-start.6 = (bf16[384,128]{1,0:T(8,128)(2,1)S(1)}, bf16[384,128]{1,0:T(8,128)(2,1)S(1)}, u32[]{:S(2)}, u32[]{:S(2)}) collective-permute-start(bf16[384,128]{1,0:T(8,128)(2,1)S(1)} %bitcast.6), channel_id=1, source_target_pairs={{0,96},{32,0},{64,32},{96,64},{1,97},{33,1},{65,33},{97,65},{2,98}... | collective-permute-start | bytes 294920 | tf_op jit(solution)/shard_map/ppermute | solution.py:290
  52.7 7.9 %collective-permute-start.4 = (bf16[384,128]{1,0:T(8,128)(2,1)S(1)}, bf16[384,128]{1,0:T(8,128)(2,1)S(1)}, u32[]{:S(2)}, u32[]{:S(2)}) collective-permute-start(bf16[384,128]{1,0:T(8,128)(2,1)S(1)} %bitcast.7), channel_id=1, source_target_pairs={{0,32},{32,64},{64,96},{96,0},{1,33},{33,65},{65,97},{97,1},{2,34}... | collective-permute-start | bytes 294920 | tf_op jit(solution)/shard_map/ppermute | solution.py:290
  52.7 8.5 %collective-permute-start.5 = (bf16[384,128]{1,0:T(8,128)(2,1)S(1)}, bf16[384,128]{1,0:T(8,128)(2,1)S(1)}, u32[]{:S(2)}, u32[]{:S(2)}) collective-permute-start(bf16[384,128]{1,0:T(8,128)(2,1)S(1)} %bitcast.8), channel_id=1, source_target_pairs={{0,64},{32,96},{64,0},{96,32},{1,65},{33,97},{65,1},{97,33},{2,66}... | collective-permute-start | bytes 294920 | tf_op jit(solution)/shard_map/ppermute | solution.py:290
  54.3 20.4 %collective-permute-start.7 = (bf16[384,128]{1,0:T(8,128)(2,1)S(1)}, bf16[384,128]{1,0:T(8,128)(2,1)S(1)}, u32[]{:S(2)}, u32[]{:S(2)}) collective-permute-start(bf16[384,128]{1,0:T(8,128)(2,1)S(1)} %bitcast.9), channel_id=1, source_target_pairs={{0,1},{1,0},{2,3},{3,2},{4,5},{5,4},{6,7},{7,6},{8,9},{9,8},{10,11... | collective-permute-start | bytes 294920 | tf_op jit(solution)/shard_map/ppermute | solution.py:290
  55.3 19.4 %collective-permute-start.10 = (bf16[384,128]{1,0:T(8,128)(2,1)S(1)}, bf16[384,128]{1,0:T(8,128)(2,1)S(1)}, u32[]{:S(2)}, u32[]{:S(2)}) collective-permute-start(bf16[384,128]{1,0:T(8,128)(2,1)S(1)} %collective-permute-done.6.refs_3_), channel_id=1, source_target_pairs={{0,1},{1,0},{2,3},{3,2},{4,5},{5,4},{6,7},{7,6},{8,9},{9,8},{10,11... | collective-permute-start | bytes 294920 | tf_op jit(solution)/shard_map/ppermute | solution.py:290
  60.5 14.1 %collective-permute-start.8 = (bf16[384,128]{1,0:T(8,128)(2,1)S(1)}, bf16[384,128]{1,0:T(8,128)(2,1)S(1)}, u32[]{:S(2)}, u32[]{:S(2)}) collective-permute-start(bf16[384,128]{1,0:T(8,128)(2,1)S(1)} %collective-permute-done.4.refs_1_), channel_id=1, source_target_pairs={{0,1},{1,0},{2,3},{3,2},{4,5},{5,4},{6,7},{7,6},{8,9},{9,8},{10,11... | collective-permute-start | bytes 294920 | tf_op jit(solution)/shard_map/ppermute | solution.py:290
  61.2 13.5 %collective-permute-start.9 = (bf16[384,128]{1,0:T(8,128)(2,1)S(1)}, bf16[384,128]{1,0:T(8,128)(2,1)S(1)}, u32[]{:S(2)}, u32[]{:S(2)}) collective-permute-start(bf16[384,128]{1,0:T(8,128)(2,1)S(1)} %collective-permute-done.5.refs_2_), channel_id=1, source_target_pairs={{0,1},{1,0},{2,3},{3,2},{4,5},{5,4},{6,7},{7,6},{8,9},{9,8},{10,11... | collective-permute-start | bytes 294920 | tf_op jit(solution)/shard_map/ppermute | solution.py:290
  61.2 2.0 %copy-start.3 = (bf16[768,2304]{1,0:T(8,128)(2,1)S(1)}, bf16[768,2304]{1,0:T(8,128)(2,1)}, u32[]{:S(2)}) copy-start(bf16[768,2304]{1,0:T(8,128)(2,1)} %w_ref.4) | copy-start | bytes 10616836
  63.2 11.5 %copy-start.4 = (bf16[768,768]{1,0:T(8,128)(2,1)S(1)}, bf16[768,768]{1,0:T(8,128)(2,1)}, u32[]{:S(2)}) copy-start(bf16[768,768]{1,0:T(8,128)(2,1)} %w_ref.5) | copy-start | bytes 3538948

commit v2 on v1

--- a/solution.py
+++ b/solution.py
@@ -44,17 +44,26 @@
     return one_hot(lane % (LANES // 2) == wanted)
 
 
-def project_kernel(tok_ref, w_ref, cm_ref, cc_ref, kv_ref, med_ref, pay_ref, w_buf, c_buf, sems):
+def project_kernel(
+    tok_hbm, w_hbm, cm_hbm, cc_hbm, kv_hbm, med_ref, pay_ref,
+    tok_ref, w_buf, cm_ref, cc_ref, kv_ref, c_buf, sems, in_sems, out_sems,
+):
     tok_rows = tok_ref.shape[0]
-    heads, _, med_len = cm_ref.shape
+    _, _, med_len = cm_ref.shape
     coarse_len = cc_ref.shape[2]
-    inner = kv_ref.shape[1] // 2
+    inner = kv_hbm.shape[1] // 2
     width = w_buf.shape[2]
     steps = w_buf.shape[0]
+    fetches = [
+        pltpu.make_async_copy(src, dst, in_sems.at[n])
+        for n, (src, dst) in enumerate(((cm_hbm, cm_ref), (cc_hbm, cc_ref), (tok_hbm, tok_ref)))
+    ]
+    for fetch in fetches:
+        fetch.start()
     copies = []
     for g in range(steps):
         columns = pl.ds(inner + g * width, width)
-        copies.append(pltpu.make_async_copy(w_ref.at[:, columns], w_buf.at[g], sems.at[g]))
+        copies.append(pltpu.make_async_copy(w_hbm.at[:, columns], w_buf.at[g], sems.at[g]))
         copies[-1].start()
     med_blocks = tok_rows // med_len
     coarse_blocks = tok_rows // coarse_len
@@ -64,6 +73,11 @@
         iota((per * med_blocks, tok_rows), 1) // med_len
     )
     own_coarse = iota((8, tok_rows), 0) == iota((8, tok_rows), 1) // coarse_len
+    count = c_buf.shape[0]
+    total = pay_ref.shape[0]
+    repeat = one_hot(iota((total, count), 0) % count == iota((total, count), 1))
+    fetches[0].wait()
+    fetches[1].wait()
     mixes = []
     for g in range(steps):
         side, first = (2 * g) // steps, (g % (steps // 2)) * per
@@ -77,10 +91,16 @@
         med_mix = dot(jnp.concatenate(med_rows, 0).astype(BF16), tile_up)
         med_mix = jnp.where(own_block, med_mix, 0.0)
         mixes.append(jnp.concatenate([med_mix] + coarse_rows, 0).astype(BF16))
+    fetches[2].wait()
+    stores = []
     for g in range(steps):
         copies[g].wait()
         rows = dot(tok_ref[...], w_buf[g]).astype(BF16)
-        kv_ref[:, g * width : (g + 1) * width] = rows
+        kv_ref[g] = rows
+        stores.append(
+            pltpu.make_async_copy(kv_ref.at[g], kv_hbm.at[:, pl.ds(g * width, width)], out_sems.at[g])
+        )
+        stores[-1].start()
         packed = dot(mixes[g], rows)
         med_head = iota((med_blocks, width), 1) // 64
         coarse_head = iota((8, width), 1) // 64
@@ -96,10 +116,9 @@
             c_buf[tile * coarse_blocks : (tile + 1) * coarse_blocks, :] = coarse[
                 :coarse_blocks, i * LANES : (i + 1) * LANES
             ]
-    count = c_buf.shape[0]
-    total = pay_ref.shape[0]
-    repeat = one_hot(iota((total, count), 0) % count == iota((total, count), 1))
     pay_ref[...] = dot(repeat, c_buf[...].astype(BF16)).astype(BF16)
+    for store in stores:
+        store.wait()
 
 
 def values_up(tile, odd):
@@ -110,50 +129,31 @@
     return jnp.concatenate([turned[half * odd : half * (odd + 1)], ones], 0)
 
 
-def near_kernel(
-    tok_ref, tail_ref, w_ref, wg_ref, kv_ref, far3_ref, far2_ref, far1_ref, med_ref, gid_ref,
-    q_ref, gate_ref, mix_ref, w_buf, tail_buf, bias_buf, hot_buf, sems,
+def window_kernel(
+    tok_hbm, tail_ref, w_hbm, wg_ref, kv_hbm,
+    q_ref, gate_ref, mix_ref, tok_ref, kv_ref, w_buf, tail_buf, sems, in_sems,
 ):
-    tok_rows, depth = tok_ref.shape
+    tok_rows, _ = tok_ref.shape
     inner = kv_ref.shape[1] // 2
     width = w_buf.shape[2]
     steps = w_buf.shape[0]
     heads = gate_ref.shape[0] // 3
-    med_blocks = med_ref.shape[0]
-    med_len = tok_rows // med_blocks
-    near = (REACH + 1) * med_blocks
     half = LANES // 2
+    fetch = pltpu.make_async_copy(tok_hbm, tok_ref, in_sems.at[0])
+    fetch.start()
     copies = []
     for g in range(steps):
         copies.append(
-            pltpu.make_async_copy(w_ref.at[:, pl.ds(g * width, width)], w_buf.at[g], sems.at[g])
+            pltpu.make_async_copy(w_hbm.at[:, pl.ds(g * width, width)], w_buf.at[g], sems.at[g])
         )
         copies[-1].start()
+    fetch_kv = pltpu.make_async_copy(kv_hbm, kv_ref, in_sems.at[1])
+    fetch_kv.start()
     position = (lax.axis_index(AX_X) * lax.axis_size(AX_Z) + lax.axis_index(AX_Z)) * lax.axis_size(
         AX_C
     ) + lax.axis_index(AX_C)
+    fetch.wait()
     gate_ref[...] = 1.0 / (1.0 + jnp.exp(-dot_nt(wg_ref[...], tok_ref[...])))
-    hot_buf[...] = token_classes(tok_rows, med_len)
-
-    first = (position - REACH) * med_blocks
-    padded = first + near
-    row = padded // LANES - 1
-    offset = padded % LANES
-    low = gid_ref[pl.ds(jnp.maximum(row, 0), 1), :]
-    high = gid_ref[pl.ds(jnp.minimum(row + 1, gid_ref.shape[0] - 1), 1), :]
-    lane = iota((1, LANES), 1)
-    both = jnp.where(lane >= offset, low, high)
-    near_groups = pltpu.roll(jnp.broadcast_to(both, (8, LANES)), (LANES - offset) % LANES, 1)[:1]
-    near_groups = jnp.where(lane + first >= 0, near_groups, -1).astype(F32).astype(BF16)
-    spread = jnp.broadcast_to(near_groups.astype(F32), (near, LANES)).astype(BF16)
-    i0, i1 = iota((near, LANES), 0), iota((near, LANES), 1)
-    key_group = dot_nt(one_hot(i0 == i1), spread)
-    own = (i1 % half) // 2 + REACH * med_blocks
-    pick = one_hot(i0 == own)
-    token_group = dot(spread, pick)
-    visible = (key_group == token_group) & ((i0 < own) | ((i0 == own) & (i1 % 2 == 1)))
-    bias_buf[...] = jnp.where(visible, 0.0, NEG).astype(BF16)
-
     for g in range(steps):
         copies[g].wait()
         lo = g * width
@@ -163,6 +163,7 @@
         else:
             tail_buf[:, lo - inner : lo - inner + width] = dot(tail_ref[...], w_buf[g]).astype(BF16)
 
+    fetch_kv.wait()
     below = iota((WINDOW, WINDOW), 0) <= iota((WINDOW, WINDOW), 1)
     chunks = tok_rows // WINDOW
     first_bias = jnp.where(position == 0, NEG, 0.0)
@@ -174,19 +175,14 @@
         q_tile = q_ref[:, pl.ds(at, LANES)]
         keys = jnp.concatenate([tail_buf[:, pl.ds(at, LANES)], kv_ref[:, pl.ds(at, LANES)]], 0)
         values = jnp.concatenate([tail_buf[:, pl.ds(at_v, LANES)], kv_ref[:, pl.ds(at_v, LANES)]], 0)
-        blocks = (far3_ref, far2_ref, far1_ref, med_ref)
-        med_k = jnp.concatenate([b[:, pl.ds(at, LANES)] for b in blocks], 0)
-        med_v = jnp.concatenate([b[:, pl.ds(at_v, LANES)] for b in blocks], 0)
         for odd in range(2):
             head = 2 * pair + odd
-            mine = half_lanes(tok_rows) if odd == 0 else ~half_lanes(tok_rows)
-            q_ext = jnp.where(mine, q_tile, hot_buf[...])
             mine_k = half_lanes(keys.shape[0]) if odd == 0 else ~half_lanes(keys.shape[0])
             k_ext = jnp.where(mine_k, keys, jnp.zeros_like(keys))
             merged = []
             for c in range(chunks):
                 s = dot_nt(
-                    k_ext[c * WINDOW : (c + 2) * WINDOW], q_ext[c * WINDOW : (c + 1) * WINDOW]
+                    k_ext[c * WINDOW : (c + 2) * WINDOW], q_tile[c * WINDOW : (c + 1) * WINDOW]
                 )
                 left, right = s[:WINDOW], s[WINDOW:]
                 if c == 0:
@@ -206,22 +202,73 @@
                 outs.append(dot(v_up[:, c * WINDOW : (c + 2) * WINDOW], both_parts))
             out = jnp.concatenate(outs, 1)
             factor = gate_ref[pl.ds(head, 1), :] / out[half : half + 1]
-            mixed = out[:half] * factor
-
+            mix_ref[pl.ds(pl.multiple_of(head * half, half), half), :] = out[:half] * factor
+
+
+def medium_kernel(
+    q_ref, gate_ref, old_hbm, far3_ref, far2_ref, far1_ref, med_ref, gid_ref, mix_ref,
+    old_ref, bias_buf, hot_buf, sem,
+):
+    tok_rows, inner = q_ref.shape
+    heads = gate_ref.shape[0] // 3
+    med_blocks = med_ref.shape[0]
+    near = (REACH + 1) * med_blocks
+    half = LANES // 2
+    fetch = pltpu.make_async_copy(old_hbm, old_ref, sem)
+    fetch.start()
+    position = (lax.axis_index(AX_X) * lax.axis_size(AX_Z) + lax.axis_index(AX_Z)) * lax.axis_size(
+        AX_C
+    ) + lax.axis_index(AX_C)
+    hot_buf[...] = token_classes(tok_rows, tok_rows // med_blocks)
+
+    first = (position - REACH) * med_blocks
+    padded = first + near
+    row = padded // LANES - 1
+    offset = padded % LANES
+    low = gid_ref[pl.ds(jnp.maximum(row, 0), 1), :]
+    high = gid_ref[pl.ds(jnp.minimum(row + 1, gid_ref.shape[0] - 1), 1), :]
+    lane = iota((1, LANES), 1)
+    both = jnp.where(lane >= offset, low, high)
+    near_groups = pltpu.roll(jnp.broadcast_to(both, (8, LANES)), (LANES - offset) % LANES, 1)[:1]
+    near_groups = jnp.where(lane + first >= 0, near_groups, -1).astype(F32)
+    spread = jnp.broadcast_to(near_groups, (near, LANES)).astype(BF16)
+    i0, i1 = iota((near, LANES), 0), iota((near, LANES), 1)
+    key_group = dot_nt(one_hot(i0 == i1), spread)
+    own = (i1 % half) // 2 + REACH * med_blocks
+    token_group = dot(spread, one_hot(i0 == own))
+    visible = (key_group == token_group) & ((i0 < own) | ((i0 == own) & (i1 % 2 == 1)))
+    bias_buf[...] = jnp.where(visible, 0.0, NEG).astype(BF16)
+    fetch.wait()
+
+    @pl.loop(0, heads // 2)
+    def _(pair):
+        at = pl.multiple_of(pair * LANES, LANES)
+        at_v = pl.multiple_of(inner + pair * LANES, LANES)
+        q_tile = q_ref[:, pl.ds(at, LANES)]
+        blocks = (far3_ref, far2_ref, far1_ref, med_ref)
+        med_k = jnp.concatenate([b[:, pl.ds(at, LANES)] for b in blocks], 0)
+        med_v = jnp.concatenate([b[:, pl.ds(at_v, LANES)] for b in blocks], 0)
+        for odd in range(2):
+            head = 2 * pair + odd
+            mine = half_lanes(tok_rows) if odd == 0 else ~half_lanes(tok_rows)
+            q_ext = jnp.where(mine, q_tile, hot_buf[...])
             mine_m = half_lanes(near) if odd == 0 else ~half_lanes(near)
             scores = dot_nt(jnp.where(mine_m, med_k, bias_buf[...]), q_ext)
             peak = jnp.maximum(jnp.max(scores, axis=0, keepdims=True), 0.0)
             terms = jnp.exp(scores - peak).astype(BF16)
             out = dot(values_up(med_v, odd), terms)
             factor = gate_ref[pl.ds(heads + head, 1), :] / (jnp.exp(-peak) + out[half : half + 1])
-            mixed = mixed + out[:half] * factor
-            mix_ref[pl.ds(pl.multiple_of(head * half, half), half), :] = mixed
+            rows = pl.ds(pl.multiple_of(head * half, half), half)
+            mix_ref[rows, :] = old_ref[rows, :] + out[:half] * factor
 
 
 def far_kernel(
-    q_ref, gate_ref, mix_ref, w_ref, *refs
+    q_ref, gate_ref, mix_ref, w_hbm, *refs
 ):
-    pieces, (out_ref, keys_buf, values_buf, bias_buf, hot_buf, mixed_buf) = refs[:-6], refs[-6:]
+    pieces, scratch = refs[:-8], refs[-8:]
+    out_ref, keys_buf, values_buf, bias_buf, hot_buf, mixed_buf, w_ref, sem = scratch
+    fetch = pltpu.make_async_copy(w_hbm, w_ref, sem)
+    fetch.start()
     tok_rows, inner = q_ref.shape
     heads = gate_ref.shape[0] // 3
     half = LANES // 2
@@ -275,6 +322,7 @@
             rows = pl.ds(pl.multiple_of(head * half, half), half)
             mixed_buf[rows, :] = (mix_ref[rows, :] + out[:half] * factor).astype(BF16)
 
+    fetch.wait()
     out_ref[...] = lax.dot_general(
         mixed_buf[...], w_ref[...], TN, preferred_element_type=F32
     ).astype(BF16)
@@ -291,11 +339,15 @@
 
 
 VMEM = pl.BlockSpec(memory_space=pltpu.VMEM)
-HBM = pl.BlockSpec(memory_space=pl.ANY)
-
-
-def params(mib):
-    return pltpu.CompilerParams(vmem_limit_bytes=mib << 20)
+HBM = pl.BlockSpec(memory_space=pltpu.HBM)
+
+
+def params(kib):
+    return pltpu.CompilerParams(vmem_limit_bytes=kib << 10)
+
+
+def cost(flops, moved):
+    return pl.CostEstimate(flops=int(flops), bytes_accessed=int(moved), transcendentals=0)
 
 
 def shards(tokens, w_qkv, w_gate, w_out, cmp_med, cmp_coarse, group_id):
@@ -310,6 +362,7 @@
     tail = shifted(tokens[tok_rows - WINDOW :], SEQ, 1)
 
     kv_steps = 2 * inner // width
+    cmp_med, cmp_coarse = cmp_med.transpose(1, 0, 2), cmp_coarse.transpose(1, 0, 2)
     kv, med, payload = pl.pallas_call(
         project_kernel,
         out_shape=(
@@ -317,50 +370,72 @@
             jax.ShapeDtypeStruct((med_blocks, 2 * inner), BF16),
             jax.ShapeDtypeStruct((zs * count, LANES), BF16),
         ),
-        in_specs=[VMEM, HBM, VMEM, VMEM],
-        out_specs=(VMEM, VMEM, VMEM),
+        in_specs=[HBM] * 4,
+        out_specs=(HBM, VMEM, VMEM),
         scratch_shapes=[
+            pltpu.VMEM(tokens.shape, BF16),
             pltpu.VMEM((kv_steps, depth, width), BF16),
+            pltpu.VMEM(cmp_med.shape, BF16),
+            pltpu.VMEM(cmp_coarse.shape, BF16),
+            pltpu.VMEM((kv_steps, tok_rows, width), BF16),
             pltpu.VMEM((count, LANES), F32),
             pltpu.SemaphoreType.DMA((kv_steps,)),
+            pltpu.SemaphoreType.DMA((3,)),
+            pltpu.SemaphoreType.DMA((kv_steps,)),
         ],
-        compiler_params=params(24),
-        cost_estimate=pl.CostEstimate(flops=2 * tok_rows * depth * 2 * inner, bytes_accessed=4 << 20, transcendentals=0),
+        compiler_params=params(62100),
+        cost_estimate=cost(4e9, 4e6),
         name="project",
-    )(tokens, w_qkv, cmp_med.transpose(1, 0, 2), cmp_coarse.transpose(1, 0, 2))
+    )(tokens, w_qkv, cmp_med, cmp_coarse)
 
     column = lax.all_to_all(payload, AX_Z, 0, 0, tiled=True)
     far1, far2, far3 = (shifted(med, SEQ, k) for k in (1, 2, 3))
 
     all_steps = 3 * inner // width
     q, gates, mixed = pl.pallas_call(
-        near_kernel,
+        window_kernel,
         out_shape=(
             jax.ShapeDtypeStruct((tok_rows, inner), BF16),
             jax.ShapeDtypeStruct((3 * heads, tok_rows), F32),
             jax.ShapeDtypeStruct((inner, tok_rows), F32),
         ),
-        in_specs=[VMEM, VMEM, HBM] + [VMEM] * 7,
+        in_specs=[HBM, VMEM, HBM, VMEM, HBM],
         out_specs=(VMEM, VMEM, VMEM),
         scratch_shapes=[
+            pltpu.VMEM(tokens.shape, BF16),
+            pltpu.VMEM((tok_rows, 2 * inner), BF16),
             pltpu.VMEM((all_steps, depth, width), BF16),
             pltpu.VMEM((WINDOW, 2 * inner), BF16),
+            pltpu.SemaphoreType.DMA((all_steps,)),
+            pltpu.SemaphoreType.DMA((2,)),
+        ],
+        compiler_params=params(54000),
+        cost_estimate=cost(8e9, 8e6),
+        name="window",
+    )(tokens, tail, w_qkv, w_gate.T, kv)
+
+    columns = [column] + [turned(column, AX_X, k) for k in range(1, lax.axis_size(AX_X))]
+    mixed = pl.pallas_call(
+        medium_kernel,
+        out_shape=jax.ShapeDtypeStruct((inner, tok_rows), F32),
+        in_specs=[VMEM, VMEM, HBM] + [VMEM] * 5,
+        out_specs=VMEM,
+        scratch_shapes=[
+            pltpu.VMEM((inner, tok_rows), F32),
             pltpu.VMEM(((REACH + 1) * med_blocks, LANES), BF16),
             pltpu.VMEM((tok_rows, LANES), BF16),
-            pltpu.SemaphoreType.DMA((all_steps,)),
+            pltpu.SemaphoreType.DMA,
         ],
-        compiler_params=params(30),
-        cost_estimate=pl.CostEstimate(flops=4 << 30, bytes_accessed=8 << 20, transcendentals=0),
-        name="near",
-    )(tokens, tail, w_qkv, w_gate.T, kv, far3, far2, far1, med, group_id.reshape(-1, LANES))
-
-    columns = [column] + [turned(column, AX_X, k) for k in range(1, lax.axis_size(AX_X))]
+        compiler_params=params(48000),
+        cost_estimate=cost(4e9, 4e6),
+        name="medium",
+    )(q, gates, mixed, far3, far2, far1, med, group_id.reshape(-1, LANES))
     columns += [turned(c, AX_C, 1) for c in columns]
     keys_count = coarse_blocks * lax.axis_size(SEQ)
     return pl.pallas_call(
         far_kernel,
         out_shape=jax.ShapeDtypeStruct((tok_rows, inner), BF16),
-        in_specs=[VMEM] * (4 + len(columns)),
+        in_specs=[VMEM] * 3 + [HBM] + [VMEM] * len(columns),
         out_specs=VMEM,
         scratch_shapes=[
             pltpu.VMEM((keys_count, inner), BF16),
@@ -368,15 +443,18 @@
             pltpu.VMEM((keys_count, LANES), BF16),
             pltpu.VMEM((tok_rows, LANES), BF16),
             pltpu.VMEM((inner, tok_rows), BF16),
+            pltpu.VMEM(w_out.shape, BF16),
+            pltpu.SemaphoreType.DMA,
         ],
-        compiler_params=params(24),
-        cost_estimate=pl.CostEstimate(flops=2 << 30, bytes_accessed=4 << 20, transcendentals=0),
+        compiler_params=params(48000),
+        cost_estimate=cost(4e9, 4e6),
         name="far",
     )(q, gates, mixed, w_out, *columns)
 
 
 def solution(mesh):
     torus = Mesh(mesh.devices.reshape(mesh.shape["rep"], 4, 16, 2), REP_SEQ)
+
     return jax.shard_map(
         shards,
         mesh=torus,

time: 82.7 us -> 79.4 us (0.960)
  Pallas kernels: 24.6 us -> 31 us
  waiting for transfers between devices: 5.54 us -> 0.03 us
  local copies, waits for them, and re-layouts: 6.56 us -> 2.36 us
    ppermute x7, waiting for transfers between devices: 5.53 us -> 0.02 us  [turned(): lax.ppermute(block, axis, [(i, (i + distance) % size) for i in range(size)])]
    unnamed x18 -> x10, local copies, waits for them, and re-layouts: 6.54 us -> 1.42 us
    pallas_call x1 -> x2, Pallas kernels: 11.4 us -> 15.8 us  [the longest x1 11.2 us: shards(): pl.pallas_call(window_kernel, out_shape=(jax.ShapeDtypeStruct((tok_rows,...]
    pallas_call x1, Pallas kernels: 5.69 us -> 7.44 us  [shards(): pl.pallas_call(project_kernel, out_shape=(jax.ShapeDtypeStruct((tok_rows,...]
    slice x1, local copies, waits for them, and re-layouts: 0.01 us -> 0.94 us  [shards(): tail = shifted(tokens[tok_rows - WINDOW:], SEQ, 1)]
  transfers between devices with their start and end apart: 12 -> 12, of which waited for: 2 -> 0; matrix products, arithmetic and copies ran while one was open for 0% -> 1% of each run, Pallas kernels for 14% -> 20%
where the time goes in v2:
time: 79.4 us; the launch traced here: 79.1 us
  starting transfers between devices  45.5 us (57%)
  Pallas kernels  31 us (39%)
  local copies, waits for them, and re-layouts  2.36 us (3%)
    all_to_all x1, starting transfers between devices, shards(): column = lax.all_to_all(payload, AX_Z, 0, 0, tiled=True)  24.5 us
    ppermute x4, starting transfers between devices, shifted(): lax.ppermute(block, axis, [(i - distance, i) for i in range(distance, siz...  15.3 us
    pallas_call x1, Pallas kernels, shards(): pl.pallas_call(window_kernel, out_shape=(jax.ShapeDtypeStruct((tok_rows,...  11.2 us
    pallas_call x1, Pallas kernels, shards(): pl.pallas_call(far_kernel, out_shape=jax.ShapeDtypeStruct((tok_rows, inne...  7.75 us
    pallas_call x1, Pallas kernels, shards(): pl.pallas_call(project_kernel, out_shape=(jax.ShapeDtypeStruct((tok_rows,...  7.44 us
    ppermute x7, starting transfers between devices, turned(): lax.ppermute(block, axis, [(i, (i + distance) % size) for i in range(size)])  5.72 us
    pallas_call x1, Pallas kernels, shards(): pl.pallas_call(medium_kernel, out_shape=jax.ShapeDtypeStruct((inner, tok_...  4.55 us
  transfers between devices with their start and end apart: 12, of which 0 were waited for; matrix products, arithmetic and copies ran while one was open for 1% of the time, Pallas kernels for 20%

profile of v2, /device:TPU:33, one launch (start us, length us, event | category | flops | bytes accessed | tf_op | source)
XLA Modules:
  0.0 79.1 jit_solution(1334433317772975679)
XLA Ops:
  0.0 0.0 copy-start.2
  0.0 7.4 %project.1 = (bf16[512,1536]{1,0:T(8,128)(2,1)}, bf16[32,1536]{1,0:T(8,128)(2,1)}, bf16[384,128]{1,0:T(8,128)(2,1)}) custom-call(bf16[512,768]{1,0:T(8,128)(2,1)} %tok_hbm.3, bf16[768,2304]{1,0:T(8,128)(2,1)} %w_hbm.4, bf16[12,2,16]{2,1,0:T(2,128)(2,1)} %bitcast.15, bf16[12,2,256]{2,1,0:T(2,128)(2,1)} %bitcast.14), custom_call_target="tpu_custom_call" | custom-call | flops 4000000000 | bytes 4000000 | tf_op jit(solution)/shard_map/project/pallas_call | solution.py:366
  7.4 24.5 %all-to-all-start = ((bf16[16,24,128]{2,1,0:T(8,128)(2,1)}), bf16[16,24,128]{2,1,0:T(8,128)(2,1)S(1)}, u32[]{:S(2)}, u32[]{:S(2)}) async-start(bf16[16,24,128]{2,1,0:T(8,128)(2,1)} %bitcast.13), calls=%async_computation | async-start | bytes 196608 | tf_op jit(solution)/shard_map/all_to_all | solution.py:391
  32.0 0.9 %slice.3 = bf16[128,768]{1,0:T(8,128)(2,1)S(1)} slice(bf16[512,768]{1,0:T(8,128)(2,1)} %tok_hbm.3), slice={[384:512], [0:768]} | slice | bytes 393216 | tf_op jit(solution)/shard_map/slice | solution.py:362
  32.9 4.1 %collective-permute-start = (bf16[128,768]{1,0:T(8,128)(2,1)S(1)}, bf16[128,768]{1,0:T(8,128)(2,1)S(1)}, u32[]{:S(2)}, u32[]{:S(2)}) collective-permute-start(bf16[128,768]{1,0:T(8,128)(2,1)S(1)} %slice.3), channel_id=1, source_target_pairs={{0,1},{1,2},{2,3},{3,4},{4,5},{5,6},{6,7},{7,8},{8,9},{9,10},{10,1... | collective-permute-start | bytes 589832 | tf_op jit(solution)/shard_map/ppermute | solution.py:333
  37.1 2.9 %collective-permute-start.1 = (bf16[32,1536]{1,0:T(8,128)(2,1)}, bf16[32,1536]{1,0:T(8,128)(2,1)S(1)}, u32[]{:S(2)}, u32[]{:S(2)}) collective-permute-start(bf16[32,1536]{1,0:T(8,128)(2,1)} %get-tuple-element.15.med_ref), channel_id=1, source_target_pairs={{0,3},{1,4},{2,5},{3,6},{4,7},{5,8},{6,9},{7,10},{8,11},{9,12},{10... | collective-permute-start | bytes 294920 | tf_op jit(solution)/shard_map/ppermute | solution.py:333
  39.9 3.1 %collective-permute-start.2 = (bf16[32,1536]{1,0:T(8,128)(2,1)}, bf16[32,1536]{1,0:T(8,128)(2,1)S(1)}, u32[]{:S(2)}, u32[]{:S(2)}) collective-permute-start(bf16[32,1536]{1,0:T(8,128)(2,1)} %get-tuple-element.15.med_ref), channel_id=1, source_target_pairs={{0,2},{1,3},{2,4},{3,5},{4,6},{5,7},{6,8},{7,9},{8,10},{9,11},{10,... | collective-permute-start | bytes 294920 | tf_op jit(solution)/shard_map/ppermute | solution.py:333
  43.1 5.2 %collective-permute-start.3 = (bf16[32,1536]{1,0:T(8,128)(2,1)}, bf16[32,1536]{1,0:T(8,128)(2,1)S(1)}, u32[]{:S(2)}, u32[]{:S(2)}) collective-permute-start(bf16[32,1536]{1,0:T(8,128)(2,1)} %get-tuple-element.15.med_ref), channel_id=1, source_target_pairs={{0,1},{1,2},{2,3},{3,4},{4,5},{5,6},{6,7},{7,8},{8,9},{9,10},{10,1... | collective-permute-start | bytes 294920 | tf_op jit(solution)/shard_map/ppermute | solution.py:333
  48.2 0.0 all-to-all-done
  48.3 3.0 %collective-permute-start.6 = (bf16[384,128]{1,0:T(8,128)(2,1)S(1)}, bf16[384,128]{1,0:T(8,128)(2,1)S(1)}, u32[]{:S(2)}, u32[]{:S(2)}) collective-permute-start(bf16[384,128]{1,0:T(8,128)(2,1)S(1)} %bitcast.6), channel_id=1, source_target_pairs={{0,96},{32,0},{64,32},{96,64},{1,97},{33,1},{65,33},{97,65},{2,98}... | collective-permute-start | bytes 294920 | tf_op jit(solution)/shard_map/ppermute | solution.py:338
  51.3 0.0 collective-permute-done.1.far3_ref
  51.3 0.0 collective-permute-start.4
  51.3 0.0 collective-permute-done.tail_ref
  51.3 1.6 %collective-permute-start.5 = (bf16[384,128]{1,0:T(8,128)(2,1)S(1)}, bf16[384,128]{1,0:T(8,128)(2,1)S(1)}, u32[]{:S(2)}, u32[]{:S(2)}) collective-permute-start(bf16[384,128]{1,0:T(8,128)(2,1)S(1)} %bitcast.8), channel_id=1, source_target_pairs={{0,64},{32,96},{64,0},{96,32},{1,65},{33,97},{65,1},{97,33},{2,66}... | collective-permute-start | bytes 294920 | tf_op jit(solution)/shard_map/ppermute | solution.py:338
  52.9 0.0 copy-done.2
  52.9 0.0 copy-start.1
  52.9 0.0 copy-start.3
  52.9 11.2 %window.1 = (bf16[512,768]{1,0:T(8,128)(2,1)S(1)}, f32[36,512]{1,0:T(8,128)S(1)}, f32[768,512]{1,0:T(8,128)}) custom-call(bf16[512,768]{1,0:T(8,128)(2,1)} %tok_hbm.3, bf16[128,768]{1,0:T(8,128)(2,1)S(1)} %collective-permute-done.tail_ref, bf16[768,2304]{1,0:T(8,128)(2,1)} %w_hbm.4, bf16[36,768]{1,0:T(8,128)(2,1)S(1)} %bitcast.11, ...), custom_call_target="tpu_custom_call" | custom-call | flops 8000000000 | bytes 8000000 | tf_op jit(solution)/shard_map/window/pallas_call | solution.py:395
  64.1 0.0 collective-permute-done.2.far2_ref
  64.1 0.1 collective-permute-start.7
  64.3 0.0 collective-permute-done.6.refs_3_
  64.3 0.5 collective-permute-start.10
  64.8 0.0 collective-permute-done.4.refs_1_
  64.8 0.2 collective-permute-start.8
  64.9 0.0 collective-permute-done.5.refs_2_
  64.9 0.4 collective-permute-start.9
  65.3 0.0 collective-permute-done.3.far1_ref
  65.3 0.0 copy-done.1
  65.3 0.0 copy-done.3
  65.3 0.0 copy-start.4
  65.3 1.4 %copy-done.4 = f32[768,512]{1,0:T(8,128)S(1)} copy-done((f32[768,512]{1,0:T(8,128)S(1)}, f32[768,512]{1,0:T(8,128)}, u32[]{:S(2)}) %copy-start.4) | copy-done | bytes 1572888
  66.7 0.0 copy-start
  66.7 4.6 %medium.1.mix_ref = f32[768,512]{1,0:T(8,128)S(1)} custom-call(bf16[512,768]{1,0:T(8,128)(2,1)S(1)} %get-tuple-element.12.q_ref, f32[36,512]{1,0:T(8,128)S(1)} %get-tuple-element.13.gate_ref, f32[768,512]{1,0:T(8,128)S(1)} %copy-done.4, bf16[32,1536]{1,0:T(8,128)(2,1)S(1)} %collective-permute-done.1.far3_ref, ...), custom_call_target="tpu_custom_call" | custom-call | flops 4000000000 | bytes 4000000 | tf_op jit(solution)/shard_map/medium/pallas_call | solution.py:418
  71.3 0.0 collective-permute-done.7.refs_4_
  71.3 0.0 collective-permute-done.10.refs_7_
  71.3 0.0 collective-permute-done.8.refs_5_
  71.3 0.0 collective-permute-done.9.refs_6_
  71.3 0.0 copy-done
  71.3 7.7 %far.1 = bf16[512,768]{1,0:T(8,128)(2,1)} custom-call(bf16[512,768]{1,0:T(8,128)(2,1)S(1)} %get-tuple-element.12.q_ref, f32[36,512]{1,0:T(8,128)S(1)} %get-tuple-element.13.gate_ref, f32[768,512]{1,0:T(8,128)S(1)} %medium.1.mix_ref, bf16[768,768]{1,0:T(8,128)(2,1)S(1)} %copy-done, bf16[384,128]{1,0:T(8,128)(2,1)S(1)} %bitcast.10, ...), custom_call_target="tpu_custom_call" | custom-call | flops 4000000000 | bytes 4000000 | tf_op jit(solution)/shard_map/far/pallas_call | solution.py:435
Async XLA Ops:
  0.0 52.9 %copy-start.2 = (bf16[768,36]{0,1:T(8,128)(2,1)S(1)}, bf16[768,36]{0,1:T(8,128)(2,1)}, u32[]{:S(2)}) copy-start(bf16[768,36]{0,1:T(8,128)(2,1)} %param.9) | copy-start | bytes 165892
  7.4 40.8 %all-to-all-start = ((bf16[16,24,128]{2,1,0:T(8,128)(2,1)}), bf16[16,24,128]{2,1,0:T(8,128)(2,1)S(1)}, u32[]{:S(2)}, u32[]{:S(2)}) async-start(bf16[16,24,128]{2,1,0:T(8,128)(2,1)} %bitcast.13), calls=%async_computation | async-start | bytes 196608 | tf_op jit(solution)/shard_map/all_to_all | solution.py:391
  32.9 18.3 %collective-permute-start = (bf16[128,768]{1,0:T(8,128)(2,1)S(1)}, bf16[128,768]{1,0:T(8,128)(2,1)S(1)}, u32[]{:S(2)}, u32[]{:S(2)}) collective-permute-start(bf16[128,768]{1,0:T(8,128)(2,1)S(1)} %slice.3), channel_id=1, source_target_pairs={{0,1},{1,2},{2,3},{3,4},{4,5},{5,6},{6,7},{7,8},{8,9},{9,10},{10,1... | collective-permute-start | bytes 589832 | tf_op jit(solution)/shard_map/ppermute | solution.py:333
  37.1 14.2 %collective-permute-start.1 = (bf16[32,1536]{1,0:T(8,128)(2,1)}, bf16[32,1536]{1,0:T(8,128)(2,1)S(1)}, u32[]{:S(2)}, u32[]{:S(2)}) collective-permute-start(bf16[32,1536]{1,0:T(8,128)(2,1)} %get-tuple-element.15.med_ref), channel_id=1, source_target_pairs={{0,3},{1,4},{2,5},{3,6},{4,7},{5,8},{6,9},{7,10},{8,11},{9,12},{10... | collective-permute-start | bytes 294920 | tf_op jit(solution)/shard_map/ppermute | solution.py:333
  39.9 24.2 %collective-permute-start.2 = (bf16[32,1536]{1,0:T(8,128)(2,1)}, bf16[32,1536]{1,0:T(8,128)(2,1)S(1)}, u32[]{:S(2)}, u32[]{:S(2)}) collective-permute-start(bf16[32,1536]{1,0:T(8,128)(2,1)} %get-tuple-element.15.med_ref), channel_id=1, source_target_pairs={{0,2},{1,3},{2,4},{3,5},{4,6},{5,7},{6,8},{7,9},{8,10},{9,11},{10,... | collective-permute-start | bytes 294920 | tf_op jit(solution)/shard_map/ppermute | solution.py:333
  43.1 22.2 %collective-permute-start.3 = (bf16[32,1536]{1,0:T(8,128)(2,1)}, bf16[32,1536]{1,0:T(8,128)(2,1)S(1)}, u32[]{:S(2)}, u32[]{:S(2)}) collective-permute-start(bf16[32,1536]{1,0:T(8,128)(2,1)} %get-tuple-element.15.med_ref), channel_id=1, source_target_pairs={{0,1},{1,2},{2,3},{3,4},{4,5},{5,6},{6,7},{7,8},{8,9},{9,10},{10,1... | collective-permute-start | bytes 294920 | tf_op jit(solution)/shard_map/ppermute | solution.py:333
  48.3 16.0 %collective-permute-start.6 = (bf16[384,128]{1,0:T(8,128)(2,1)S(1)}, bf16[384,128]{1,0:T(8,128)(2,1)S(1)}, u32[]{:S(2)}, u32[]{:S(2)}) collective-permute-start(bf16[384,128]{1,0:T(8,128)(2,1)S(1)} %bitcast.6), channel_id=1, source_target_pairs={{0,96},{32,0},{64,32},{96,64},{1,97},{33,1},{65,33},{97,65},{2,98}... | collective-permute-start | bytes 294920 | tf_op jit(solution)/shard_map/ppermute | solution.py:338
  51.3 13.5 %collective-permute-start.4 = (bf16[384,128]{1,0:T(8,128)(2,1)S(1)}, bf16[384,128]{1,0:T(8,128)(2,1)S(1)}, u32[]{:S(2)}, u32[]{:S(2)}) collective-permute-start(bf16[384,128]{1,0:T(8,128)(2,1)S(1)} %bitcast.7), channel_id=1, source_target_pairs={{0,32},{32,64},{64,96},{96,0},{1,33},{33,65},{65,97},{97,1},{2,34}... | collective-permute-start | bytes 294920 | tf_op jit(solution)/shard_map/ppermute | solution.py:338
  51.3 13.7 %collective-permute-start.5 = (bf16[384,128]{1,0:T(8,128)(2,1)S(1)}, bf16[384,128]{1,0:T(8,128)(2,1)S(1)}, u32[]{:S(2)}, u32[]{:S(2)}) collective-permute-start(bf16[384,128]{1,0:T(8,128)(2,1)S(1)} %bitcast.8), channel_id=1, source_target_pairs={{0,64},{32,96},{64,0},{96,32},{1,65},{33,97},{65,1},{97,33},{2,66}... | collective-permute-start | bytes 294920 | tf_op jit(solution)/shard_map/ppermute | solution.py:338
  52.9 12.4 %copy-start.1 = (bf16[32,1536]{1,0:T(8,128)(2,1)S(1)}, bf16[32,1536]{1,0:T(8,128)(2,1)}, u32[]{:S(2)}) copy-start(bf16[32,1536]{1,0:T(8,128)(2,1)} %get-tuple-element.15.med_ref) | copy-start | bytes 294916
  52.9 12.4 %copy-start.3 = (s32[4096]{0:T(1024)S(1)}, s32[4096]{0:T(1024)}, u32[]{:S(2)}) copy-start(s32[4096]{0:T(1024)} %param.13) | copy-start | bytes 49156
  64.1 7.1 %collective-permute-start.7 = (bf16[384,128]{1,0:T(8,128)(2,1)S(1)}, bf16[384,128]{1,0:T(8,128)(2,1)S(1)}, u32[]{:S(2)}, u32[]{:S(2)}) collective-permute-start(bf16[384,128]{1,0:T(8,128)(2,1)S(1)} %bitcast.9), channel_id=1, source_target_pairs={{0,1},{1,0},{2,3},{3,2},{4,5},{5,4},{6,7},{7,6},{8,9},{9,8},{10,11... | collective-permute-start | bytes 294920 | tf_op jit(solution)/shard_map/ppermute | solution.py:338
  64.3 7.0 %collective-permute-start.10 = (bf16[384,128]{1,0:T(8,128)(2,1)S(1)}, bf16[384,128]{1,0:T(8,128)(2,1)S(1)}, u32[]{:S(2)}, u32[]{:S(2)}) collective-permute-start(bf16[384,128]{1,0:T(8,128)(2,1)S(1)} %collective-permute-done.6.refs_3_), channel_id=1, source_target_pairs={{0,1},{1,0},{2,3},{3,2},{4,5},{5,4},{6,7},{7,6},{8,9},{9,8},{10,11... | collective-permute-start | bytes 294920 | tf_op jit(solution)/shard_map/ppermute | solution.py:338
  64.8 6.5 %collective-permute-start.8 = (bf16[384,128]{1,0:T(8,128)(2,1)S(1)}, bf16[384,128]{1,0:T(8,128)(2,1)S(1)}, u32[]{:S(2)}, u32[]{:S(2)}) collective-permute-start(bf16[384,128]{1,0:T(8,128)(2,1)S(1)} %collective-permute-done.4.refs_1_), channel_id=1, source_target_pairs={{0,1},{1,0},{2,3},{3,2},{4,5},{5,4},{6,7},{7,6},{8,9},{9,8},{10,11... | collective-permute-start | bytes 294920 | tf_op jit(solution)/shard_map/ppermute | solution.py:338
  64.9 6.4 %collective-permute-start.9 = (bf16[384,128]{1,0:T(8,128)(2,1)S(1)}, bf16[384,128]{1,0:T(8,128)(2,1)S(1)}, u32[]{:S(2)}, u32[]{:S(2)}) collective-permute-start(bf16[384,128]{1,0:T(8,128)(2,1)S(1)} %collective-permute-done.5.refs_2_), channel_id=1, source_target_pairs={{0,1},{1,0},{2,3},{3,2},{4,5},{5,4},{6,7},{7,6},{8,9},{9,8},{10,11... | collective-permute-start | bytes 294920 | tf_op jit(solution)/shard_map/ppermute | solution.py:338
  65.3 1.4 %copy-start.4 = (f32[768,512]{1,0:T(8,128)S(1)}, f32[768,512]{1,0:T(8,128)}, u32[]{:S(2)}) copy-start(f32[768,512]{1,0:T(8,128)} %get-tuple-element.14.old_hbm) | copy-start | bytes 4718596
  66.7 4.6 %copy-start = (bf16[768,768]{1,0:T(8,128)(2,1)S(1)}, bf16[768,768]{1,0:T(8,128)(2,1)}, u32[]{:S(2)}) copy-start(bf16[768,768]{1,0:T(8,128)(2,1)} %w_hbm.5) | copy-start | bytes 3538948

commit v3 on v2

--- a/solution.py
+++ b/solution.py
@@ -1,3 +1,5 @@
+import functools
+
 import jax
 import jax.numpy as jnp
 from jax import lax
@@ -45,7 +47,7 @@
 
 
 def project_kernel(
-    tok_hbm, w_hbm, cm_hbm, cc_hbm, kv_hbm, med_ref, pay_ref,
+    tok_hbm, w_hbm, cm_hbm, cc_hbm, kv_hbm, edge_ref, med_ref, pay_ref,
     tok_ref, w_buf, cm_ref, cc_ref, kv_ref, c_buf, sems, in_sems, out_sems,
 ):
     tok_rows = tok_ref.shape[0]
@@ -111,6 +113,8 @@
             at = per * med_blocks + 8 * i
             coarse = jnp.where(coarse_head == i, packed[at : at + 8], coarse)
         med_ref[:, g * width : (g + 1) * width] = med.astype(BF16)
+        edge_ref[WINDOW:, g * width : (g + 1) * width] = med.astype(BF16)
+        edge_ref[:WINDOW, g * width : (g + 1) * width] = rows[tok_rows - WINDOW :]
         for i in range(width // LANES):
             tile = g * (width // LANES) + i
             c_buf[tile * coarse_blocks : (tile + 1) * coarse_blocks, :] = coarse[
@@ -129,96 +133,109 @@
     return jnp.concatenate([turned[half * odd : half * (odd + 1)], ones], 0)
 
 
-def window_kernel(
-    tok_hbm, tail_ref, w_hbm, wg_ref, kv_hbm,
-    q_ref, gate_ref, mix_ref, tok_ref, kv_ref, w_buf, tail_buf, sems, in_sems,
-):
-    tok_rows, _ = tok_ref.shape
-    inner = kv_ref.shape[1] // 2
-    width = w_buf.shape[2]
-    steps = w_buf.shape[0]
-    heads = gate_ref.shape[0] // 3
-    half = LANES // 2
-    fetch = pltpu.make_async_copy(tok_hbm, tok_ref, in_sems.at[0])
-    fetch.start()
-    copies = []
-    for g in range(steps):
-        copies.append(
-            pltpu.make_async_copy(w_hbm.at[:, pl.ds(g * width, width)], w_buf.at[g], sems.at[g])
-        )
-        copies[-1].start()
-    fetch_kv = pltpu.make_async_copy(kv_hbm, kv_ref, in_sems.at[1])
-    fetch_kv.start()
-    position = (lax.axis_index(AX_X) * lax.axis_size(AX_Z) + lax.axis_index(AX_Z)) * lax.axis_size(
+def device_position():
+    return (lax.axis_index(AX_X) * lax.axis_size(AX_Z) + lax.axis_index(AX_Z)) * lax.axis_size(
         AX_C
     ) + lax.axis_index(AX_C)
-    fetch.wait()
-    gate_ref[...] = 1.0 / (1.0 + jnp.exp(-dot_nt(wg_ref[...], tok_ref[...])))
-    for g in range(steps):
-        copies[g].wait()
-        lo = g * width
-        if lo < inner:
+
+
+def window_scores(keys, q_tile, odd, first_bias=None):
+    below = iota((WINDOW, WINDOW), 0) <= iota((WINDOW, WINDOW), 1)
+    mine = half_lanes(keys.shape[0]) if odd == 0 else ~half_lanes(keys.shape[0])
+    k_ext = jnp.where(mine, keys, jnp.zeros_like(keys))
+    merged = []
+    for c in range(q_tile.shape[0] // WINDOW):
+        s = dot_nt(k_ext[c * WINDOW : (c + 2) * WINDOW], q_tile[c * WINDOW : (c + 1) * WINDOW])
+        left, right = s[:WINDOW], s[WINDOW:]
+        if first_bias is not None:
+            left = left + first_bias
+        merged.append(jnp.where(below, right, left))
+    return jnp.concatenate(merged, 1)
+
+
+def window_values(scores, v_up, gate):
+    below = iota((WINDOW, WINDOW), 0) <= iota((WINDOW, WINDOW), 1)
+    half = LANES // 2
+    terms = jnp.exp(scores - jnp.max(scores, axis=0, keepdims=True)).astype(BF16)
+    outs = []
+    for c in range(scores.shape[1] // WINDOW):
+        part = terms[:, c * WINDOW : (c + 1) * WINDOW]
+        zero = jnp.zeros_like(part)
+        both = jnp.concatenate([jnp.where(below, zero, part), jnp.where(below, part, zero)], 0)
+        outs.append(dot(v_up[:, c * WINDOW : (c + 2) * WINDOW], both))
+    out = jnp.concatenate(outs, 1)
+    return out[:half] * (gate / out[half : half + 1])
+
+
+def window_kernel(early, tok_hbm, w_hbm, wg_ref, kv_hbm, *refs):
+    (
+        q_hbm, gate_hbm, mix_hbm,
+        tok_ref, kv_ref, w_buf, q_ref, gate_ref, mix_ref, sems, in_sems, out_sems,
+    ) = refs[-12:]
+    low = lax.axis_index(AX_Z) < lax.axis_size(AX_Z) // 2
+
+    @pl.when(low if early else jnp.logical_not(low))
+    def _():
+        inner = kv_ref.shape[1] // 2
+        steps, _, width = w_buf.shape
+        heads = gate_ref.shape[0] // 3
+        half = LANES // 2
+        fetch = pltpu.make_async_copy(tok_hbm, tok_ref, in_sems.at[0])
+        fetch.start()
+        copies = []
+        for g in range(steps):
+            copies.append(
+                pltpu.make_async_copy(w_hbm.at[:, pl.ds(g * width, width)], w_buf.at[g], sems.at[g])
+            )
+            copies[-1].start()
+        fetch_kv = pltpu.make_async_copy(kv_hbm, kv_ref, in_sems.at[1])
+        fetch_kv.start()
+        fetch.wait()
+        gate_ref[...] = 1.0 / (1.0 + jnp.exp(-dot_nt(wg_ref[...], tok_ref[...])))
+        for g in range(steps):
+            copies[g].wait()
             rows = dot(tok_ref[...], w_buf[g]).astype(BF16).astype(F32)
-            q_ref[:, lo : lo + width] = (rows * (half**-0.5)).astype(BF16)
-        else:
-            tail_buf[:, lo - inner : lo - inner + width] = dot(tail_ref[...], w_buf[g]).astype(BF16)
-
-    fetch_kv.wait()
-    below = iota((WINDOW, WINDOW), 0) <= iota((WINDOW, WINDOW), 1)
-    chunks = tok_rows // WINDOW
-    first_bias = jnp.where(position == 0, NEG, 0.0)
-
-    @pl.loop(0, heads // 2)
-    def _(pair):
-        at = pl.multiple_of(pair * LANES, LANES)
-        at_v = pl.multiple_of(inner + pair * LANES, LANES)
-        q_tile = q_ref[:, pl.ds(at, LANES)]
-        keys = jnp.concatenate([tail_buf[:, pl.ds(at, LANES)], kv_ref[:, pl.ds(at, LANES)]], 0)
-        values = jnp.concatenate([tail_buf[:, pl.ds(at_v, LANES)], kv_ref[:, pl.ds(at_v, LANES)]], 0)
-        for odd in range(2):
-            head = 2 * pair + odd
-            mine_k = half_lanes(keys.shape[0]) if odd == 0 else ~half_lanes(keys.shape[0])
-            k_ext = jnp.where(mine_k, keys, jnp.zeros_like(keys))
-            merged = []
-            for c in range(chunks):
-                s = dot_nt(
-                    k_ext[c * WINDOW : (c + 2) * WINDOW], q_tile[c * WINDOW : (c + 1) * WINDOW]
+            q_ref[:, g * width : (g + 1) * width] = (rows * (half**-0.5)).astype(BF16)
+        fetch_kv.wait()
+
+        @pl.loop(0, heads // 2)
+        def _(pair):
+            at = pl.multiple_of(pair * LANES, LANES)
+            at_v = pl.multiple_of(inner + pair * LANES, LANES)
+            q_tile = q_ref[WINDOW:, pl.ds(at, LANES)]
+            keys = kv_ref[:, pl.ds(at, LANES)]
+            values = kv_ref[:, pl.ds(at_v, LANES)]
+            for odd in range(2):
+                head = 2 * pair + odd
+                scores = window_scores(keys, q_tile, odd)
+                mix_ref[pl.ds(pl.multiple_of(head * half, half), half), :] = window_values(
+                    scores, values_up(values, odd), gate_ref[pl.ds(head, 1), :][:, WINDOW:]
                 )
-                left, right = s[:WINDOW], s[WINDOW:]
-                if c == 0:
-                    left = left + first_bias
-                merged.append(jnp.where(below, right, left))
-            scores = jnp.concatenate(merged, 1)
-            peak = jnp.max(scores, axis=0, keepdims=True)
-            terms = jnp.exp(scores - peak).astype(BF16)
-            v_up = values_up(values, odd)
-            outs = []
-            for c in range(chunks):
-                part = terms[:, c * WINDOW : (c + 1) * WINDOW]
-                zero = jnp.zeros_like(part)
-                both_parts = jnp.concatenate(
-                    [jnp.where(below, zero, part), jnp.where(below, part, zero)], 0
-                )
-                outs.append(dot(v_up[:, c * WINDOW : (c + 2) * WINDOW], both_parts))
-            out = jnp.concatenate(outs, 1)
-            factor = gate_ref[pl.ds(head, 1), :] / out[half : half + 1]
-            mix_ref[pl.ds(pl.multiple_of(head * half, half), half), :] = out[:half] * factor
+
+        stores = [
+            pltpu.make_async_copy(src, dst, out_sems.at[n])
+            for n, (src, dst) in enumerate(((q_ref, q_hbm), (gate_ref, gate_hbm), (mix_ref, mix_hbm)))
+        ]
+        for store in stores:
+            store.start()
+        for store in stores:
+            store.wait()
 
 
 def medium_kernel(
-    q_ref, gate_ref, old_hbm, far3_ref, far2_ref, far1_ref, med_ref, gid_ref, mix_ref,
-    old_ref, bias_buf, hot_buf, sem,
+    q_hbm, gate_hbm, old_hbm, kv_hbm, far3_ref, far2_ref, edge_ref, med_ref, gid_ref, mix_ref,
+    q_ref, gate_ref, old_ref, kv_ref, bias_buf, hot_buf, sems,
 ):
     tok_rows, inner = q_ref.shape
     heads = gate_ref.shape[0] // 3
     med_blocks = med_ref.shape[0]
     near = (REACH + 1) * med_blocks
     half = LANES // 2
-    fetch = pltpu.make_async_copy(old_hbm, old_ref, sem)
-    fetch.start()
-    position = (lax.axis_index(AX_X) * lax.axis_size(AX_Z) + lax.axis_index(AX_Z)) * lax.axis_size(
-        AX_C
-    ) + lax.axis_index(AX_C)
+    moves = ((q_hbm, q_ref), (gate_hbm, gate_ref), (kv_hbm.at[pl.ds(0, WINDOW)], kv_ref), (old_hbm, old_ref))
+    fetches = [pltpu.make_async_copy(src, dst, sems.at[n]) for n, (src, dst) in enumerate(moves)]
+    for fetch in fetches:
+        fetch.start()
+    position = device_position()
     hot_buf[...] = token_classes(tok_rows, tok_rows // med_blocks)
 
     first = (position - REACH) * med_blocks
@@ -238,14 +255,20 @@
     token_group = dot(spread, one_hot(i0 == own))
     visible = (key_group == token_group) & ((i0 < own) | ((i0 == own) & (i1 % 2 == 1)))
     bias_buf[...] = jnp.where(visible, 0.0, NEG).astype(BF16)
-    fetch.wait()
+    first_bias = jnp.where(position == 0, NEG, 0.0)
+    for fetch in fetches:
+        fetch.wait()
 
     @pl.loop(0, heads // 2)
     def _(pair):
         at = pl.multiple_of(pair * LANES, LANES)
         at_v = pl.multiple_of(inner + pair * LANES, LANES)
         q_tile = q_ref[:, pl.ds(at, LANES)]
-        blocks = (far3_ref, far2_ref, far1_ref, med_ref)
+        keys = jnp.concatenate([edge_ref[:WINDOW, pl.ds(at, LANES)], kv_ref[:, pl.ds(at, LANES)]], 0)
+        values = jnp.concatenate(
+            [edge_ref[:WINDOW, pl.ds(at_v, LANES)], kv_ref[:, pl.ds(at_v, LANES)]], 0
+        )
+        blocks = (far3_ref, far2_ref, edge_ref.at[pl.ds(WINDOW, med_blocks)], med_ref)
         med_k = jnp.concatenate([b[:, pl.ds(at, LANES)] for b in blocks], 0)
         med_v = jnp.concatenate([b[:, pl.ds(at_v, LANES)] for b in blocks], 0)
         for odd in range(2):
@@ -254,21 +277,25 @@
             q_ext = jnp.where(mine, q_tile, hot_buf[...])
             mine_m = half_lanes(near) if odd == 0 else ~half_lanes(near)
             scores = dot_nt(jnp.where(mine_m, med_k, bias_buf[...]), q_ext)
+            rim_scores = window_scores(keys, q_tile[:WINDOW], odd, first_bias)
             peak = jnp.maximum(jnp.max(scores, axis=0, keepdims=True), 0.0)
             terms = jnp.exp(scores - peak).astype(BF16)
             out = dot(values_up(med_v, odd), terms)
             factor = gate_ref[pl.ds(heads + head, 1), :] / (jnp.exp(-peak) + out[half : half + 1])
+            rim = window_values(rim_scores, values_up(values, odd), gate_ref[pl.ds(head, 1), :][:, :WINDOW])
             rows = pl.ds(pl.multiple_of(head * half, half), half)
-            mix_ref[rows, :] = old_ref[rows, :] + out[:half] * factor
+            mix_ref[rows, :] = jnp.concatenate([rim, old_ref[rows, :]], 1) + out[:half] * factor
 
 
 def far_kernel(
-    q_ref, gate_ref, mix_ref, w_hbm, *refs
+    q_hbm, gate_hbm, mix_ref, w_hbm, *refs
 ):
-    pieces, scratch = refs[:-8], refs[-8:]
-    out_ref, keys_buf, values_buf, bias_buf, hot_buf, mixed_buf, w_ref, sem = scratch
-    fetch = pltpu.make_async_copy(w_hbm, w_ref, sem)
-    fetch.start()
+    pieces, scratch = refs[:-10], refs[-10:]
+    out_ref, keys_buf, values_buf, bias_buf, hot_buf, mixed_buf, w_ref, q_ref, gate_ref, sems = scratch
+    moves = ((q_hbm, q_ref), (gate_hbm, gate_ref), (w_hbm, w_ref))
+    fetches = [pltpu.make_async_copy(src, dst, sems.at[n]) for n, (src, dst) in enumerate(moves)]
+    for fetch in fetches:
+        fetch.start()
     tok_rows, inner = q_ref.shape
     heads = gate_ref.shape[0] // 3
     half = LANES // 2
@@ -302,6 +329,8 @@
         bias_buf[n * each : (n + 1) * each, :] = jnp.where(index < seen, 0.0, NEG).astype(BF16)
 
     keys_count = keys_buf.shape[0]
+    fetches[0].wait()
+    fetches[1].wait()
 
     @pl.loop(0, tiles)
     def _(pair):
@@ -322,7 +351,7 @@
             rows = pl.ds(pl.multiple_of(head * half, half), half)
             mixed_buf[rows, :] = (mix_ref[rows, :] + out[:half] * factor).astype(BF16)
 
-    fetch.wait()
+    fetches[2].wait()
     out_ref[...] = lax.dot_general(
         mixed_buf[...], w_ref[...], TN, preferred_element_type=F32
     ).astype(BF16)
@@ -359,19 +388,18 @@
     coarse_blocks = tok_rows // coarse_len
     zs = lax.axis_size(AX_Z)
     count = coarse_blocks * 2 * inner // LANES
-    tail = shifted(tokens[tok_rows - WINDOW :], SEQ, 1)
-
     kv_steps = 2 * inner // width
     cmp_med, cmp_coarse = cmp_med.transpose(1, 0, 2), cmp_coarse.transpose(1, 0, 2)
-    kv, med, payload = pl.pallas_call(
+    kv, edge, med, payload = pl.pallas_call(
         project_kernel,
         out_shape=(
             jax.ShapeDtypeStruct((tok_rows, 2 * inner), BF16),
+            jax.ShapeDtypeStruct((WINDOW + med_blocks, 2 * inner), BF16),
             jax.ShapeDtypeStruct((med_blocks, 2 * inner), BF16),
             jax.ShapeDtypeStruct((zs * count, LANES), BF16),
         ),
         in_specs=[HBM] * 4,
-        out_specs=(HBM, VMEM, VMEM),
+        out_specs=(HBM, VMEM, VMEM, VMEM),
         scratch_shapes=[
             pltpu.VMEM(tokens.shape, BF16),
             pltpu.VMEM((kv_steps, depth, width), BF16),
@@ -383,59 +411,66 @@
             pltpu.SemaphoreType.DMA((3,)),
             pltpu.SemaphoreType.DMA((kv_steps,)),
         ],
-        compiler_params=params(62100),
+        compiler_params=params(58000),
         cost_estimate=cost(4e9, 4e6),
         name="project",
     )(tokens, w_qkv, cmp_med, cmp_coarse)
 
+    q_steps = inner // width
+    window_shapes = (
+        jax.ShapeDtypeStruct((tok_rows, inner), BF16),
+        jax.ShapeDtypeStruct((3 * heads, tok_rows), F32),
+        jax.ShapeDtypeStruct((inner, tok_rows - WINDOW), F32),
+    )
+
+    def window(early, *given):
+        return pl.pallas_call(
+            functools.partial(window_kernel, early),
+            out_shape=window_shapes,
+            in_specs=[HBM, HBM, VMEM, HBM] + [HBM] * len(given),
+            out_specs=(HBM, HBM, HBM),
+            input_output_aliases={4 + n: n for n in range(len(given))},
+            scratch_shapes=[
+                pltpu.VMEM(tokens.shape, BF16),
+                pltpu.VMEM((tok_rows, 2 * inner), BF16),
+                pltpu.VMEM((q_steps, depth, width), BF16),
+                *(pltpu.VMEM(o.shape, o.dtype) for o in window_shapes),
+                pltpu.SemaphoreType.DMA((q_steps,)),
+                pltpu.SemaphoreType.DMA((2,)),
+                pltpu.SemaphoreType.DMA((3,)),
+            ],
+            compiler_params=params(54000),
+            cost_estimate=cost(8e9, 8e6),
+            name="window",
+        )(tokens, w_qkv, w_gate.T, kv, *given)
+
+    parts = window(True)
     column = lax.all_to_all(payload, AX_Z, 0, 0, tiled=True)
-    far1, far2, far3 = (shifted(med, SEQ, k) for k in (1, 2, 3))
-
-    all_steps = 3 * inner // width
-    q, gates, mixed = pl.pallas_call(
-        window_kernel,
-        out_shape=(
-            jax.ShapeDtypeStruct((tok_rows, inner), BF16),
-            jax.ShapeDtypeStruct((3 * heads, tok_rows), F32),
-            jax.ShapeDtypeStruct((inner, tok_rows), F32),
-        ),
-        in_specs=[HBM, VMEM, HBM, VMEM, HBM],
-        out_specs=(VMEM, VMEM, VMEM),
-        scratch_shapes=[
-            pltpu.VMEM(tokens.shape, BF16),
-            pltpu.VMEM((tok_rows, 2 * inner), BF16),
-            pltpu.VMEM((all_steps, depth, width), BF16),
-            pltpu.VMEM((WINDOW, 2 * inner), BF16),
-            pltpu.SemaphoreType.DMA((all_steps,)),
-            pltpu.SemaphoreType.DMA((2,)),
-        ],
-        compiler_params=params(54000),
-        cost_estimate=cost(8e9, 8e6),
-        name="window",
-    )(tokens, tail, w_qkv, w_gate.T, kv)
-
+    edge1, far2, far3 = shifted(edge, SEQ, 1), shifted(med, SEQ, 2), shifted(med, SEQ, 3)
+    q, gates, mixed = window(False, *parts)
     columns = [column] + [turned(column, AX_X, k) for k in range(1, lax.axis_size(AX_X))]
     mixed = pl.pallas_call(
         medium_kernel,
         out_shape=jax.ShapeDtypeStruct((inner, tok_rows), F32),
-        in_specs=[VMEM, VMEM, HBM] + [VMEM] * 5,
+        in_specs=[HBM] * 4 + [VMEM] * 5,
         out_specs=VMEM,
         scratch_shapes=[
-            pltpu.VMEM((inner, tok_rows), F32),
+            *(pltpu.VMEM(o.shape, o.dtype) for o in window_shapes),
+            pltpu.VMEM((WINDOW, 2 * inner), BF16),
             pltpu.VMEM(((REACH + 1) * med_blocks, LANES), BF16),
             pltpu.VMEM((tok_rows, LANES), BF16),
-            pltpu.SemaphoreType.DMA,
+            pltpu.SemaphoreType.DMA((4,)),
         ],
         compiler_params=params(48000),
         cost_estimate=cost(4e9, 4e6),
         name="medium",
-    )(q, gates, mixed, far3, far2, far1, med, group_id.reshape(-1, LANES))
+    )(q, gates, mixed, kv, far3, far2, edge1, med, group_id.reshape(-1, LANES))
     columns += [turned(c, AX_C, 1) for c in columns]
     keys_count = coarse_blocks * lax.axis_size(SEQ)
     return pl.pallas_call(
         far_kernel,
         out_shape=jax.ShapeDtypeStruct((tok_rows, inner), BF16),
-        in_specs=[VMEM] * 3 + [HBM] + [VMEM] * len(columns),
+        in_specs=[HBM, HBM, VMEM, HBM] + [VMEM] * len(columns),
         out_specs=VMEM,
         scratch_shapes=[
             pltpu.VMEM((keys_count, inner), BF16),
@@ -444,7 +479,8 @@
             pltpu.VMEM((tok_rows, LANES), BF16),
             pltpu.VMEM((inner, tok_rows), BF16),
             pltpu.VMEM(w_out.shape, BF16),
-            pltpu.SemaphoreType.DMA,
+            *(pltpu.VMEM(o.shape, o.dtype) for o in window_shapes[:2]),
+            pltpu.SemaphoreType.DMA((3,)),
         ],
         compiler_params=params(48000),
         cost_estimate=cost(4e9, 4e6),

time: 79.4 us -> 81.9 us (1.031)
  waiting for transfers between devices: 0.03 us -> 3.18 us
  starting transfers between devices: 45.5 us -> 46.9 us
  Pallas kernels: 31 us -> 29.9 us
  local copies, waits for them, and re-layouts: 2.36 us -> 1.28 us
    ppermute x7, starting transfers between devices: 5.72 us -> 11.7 us  [turned(): lax.ppermute(block, axis, [(i, (i + distance) % size) for i in range(size)])]
    all_to_all x1, starting transfers between devices: 24.5 us -> 20.6 us  [shards(): column = lax.all_to_all(payload, AX_Z, 0, 0, tiled=True)]
    all_to_all x1, waiting for transfers between devices: 0.01 us -> 3.16 us  [shards(): column = lax.all_to_all(payload, AX_Z, 0, 0, tiled=True)]
    pallas_call x1 -> x2, Pallas kernels: 11.2 us -> 8.62 us  [window(): pl.pallas_call(functools.partial(window_kernel, early), out_shape=window_...]
    pallas_call x1, Pallas kernels: 4.55 us -> 5.72 us  [shards(): pl.pallas_call(medium_kernel, out_shape=jax.ShapeDtypeStruct((inner, tok_...]
    slice x1 -> x0, local copies, waits for them, and re-layouts: 0.94 us -> none  [shards(): tail = shifted(tokens[tok_rows - WINDOW:], SEQ, 1)]
    ppermute x4 -> x3, starting transfers between devices: 15.3 us -> 14.7 us  [shifted(): lax.ppermute(block, axis, [(i - distance, i) for i in range(distance, siz...]
  transfers between devices with their start and end apart: 12 -> 11, of which waited for: 0 -> 1; matrix products, arithmetic and copies ran while one was open for 1% -> 0% of each run, Pallas kernels for 20% -> 18%
where the time goes in v3:
time: 81.9 us; the launch traced here: 81.6 us
  starting transfers between devices  46.9 us (57%)
  Pallas kernels  29.9 us (37%)
  waiting for transfers between devices  3.18 us (4%)
  local copies, waits for them, and re-layouts  1.28 us (2%)
    all_to_all x1, starting transfers between devices, shards(): column = lax.all_to_all(payload, AX_Z, 0, 0, tiled=True)  20.6 us
    ppermute x3, starting transfers between devices, shifted(): lax.ppermute(block, axis, [(i - distance, i) for i in range(distance, siz...  14.7 us
    ppermute x7, starting transfers between devices, turned(): lax.ppermute(block, axis, [(i, (i + distance) % size) for i in range(size)])  11.7 us
    pallas_call x2, Pallas kernels, window(): pl.pallas_call(functools.partial(window_kernel, early), out_shape=window_...  8.62 us
    pallas_call x1, Pallas kernels, shards(): pl.pallas_call(far_kernel, out_shape=jax.ShapeDtypeStruct((tok_rows, inne...  7.92 us
    pallas_call x1, Pallas kernels, shards(): pl.pallas_call(project_kernel, out_shape=(jax.ShapeDtypeStruct((tok_rows,...  7.64 us
    pallas_call x1, Pallas kernels, shards(): pl.pallas_call(medium_kernel, out_shape=jax.ShapeDtypeStruct((inner, tok_...  5.72 us
    all_to_all x1, waiting for transfers between devices, shards(): column = lax.all_to_all(payload, AX_Z, 0, 0, tiled=True)  3.16 us
  transfers between devices with their start and end apart: 11, of which 1 were waited for; matrix products, arithmetic and copies ran while one was open for 0% of the time, Pallas kernels for 18%

profile of v3, /device:TPU:33, one launch (start us, length us, event | category | flops | bytes accessed | tf_op | source)
XLA Modules:
  0.0 81.6 jit_solution(3851504594672854039)
XLA Ops:
  0.0 0.0 copy-start.2
  0.0 7.6 %project.1 = (bf16[512,1536]{1,0:T(8,128)(2,1)}, bf16[160,1536]{1,0:T(8,128)(2,1)}, bf16[32,1536]{1,0:T(8,128)(2,1)}, bf16[384,128]{1,0:T(8,128)(2,1)}) custom-call(bf16[512,768]{1,0:T(8,128)(2,1)} %tok_hbm.5, bf16[768,2304]{1,0:T(8,128)(2,1)} %w_hbm.6, bf16[12,2,16]{2,1,0:T(2,128)(2,1)} %bitcast.16, bf16[12,2,256]{2,1,0:T(2,128)(2,1)} %bitcast.15), custom_call_target="tpu_custom_call" | custom-call | flops 4000000000 | bytes 4000000 | tf_op jit(solution)/shard_map/project/pallas_call | solution.py:393
  7.7 8.0 %collective-permute-start = (bf16[32,1536]{1,0:T(8,128)(2,1)}, bf16[32,1536]{1,0:T(8,128)(2,1)S(1)}, u32[]{:S(2)}, u32[]{:S(2)}) collective-permute-start(bf16[32,1536]{1,0:T(8,128)(2,1)} %get-tuple-element.22.med_ref), channel_id=1, source_target_pairs={{0,3},{1,4},{2,5},{3,6},{4,7},{5,8},{6,9},{7,10},{8,11},{9,12},{10... | collective-permute-start | bytes 294920 | tf_op jit(solution)/shard_map/ppermute | solution.py:362
  15.6 4.4 %collective-permute-start.1 = (bf16[32,1536]{1,0:T(8,128)(2,1)}, bf16[32,1536]{1,0:T(8,128)(2,1)S(1)}, u32[]{:S(2)}, u32[]{:S(2)}) collective-permute-start(bf16[32,1536]{1,0:T(8,128)(2,1)} %get-tuple-element.22.med_ref), channel_id=1, source_target_pairs={{0,2},{1,3},{2,4},{3,5},{4,6},{5,7},{6,8},{7,9},{8,10},{9,11},{10,... | collective-permute-start | bytes 294920 | tf_op jit(solution)/shard_map/ppermute | solution.py:362
  20.1 2.3 %collective-permute-start.2 = (bf16[160,1536]{1,0:T(8,128)(2,1)}, bf16[160,1536]{1,0:T(8,128)(2,1)S(1)}, u32[]{:S(2)}, u32[]{:S(2)}) collective-permute-start(bf16[160,1536]{1,0:T(8,128)(2,1)} %get-tuple-element.23), channel_id=1, source_target_pairs={{0,1},{1,2},{2,3},{3,4},{4,5},{5,6},{6,7},{7,8},{8,9},{9,10},{10,1... | collective-permute-start | bytes 1474568 | tf_op jit(solution)/shard_map/ppermute | solution.py:362
  22.4 20.6 %all-to-all-start = ((bf16[16,24,128]{2,1,0:T(8,128)(2,1)}), bf16[16,24,128]{2,1,0:T(8,128)(2,1)S(1)}, u32[]{:S(2)}, u32[]{:S(2)}) async-start(bf16[16,24,128]{2,1,0:T(8,128)(2,1)} %bitcast.14), calls=%async_computation | async-start | bytes 196608 | tf_op jit(solution)/shard_map/all_to_all | solution.py:448
  42.9 0.0 copy-done.2
  42.9 8.5 %window.2 = (bf16[512,768]{1,0:T(8,128)(2,1)S(1)}, f32[36,512]{1,0:T(8,128)S(1)}, f32[768,384]{1,0:T(8,128)}) custom-call(bf16[512,768]{1,0:T(8,128)(2,1)} %tok_hbm.5, bf16[768,2304]{1,0:T(8,128)(2,1)} %w_hbm.6, bf16[36,768]{1,0:T(8,128)(2,1)S(1)} %bitcast.11, bf16[512,1536]{1,0:T(8,128)(2,1)} %get-tuple-element.15.kv_hbm), custom_call_target="tpu_custom_call" | custom-call | flops 8000000000 | bytes 8000000 | tf_op jit(solution)/shard_map/window/pallas_call | solution.py:427
  51.5 3.2 %all-to-all-done = bf16[16,24,128]{2,1,0:T(8,128)(2,1)S(1)} async-done(((bf16[16,24,128]{2,1,0:T(8,128)(2,1)}), bf16[16,24,128]{2,1,0:T(8,128)(2,1)S(1)}, u32[]{:S(2)}, u32[]{:S(2)}) %all-to-all-start) | async-done | bytes 98336 | tf_op jit(solution)/shard_map/all_to_all | solution.py:448
  54.6 1.3 %collective-permute-start.3 = (bf16[384,128]{1,0:T(8,128)(2,1)S(1)}, bf16[384,128]{1,0:T(8,128)(2,1)S(1)}, u32[]{:S(2)}, u32[]{:S(2)}) collective-permute-start(bf16[384,128]{1,0:T(8,128)(2,1)S(1)} %bitcast.6), channel_id=1, source_target_pairs={{0,32},{32,64},{64,96},{96,0},{1,33},{33,65},{65,97},{97,1},{2,34}... | collective-permute-start | bytes 294920 | tf_op jit(solution)/shard_map/ppermute | solution.py:367
  56.0 2.7 %collective-permute-start.4 = (bf16[384,128]{1,0:T(8,128)(2,1)S(1)}, bf16[384,128]{1,0:T(8,128)(2,1)S(1)}, u32[]{:S(2)}, u32[]{:S(2)}) collective-permute-start(bf16[384,128]{1,0:T(8,128)(2,1)S(1)} %bitcast.7), channel_id=1, source_target_pairs={{0,64},{32,96},{64,0},{96,32},{1,65},{33,97},{65,1},{97,33},{2,66}... | collective-permute-start | bytes 294920 | tf_op jit(solution)/shard_map/ppermute | solution.py:367
  58.7 0.0 collective-permute-done.far3_ref
  58.7 1.0 %collective-permute-start.5 = (bf16[384,128]{1,0:T(8,128)(2,1)S(1)}, bf16[384,128]{1,0:T(8,128)(2,1)S(1)}, u32[]{:S(2)}, u32[]{:S(2)}) collective-permute-start(bf16[384,128]{1,0:T(8,128)(2,1)S(1)} %bitcast.8), channel_id=1, source_target_pairs={{0,96},{32,0},{64,32},{96,64},{1,97},{33,1},{65,33},{97,65},{2,98}... | collective-permute-start | bytes 294920 | tf_op jit(solution)/shard_map/ppermute | solution.py:367
  59.7 0.0 copy-start.1
  59.7 0.0 copy-start.3
  59.7 0.0 copy-start.4
  59.7 0.1 window.3
  59.8 0.0 collective-permute-done.1.far2_ref
  59.8 3.5 %collective-permute-start.6 = (bf16[384,128]{1,0:T(8,128)(2,1)S(1)}, bf16[384,128]{1,0:T(8,128)(2,1)S(1)}, u32[]{:S(2)}, u32[]{:S(2)}) collective-permute-start(bf16[384,128]{1,0:T(8,128)(2,1)S(1)} %bitcast.9), channel_id=1, source_target_pairs={{0,1},{1,0},{2,3},{3,2},{4,5},{5,4},{6,7},{7,6},{8,9},{9,8},{10,11... | collective-permute-start | bytes 294920 | tf_op jit(solution)/shard_map/ppermute | solution.py:367
  63.3 0.0 collective-permute-done.3.refs_1_
  63.3 0.2 collective-permute-start.7
  63.5 0.0 collective-permute-done.4.refs_2_
  63.5 1.9 %collective-permute-start.8 = (bf16[384,128]{1,0:T(8,128)(2,1)S(1)}, bf16[384,128]{1,0:T(8,128)(2,1)S(1)}, u32[]{:S(2)}, u32[]{:S(2)}) collective-permute-start(bf16[384,128]{1,0:T(8,128)(2,1)S(1)} %collective-permute-done.4.refs_2_), channel_id=1, source_target_pairs={{0,1},{1,0},{2,3},{3,2},{4,5},{5,4},{6,7},{7,6},{8,9},{9,8},{10,11... | collective-permute-start | bytes 294920 | tf_op jit(solution)/shard_map/ppermute | solution.py:367
  65.5 0.0 collective-permute-done.5.refs_3_
  65.5 1.0 %collective-permute-start.9 = (bf16[384,128]{1,0:T(8,128)(2,1)S(1)}, bf16[384,128]{1,0:T(8,128)(2,1)S(1)}, u32[]{:S(2)}, u32[]{:S(2)}) collective-permute-start(bf16[384,128]{1,0:T(8,128)(2,1)S(1)} %collective-permute-done.5.refs_3_), channel_id=1, source_target_pairs={{0,1},{1,0},{2,3},{3,2},{4,5},{5,4},{6,7},{7,6},{8,9},{9,8},{10,11... | collective-permute-start | bytes 294920 | tf_op jit(solution)/shard_map/ppermute | solution.py:367
  66.4 0.0 collective-permute-done.2.edge_ref
  66.4 0.0 copy-done.1
  66.4 0.0 copy-done.3
  66.4 0.0 copy-done.4
  66.4 0.0 copy-start.5
  66.5 1.3 %copy-done.5 = f32[768,384]{1,0:T(8,128)S(1)} copy-done((f32[768,384]{1,0:T(8,128)S(1)}, f32[768,384]{1,0:T(8,128)}, u32[]{:S(2)}) %copy-start.5) | copy-done | bytes 1179672
  67.7 0.0 copy-start
  67.7 5.7 %medium.1.mix_ref = f32[768,512]{1,0:T(8,128)S(1)} custom-call(bf16[512,768]{1,0:T(8,128)(2,1)S(1)} %get-tuple-element.19.q_hbm, f32[36,512]{1,0:T(8,128)S(1)} %get-tuple-element.20.gate_hbm, f32[768,384]{1,0:T(8,128)S(1)} %copy-done.5, bf16[512,1536]{1,0:T(8,128)(2,1)S(1)} %copy-done.4, bf16[32,1536]{1,0:T(8,128)(2,1)S(1)} %collective-permute-done.far3_ref, ...), custom_call_target="tpu_custom_call" | custom-call | flops 4000000000 | bytes 4000000 | tf_op jit(solution)/shard_map/medium/pallas_call | solution.py:452
  73.5 0.0 collective-permute-done.6.refs_4_
  73.5 0.0 collective-permute-done.7.refs_5_
  73.5 0.0 collective-permute-done.8.refs_6_
  73.5 0.0 collective-permute-done.9.refs_7_
  73.5 0.0 copy-done
  73.5 7.9 %far.1 = bf16[512,768]{1,0:T(8,128)(2,1)} custom-call(bf16[512,768]{1,0:T(8,128)(2,1)S(1)} %get-tuple-element.19.q_hbm, f32[36,512]{1,0:T(8,128)S(1)} %get-tuple-element.20.gate_hbm, f32[768,512]{1,0:T(8,128)S(1)} %medium.1.mix_ref, bf16[768,768]{1,0:T(8,128)(2,1)S(1)} %copy-done, bf16[384,128]{1,0:T(8,128)(2,1)S(1)} %bitcast.10, ...), custom_call_target="tpu_custom_call" | custom-call | flops 4000000000 | bytes 4000000 | tf_op jit(solution)/shard_map/far/pallas_call | solution.py:470
Async XLA Ops:
  0.0 42.9 %copy-start.2 = (bf16[768,36]{0,1:T(8,128)(2,1)S(1)}, bf16[768,36]{0,1:T(8,128)(2,1)}, u32[]{:S(2)}) copy-start(bf16[768,36]{0,1:T(8,128)(2,1)} %param.9) | copy-start | bytes 165892
  7.7 51.1 %collective-permute-start = (bf16[32,1536]{1,0:T(8,128)(2,1)}, bf16[32,1536]{1,0:T(8,128)(2,1)S(1)}, u32[]{:S(2)}, u32[]{:S(2)}) collective-permute-start(bf16[32,1536]{1,0:T(8,128)(2,1)} %get-tuple-element.22.med_ref), channel_id=1, source_target_pairs={{0,3},{1,4},{2,5},{3,6},{4,7},{5,8},{6,9},{7,10},{8,11},{9,12},{10... | collective-permute-start | bytes 294920 | tf_op jit(solution)/shard_map/ppermute | solution.py:362
  15.6 44.2 %collective-permute-start.1 = (bf16[32,1536]{1,0:T(8,128)(2,1)}, bf16[32,1536]{1,0:T(8,128)(2,1)S(1)}, u32[]{:S(2)}, u32[]{:S(2)}) collective-permute-start(bf16[32,1536]{1,0:T(8,128)(2,1)} %get-tuple-element.22.med_ref), channel_id=1, source_target_pairs={{0,2},{1,3},{2,4},{3,5},{4,6},{5,7},{6,8},{7,9},{8,10},{9,11},{10,... | collective-permute-start | bytes 294920 | tf_op jit(solution)/shard_map/ppermute | solution.py:362
  20.1 46.4 %collective-permute-start.2 = (bf16[160,1536]{1,0:T(8,128)(2,1)}, bf16[160,1536]{1,0:T(8,128)(2,1)S(1)}, u32[]{:S(2)}, u32[]{:S(2)}) collective-permute-start(bf16[160,1536]{1,0:T(8,128)(2,1)} %get-tuple-element.23), channel_id=1, source_target_pairs={{0,1},{1,2},{2,3},{3,4},{4,5},{5,6},{6,7},{7,8},{8,9},{9,10},{10,1... | collective-permute-start | bytes 1474568 | tf_op jit(solution)/shard_map/ppermute | solution.py:362
  22.4 32.3 %all-to-all-start = ((bf16[16,24,128]{2,1,0:T(8,128)(2,1)}), bf16[16,24,128]{2,1,0:T(8,128)(2,1)S(1)}, u32[]{:S(2)}, u32[]{:S(2)}) async-start(bf16[16,24,128]{2,1,0:T(8,128)(2,1)} %bitcast.14), calls=%async_computation | async-start | bytes 196608 | tf_op jit(solution)/shard_map/all_to_all | solution.py:448
  54.6 8.7 %collective-permute-start.3 = (bf16[384,128]{1,0:T(8,128)(2,1)S(1)}, bf16[384,128]{1,0:T(8,128)(2,1)S(1)}, u32[]{:S(2)}, u32[]{:S(2)}) collective-permute-start(bf16[384,128]{1,0:T(8,128)(2,1)S(1)} %bitcast.6), channel_id=1, source_target_pairs={{0,32},{32,64},{64,96},{96,0},{1,33},{33,65},{65,97},{97,1},{2,34}... | collective-permute-start | bytes 294920 | tf_op jit(solution)/shard_map/ppermute | solution.py:367
  56.0 7.5 %collective-permute-start.4 = (bf16[384,128]{1,0:T(8,128)(2,1)S(1)}, bf16[384,128]{1,0:T(8,128)(2,1)S(1)}, u32[]{:S(2)}, u32[]{:S(2)}) collective-permute-start(bf16[384,128]{1,0:T(8,128)(2,1)S(1)} %bitcast.7), channel_id=1, source_target_pairs={{0,64},{32,96},{64,0},{96,32},{1,65},{33,97},{65,1},{97,33},{2,66}... | collective-permute-start | bytes 294920 | tf_op jit(solution)/shard_map/ppermute | solution.py:367
  58.7 6.7 %collective-permute-start.5 = (bf16[384,128]{1,0:T(8,128)(2,1)S(1)}, bf16[384,128]{1,0:T(8,128)(2,1)S(1)}, u32[]{:S(2)}, u32[]{:S(2)}) collective-permute-start(bf16[384,128]{1,0:T(8,128)(2,1)S(1)} %bitcast.8), channel_id=1, source_target_pairs={{0,96},{32,0},{64,32},{96,64},{1,97},{33,1},{65,33},{97,65},{2,98}... | collective-permute-start | bytes 294920 | tf_op jit(solution)/shard_map/ppermute | solution.py:367
  59.7 6.7 %copy-start.1 = (bf16[32,1536]{1,0:T(8,128)(2,1)S(1)}, bf16[32,1536]{1,0:T(8,128)(2,1)}, u32[]{:S(2)}) copy-start(bf16[32,1536]{1,0:T(8,128)(2,1)} %get-tuple-element.22.med_ref) | copy-start | bytes 294916
  59.7 6.7 %copy-start.3 = (s32[4096]{0:T(1024)S(1)}, s32[4096]{0:T(1024)}, u32[]{:S(2)}) copy-start(s32[4096]{0:T(1024)} %param.13) | copy-start | bytes 49156
  59.7 6.7 %copy-start.4 = (bf16[512,1536]{1,0:T(8,128)(2,1)S(1)}, bf16[512,1536]{1,0:T(8,128)(2,1)}, u32[]{:S(2)}) copy-start(bf16[512,1536]{1,0:T(8,128)(2,1)} %get-tuple-element.15.kv_hbm) | copy-start | bytes 4718596
  59.8 13.6 %collective-permute-start.6 = (bf16[384,128]{1,0:T(8,128)(2,1)S(1)}, bf16[384,128]{1,0:T(8,128)(2,1)S(1)}, u32[]{:S(2)}, u32[]{:S(2)}) collective-permute-start(bf16[384,128]{1,0:T(8,128)(2,1)S(1)} %bitcast.9), channel_id=1, source_target_pairs={{0,1},{1,0},{2,3},{3,2},{4,5},{5,4},{6,7},{7,6},{8,9},{9,8},{10,11... | collective-permute-start | bytes 294920 | tf_op jit(solution)/shard_map/ppermute | solution.py:367
  63.3 10.1 %collective-permute-start.7 = (bf16[384,128]{1,0:T(8,128)(2,1)S(1)}, bf16[384,128]{1,0:T(8,128)(2,1)S(1)}, u32[]{:S(2)}, u32[]{:S(2)}) collective-permute-start(bf16[384,128]{1,0:T(8,128)(2,1)S(1)} %collective-permute-done.3.refs_1_), channel_id=1, source_target_pairs={{0,1},{1,0},{2,3},{3,2},{4,5},{5,4},{6,7},{7,6},{8,9},{9,8},{10,11... | collective-permute-start | bytes 294920 | tf_op jit(solution)/shard_map/ppermute | solution.py:367
  63.5 10.0 %collective-permute-start.8 = (bf16[384,128]{1,0:T(8,128)(2,1)S(1)}, bf16[384,128]{1,0:T(8,128)(2,1)S(1)}, u32[]{:S(2)}, u32[]{:S(2)}) collective-permute-start(bf16[384,128]{1,0:T(8,128)(2,1)S(1)} %collective-permute-done.4.refs_2_), channel_id=1, source_target_pairs={{0,1},{1,0},{2,3},{3,2},{4,5},{5,4},{6,7},{7,6},{8,9},{9,8},{10,11... | collective-permute-start | bytes 294920 | tf_op jit(solution)/shard_map/ppermute | solution.py:367
  65.5 8.0 %collective-permute-start.9 = (bf16[384,128]{1,0:T(8,128)(2,1)S(1)}, bf16[384,128]{1,0:T(8,128)(2,1)S(1)}, u32[]{:S(2)}, u32[]{:S(2)}) collective-permute-start(bf16[384,128]{1,0:T(8,128)(2,1)S(1)} %collective-permute-done.5.refs_3_), channel_id=1, source_target_pairs={{0,1},{1,0},{2,3},{3,2},{4,5},{5,4},{6,7},{7,6},{8,9},{9,8},{10,11... | collective-permute-start | bytes 294920 | tf_op jit(solution)/shard_map/ppermute | solution.py:367
  66.4 1.3 %copy-start.5 = (f32[768,384]{1,0:T(8,128)S(1)}, f32[768,384]{1,0:T(8,128)}, u32[]{:S(2)}) copy-start(f32[768,384]{1,0:T(8,128)} %get-tuple-element.21.old_hbm) | copy-start | bytes 3538948
  67.7 5.8 %copy-start = (bf16[768,768]{1,0:T(8,128)(2,1)S(1)}, bf16[768,768]{1,0:T(8,128)(2,1)}, u32[]{:S(2)}) copy-start(bf16[768,768]{1,0:T(8,128)(2,1)} %w_hbm.7) | copy-start | bytes 3538948

commit v4 on v3

--- a/solution.py
+++ b/solution.py
@@ -54,8 +54,7 @@
     _, _, med_len = cm_ref.shape
     coarse_len = cc_ref.shape[2]
     inner = kv_hbm.shape[1] // 2
-    width = w_buf.shape[2]
-    steps = w_buf.shape[0]
+    steps, _, width = kv_ref.shape
     fetches = [
         pltpu.make_async_copy(src, dst, in_sems.at[n])
         for n, (src, dst) in enumerate(((cm_hbm, cm_ref), (cc_hbm, cc_ref), (tok_hbm, tok_ref)))
@@ -63,9 +62,12 @@
     for fetch in fetches:
         fetch.start()
     copies = []
+    chunk = w_buf.shape[0] // steps
     for g in range(steps):
-        columns = pl.ds(inner + g * width, width)
-        copies.append(pltpu.make_async_copy(w_hbm.at[:, columns], w_buf.at[g], sems.at[g]))
+        part = pl.ds(g * chunk, chunk)
+        copies.append(
+            pltpu.make_async_copy(w_hbm.at[part, pl.ds(inner, 2 * inner)], w_buf.at[part], sems.at[g])
+        )
         copies[-1].start()
     med_blocks = tok_rows // med_len
     coarse_blocks = tok_rows // coarse_len
@@ -95,9 +97,11 @@
         mixes.append(jnp.concatenate([med_mix] + coarse_rows, 0).astype(BF16))
     fetches[2].wait()
     stores = []
+    for copy in copies:
+        copy.wait()
+    all_rows = dot(tok_ref[...], w_buf[...]).astype(BF16)
     for g in range(steps):
-        copies[g].wait()
-        rows = dot(tok_ref[...], w_buf[g]).astype(BF16)
+        rows = all_rows[:, g * width : (g + 1) * width]
         kv_ref[g] = rows
         stores.append(
             pltpu.make_async_copy(kv_ref.at[g], kv_hbm.at[:, pl.ds(g * width, width)], out_sems.at[g])
@@ -177,7 +181,8 @@
     @pl.when(low if early else jnp.logical_not(low))
     def _():
         inner = kv_ref.shape[1] // 2
-        steps, _, width = w_buf.shape
+        steps = sems.shape[0]
+        chunk = w_buf.shape[0] // steps
         heads = gate_ref.shape[0] // 3
         half = LANES // 2
         fetch = pltpu.make_async_copy(tok_hbm, tok_ref, in_sems.at[0])
@@ -185,17 +190,21 @@
         copies = []
         for g in range(steps):
             copies.append(
-                pltpu.make_async_copy(w_hbm.at[:, pl.ds(g * width, width)], w_buf.at[g], sems.at[g])
+                pltpu.make_async_copy(
+                    w_hbm.at[pl.ds(g * chunk, chunk), pl.ds(0, inner)],
+                    w_buf.at[pl.ds(g * chunk, chunk)],
+                    sems.at[g],
+                )
             )
             copies[-1].start()
         fetch_kv = pltpu.make_async_copy(kv_hbm, kv_ref, in_sems.at[1])
         fetch_kv.start()
         fetch.wait()
         gate_ref[...] = 1.0 / (1.0 + jnp.exp(-dot_nt(wg_ref[...], tok_ref[...])))
-        for g in range(steps):
-            copies[g].wait()
-            rows = dot(tok_ref[...], w_buf[g]).astype(BF16).astype(F32)
-            q_ref[:, g * width : (g + 1) * width] = (rows * (half**-0.5)).astype(BF16)
+        for copy in copies:
+            copy.wait()
+        rows = dot(tok_ref[...], w_buf[...]).astype(BF16).astype(F32)
+        q_ref[...] = (rows * (half**-0.5)).astype(BF16)
         fetch_kv.wait()
 
         @pl.loop(0, heads // 2)
@@ -259,7 +268,7 @@
     for fetch in fetches:
         fetch.wait()
 
-    @pl.loop(0, heads // 2)
+    @pl.loop(0, heads // 2, unroll=heads // 2)
     def _(pair):
         at = pl.multiple_of(pair * LANES, LANES)
         at_v = pl.multiple_of(inner + pair * LANES, LANES)
@@ -271,20 +280,36 @@
         blocks = (far3_ref, far2_ref, edge_ref.at[pl.ds(WINDOW, med_blocks)], med_ref)
         med_k = jnp.concatenate([b[:, pl.ds(at, LANES)] for b in blocks], 0)
         med_v = jnp.concatenate([b[:, pl.ds(at_v, LANES)] for b in blocks], 0)
+        both = dot_nt(pair_keys(med_k, bias_buf[...]), jnp.concatenate([q_tile, hot_buf[...]], 1))
+        mine = half_lanes(2 * WINDOW)
+        none = jnp.zeros_like(keys)
+        rim_keys = jnp.concatenate([jnp.where(mine, keys, none), jnp.where(mine, none, keys)], 0)
+        rims = dot_nt(rim_keys, q_tile[:WINDOW])
+        below = iota((WINDOW, WINDOW), 0) <= iota((WINDOW, WINDOW), 1)
         for odd in range(2):
             head = 2 * pair + odd
-            mine = half_lanes(tok_rows) if odd == 0 else ~half_lanes(tok_rows)
-            q_ext = jnp.where(mine, q_tile, hot_buf[...])
-            mine_m = half_lanes(near) if odd == 0 else ~half_lanes(near)
-            scores = dot_nt(jnp.where(mine_m, med_k, bias_buf[...]), q_ext)
-            rim_scores = window_scores(keys, q_tile[:WINDOW], odd, first_bias)
+            scores = both[odd * near : (odd + 1) * near]
             peak = jnp.maximum(jnp.max(scores, axis=0, keepdims=True), 0.0)
             terms = jnp.exp(scores - peak).astype(BF16)
             out = dot(values_up(med_v, odd), terms)
             factor = gate_ref[pl.ds(heads + head, 1), :] / (jnp.exp(-peak) + out[half : half + 1])
-            rim = window_values(rim_scores, values_up(values, odd), gate_ref[pl.ds(head, 1), :][:, :WINDOW])
+            at_rim = 2 * odd * WINDOW
+            left, right = rims[at_rim : at_rim + WINDOW], rims[at_rim + WINDOW : at_rim + 2 * WINDOW]
+            rim = window_values(
+                jnp.where(below, right, left + first_bias),
+                values_up(values, odd),
+                gate_ref[pl.ds(head, 1), :][:, :WINDOW],
+            )
             rows = pl.ds(pl.multiple_of(head * half, half), half)
             mix_ref[rows, :] = jnp.concatenate([rim, old_ref[rows, :]], 1) + out[:half] * factor
+
+
+def pair_keys(keys, bias):
+    mine = half_lanes(keys.shape[0])
+    none = jnp.zeros_like(keys)
+    bias = jnp.where(mine, bias, none)
+    even = jnp.concatenate([jnp.where(mine, keys, none), bias], 1)
+    return jnp.concatenate([even, jnp.concatenate([jnp.where(mine, none, keys), bias], 1)], 0)
 
 
 def far_kernel(
@@ -332,18 +357,15 @@
     fetches[0].wait()
     fetches[1].wait()
 
-    @pl.loop(0, tiles)
+    @pl.loop(0, tiles, unroll=tiles)
     def _(pair):
         at = pl.multiple_of(pair * LANES, LANES)
-        q_tile = q_ref[:, pl.ds(at, LANES)]
-        keys = keys_buf[:, pl.ds(at, LANES)]
+        q_ext = jnp.concatenate([q_ref[:, pl.ds(at, LANES)], hot_buf[...]], 1)
         values = values_buf[:, pl.ds(at, LANES)]
+        both = dot_nt(pair_keys(keys_buf[:, pl.ds(at, LANES)], bias_buf[...]), q_ext)
         for odd in range(2):
             head = 2 * pair + odd
-            mine = half_lanes(tok_rows) if odd == 0 else ~half_lanes(tok_rows)
-            q_ext = jnp.where(mine, q_tile, hot_buf[...])
-            mine_k = half_lanes(keys_count) if odd == 0 else ~half_lanes(keys_count)
-            scores = dot_nt(jnp.where(mine_k, keys, bias_buf[...]), q_ext)
+            scores = both[odd * keys_count : (odd + 1) * keys_count]
             peak = jnp.maximum(jnp.max(scores, axis=0, keepdims=True), 0.0)
             terms = jnp.exp(scores - peak).astype(BF16)
             out = dot(values_up(values, odd), terms)
@@ -402,7 +424,7 @@
         out_specs=(HBM, VMEM, VMEM, VMEM),
         scratch_shapes=[
             pltpu.VMEM(tokens.shape, BF16),
-            pltpu.VMEM((kv_steps, depth, width), BF16),
+            pltpu.VMEM((depth, 2 * inner), BF16),
             pltpu.VMEM(cmp_med.shape, BF16),
             pltpu.VMEM(cmp_coarse.shape, BF16),
             pltpu.VMEM((kv_steps, tok_rows, width), BF16),
@@ -433,7 +455,7 @@
             scratch_shapes=[
                 pltpu.VMEM(tokens.shape, BF16),
                 pltpu.VMEM((tok_rows, 2 * inner), BF16),
-                pltpu.VMEM((q_steps, depth, width), BF16),
+                pltpu.VMEM((depth, inner), BF16),
                 *(pltpu.VMEM(o.shape, o.dtype) for o in window_shapes),
                 pltpu.SemaphoreType.DMA((q_steps,)),
                 pltpu.SemaphoreType.DMA((2,)),
@@ -446,7 +468,8 @@
 
     parts = window(True)
     column = lax.all_to_all(payload, AX_Z, 0, 0, tiled=True)
-    edge1, far2, far3 = shifted(edge, SEQ, 1), shifted(med, SEQ, 2), shifted(med, SEQ, 3)
+    edge1 = shifted(edge, SEQ, 1)
+    far2, far3 = shifted(med, SEQ, 2), shifted(med, SEQ, 3)
     q, gates, mixed = window(False, *parts)
     columns = [column] + [turned(column, AX_X, k) for k in range(1, lax.axis_size(AX_X))]
     mixed = pl.pallas_call(
@@ -461,7 +484,7 @@
             pltpu.VMEM((tok_rows, LANES), BF16),
             pltpu.SemaphoreType.DMA((4,)),
         ],
-        compiler_params=params(48000),
+        compiler_params=params(50000),
         cost_estimate=cost(4e9, 4e6),
         name="medium",
     )(q, gates, mixed, kv, far3, far2, edge1, med, group_id.reshape(-1, LANES))

time: 81.9 us -> 75.4 us (0.921)
  Pallas kernels: 29.9 us -> 22.7 us
    pallas_call x1, Pallas kernels: 7.64 us -> 5.07 us  [shards(): pl.pallas_call(project_kernel, out_shape=(jax.ShapeDtypeStruct((tok_rows,...]
    pallas_call x1, Pallas kernels: 5.72 us -> 3.58 us  [shards(): pl.pallas_call(medium_kernel, out_shape=jax.ShapeDtypeStruct((inner, tok_...]
    pallas_call x1, Pallas kernels: 7.92 us -> 6.14 us  [shards(): pl.pallas_call(far_kernel, out_shape=jax.ShapeDtypeStruct((tok_rows, inne...]
  transfers between devices with their start and end apart: 11 -> 11, of which waited for: 1 -> 1; matrix products, arithmetic and copies ran while one was open for 0% -> 0% of each run, Pallas kernels for 18% -> 15%
where the time goes in v4:
time: 75.4 us; the launch traced here: 75.1 us
  starting transfers between devices  46.9 us (62%)
  Pallas kernels  22.7 us (30%)
  waiting for transfers between devices  3.88 us (5%)
  local copies, waits for them, and re-layouts  1.28 us (2%)
    all_to_all x1, starting transfers between devices, shards(): column = lax.all_to_all(payload, AX_Z, 0, 0, tiled=True)  20.6 us
    ppermute x3, starting transfers between devices, shifted(): lax.ppermute(block, axis, [(i - distance, i) for i in range(distance, siz...  14.7 us
    ppermute x7, starting transfers between devices, turned(): lax.ppermute(block, axis, [(i, (i + distance) % size) for i in range(size)])  11.7 us
    pallas_call x2, Pallas kernels, window(): pl.pallas_call(functools.partial(window_kernel, early), out_shape=window_...  7.92 us
    pallas_call x1, Pallas kernels, shards(): pl.pallas_call(far_kernel, out_shape=jax.ShapeDtypeStruct((tok_rows, inne...  6.14 us
    pallas_call x1, Pallas kernels, shards(): pl.pallas_call(project_kernel, out_shape=(jax.ShapeDtypeStruct((tok_rows,...  5.07 us
    all_to_all x1, waiting for transfers between devices, shards(): column = lax.all_to_all(payload, AX_Z, 0, 0, tiled=True)  3.86 us
    pallas_call x1, Pallas kernels, shards(): pl.pallas_call(medium_kernel, out_shape=jax.ShapeDtypeStruct((inner, tok_...  3.58 us
  transfers between devices with their start and end apart: 11, of which 1 were waited for; matrix products, arithmetic and copies ran while one was open for 0% of the time, Pallas kernels for 15%

profile of v4, /device:TPU:33, one launch (start us, length us, event | category | flops | bytes accessed | tf_op | source)
XLA Modules:
  0.0 75.1 jit_solution(1960597127855654369)
XLA Ops:
  0.0 0.0 copy-start.2
  0.0 5.1 %project.1 = (bf16[512,1536]{1,0:T(8,128)(2,1)}, bf16[160,1536]{1,0:T(8,128)(2,1)}, bf16[32,1536]{1,0:T(8,128)(2,1)}, bf16[384,128]{1,0:T(8,128)(2,1)}) custom-call(bf16[512,768]{1,0:T(8,128)(2,1)} %tok_hbm.5, bf16[768,2304]{1,0:T(8,128)(2,1)} %w_hbm.6, bf16[12,2,16]{2,1,0:T(2,128)(2,1)} %bitcast.16, bf16[12,2,256]{2,1,0:T(2,128)(2,1)} %bitcast.15), custom_call_target="tpu_custom_call" | custom-call | flops 4000000000 | bytes 4000000 | tf_op jit(solution)/shard_map/project/pallas_call | solution.py:415
  5.1 8.0 %collective-permute-start = (bf16[32,1536]{1,0:T(8,128)(2,1)}, bf16[32,1536]{1,0:T(8,128)(2,1)S(1)}, u32[]{:S(2)}, u32[]{:S(2)}) collective-permute-start(bf16[32,1536]{1,0:T(8,128)(2,1)} %get-tuple-element.22.med_ref), channel_id=1, source_target_pairs={{0,3},{1,4},{2,5},{3,6},{4,7},{5,8},{6,9},{7,10},{8,11},{9,12},{10... | collective-permute-start | bytes 294920 | tf_op jit(solution)/shard_map/ppermute | solution.py:384
  13.0 4.4 %collective-permute-start.1 = (bf16[32,1536]{1,0:T(8,128)(2,1)}, bf16[32,1536]{1,0:T(8,128)(2,1)S(1)}, u32[]{:S(2)}, u32[]{:S(2)}) collective-permute-start(bf16[32,1536]{1,0:T(8,128)(2,1)} %get-tuple-element.22.med_ref), channel_id=1, source_target_pairs={{0,2},{1,3},{2,4},{3,5},{4,6},{5,7},{6,8},{7,9},{8,10},{9,11},{10,... | collective-permute-start | bytes 294920 | tf_op jit(solution)/shard_map/ppermute | solution.py:384
  17.5 2.3 %collective-permute-start.2 = (bf16[160,1536]{1,0:T(8,128)(2,1)}, bf16[160,1536]{1,0:T(8,128)(2,1)S(1)}, u32[]{:S(2)}, u32[]{:S(2)}) collective-permute-start(bf16[160,1536]{1,0:T(8,128)(2,1)} %get-tuple-element.23), channel_id=1, source_target_pairs={{0,1},{1,2},{2,3},{3,4},{4,5},{5,6},{6,7},{7,8},{8,9},{9,10},{10,1... | collective-permute-start | bytes 1474568 | tf_op jit(solution)/shard_map/ppermute | solution.py:384
  19.8 20.6 %all-to-all-start = ((bf16[16,24,128]{2,1,0:T(8,128)(2,1)}), bf16[16,24,128]{2,1,0:T(8,128)(2,1)S(1)}, u32[]{:S(2)}, u32[]{:S(2)}) async-start(bf16[16,24,128]{2,1,0:T(8,128)(2,1)} %bitcast.14), calls=%async_computation | async-start | bytes 196608 | tf_op jit(solution)/shard_map/all_to_all | solution.py:470
  40.4 0.0 copy-done.2
  40.4 7.8 %window.2 = (bf16[512,768]{1,0:T(8,128)(2,1)S(1)}, f32[36,512]{1,0:T(8,128)S(1)}, f32[768,384]{1,0:T(8,128)}) custom-call(bf16[512,768]{1,0:T(8,128)(2,1)} %tok_hbm.5, bf16[768,2304]{1,0:T(8,128)(2,1)} %w_hbm.6, bf16[36,768]{1,0:T(8,128)(2,1)S(1)} %bitcast.11, bf16[512,1536]{1,0:T(8,128)(2,1)} %get-tuple-element.15.kv_hbm), custom_call_target="tpu_custom_call" | custom-call | flops 8000000000 | bytes 8000000 | tf_op jit(solution)/shard_map/window/pallas_call | solution.py:449
  48.2 3.9 %all-to-all-done = bf16[16,24,128]{2,1,0:T(8,128)(2,1)S(1)} async-done(((bf16[16,24,128]{2,1,0:T(8,128)(2,1)}), bf16[16,24,128]{2,1,0:T(8,128)(2,1)S(1)}, u32[]{:S(2)}, u32[]{:S(2)}) %all-to-all-start) | async-done | bytes 98336 | tf_op jit(solution)/shard_map/all_to_all | solution.py:470
  52.1 1.3 %collective-permute-start.3 = (bf16[384,128]{1,0:T(8,128)(2,1)S(1)}, bf16[384,128]{1,0:T(8,128)(2,1)S(1)}, u32[]{:S(2)}, u32[]{:S(2)}) collective-permute-start(bf16[384,128]{1,0:T(8,128)(2,1)S(1)} %bitcast.6), channel_id=1, source_target_pairs={{0,32},{32,64},{64,96},{96,0},{1,33},{33,65},{65,97},{97,1},{2,34}... | collective-permute-start | bytes 294920 | tf_op jit(solution)/shard_map/ppermute | solution.py:389
  53.4 2.7 %collective-permute-start.4 = (bf16[384,128]{1,0:T(8,128)(2,1)S(1)}, bf16[384,128]{1,0:T(8,128)(2,1)S(1)}, u32[]{:S(2)}, u32[]{:S(2)}) collective-permute-start(bf16[384,128]{1,0:T(8,128)(2,1)S(1)} %bitcast.7), channel_id=1, source_target_pairs={{0,64},{32,96},{64,0},{96,32},{1,65},{33,97},{65,1},{97,33},{2,66}... | collective-permute-start | bytes 294920 | tf_op jit(solution)/shard_map/ppermute | solution.py:389
  56.2 0.0 collective-permute-done.far3_ref
  56.2 1.0 %collective-permute-start.5 = (bf16[384,128]{1,0:T(8,128)(2,1)S(1)}, bf16[384,128]{1,0:T(8,128)(2,1)S(1)}, u32[]{:S(2)}, u32[]{:S(2)}) collective-permute-start(bf16[384,128]{1,0:T(8,128)(2,1)S(1)} %bitcast.8), channel_id=1, source_target_pairs={{0,96},{32,0},{64,32},{96,64},{1,97},{33,1},{65,33},{97,65},{2,98}... | collective-permute-start | bytes 294920 | tf_op jit(solution)/shard_map/ppermute | solution.py:389
  57.2 0.0 copy-start.1
  57.2 0.0 copy-start.3
  57.2 0.1 window.3
  57.3 0.0 collective-permute-done.1.far2_ref
  57.3 3.5 %collective-permute-start.6 = (bf16[384,128]{1,0:T(8,128)(2,1)S(1)}, bf16[384,128]{1,0:T(8,128)(2,1)S(1)}, u32[]{:S(2)}, u32[]{:S(2)}) collective-permute-start(bf16[384,128]{1,0:T(8,128)(2,1)S(1)} %bitcast.9), channel_id=1, source_target_pairs={{0,1},{1,0},{2,3},{3,2},{4,5},{5,4},{6,7},{7,6},{8,9},{9,8},{10,11... | collective-permute-start | bytes 294920 | tf_op jit(solution)/shard_map/ppermute | solution.py:389
  60.8 0.0 collective-permute-done.3.refs_1_
  60.8 0.2 collective-permute-start.7
  60.9 0.0 collective-permute-done.4.refs_2_
  61.0 1.9 %collective-permute-start.8 = (bf16[384,128]{1,0:T(8,128)(2,1)S(1)}, bf16[384,128]{1,0:T(8,128)(2,1)S(1)}, u32[]{:S(2)}, u32[]{:S(2)}) collective-permute-start(bf16[384,128]{1,0:T(8,128)(2,1)S(1)} %collective-permute-done.4.refs_2_), channel_id=1, source_target_pairs={{0,1},{1,0},{2,3},{3,2},{4,5},{5,4},{6,7},{7,6},{8,9},{9,8},{10,11... | collective-permute-start | bytes 294920 | tf_op jit(solution)/shard_map/ppermute | solution.py:389
  62.9 0.0 collective-permute-done.5.refs_3_
  62.9 1.0 %collective-permute-start.9 = (bf16[384,128]{1,0:T(8,128)(2,1)S(1)}, bf16[384,128]{1,0:T(8,128)(2,1)S(1)}, u32[]{:S(2)}, u32[]{:S(2)}) collective-permute-start(bf16[384,128]{1,0:T(8,128)(2,1)S(1)} %collective-permute-done.5.refs_3_), channel_id=1, source_target_pairs={{0,1},{1,0},{2,3},{3,2},{4,5},{5,4},{6,7},{7,6},{8,9},{9,8},{10,11... | collective-permute-start | bytes 294920 | tf_op jit(solution)/shard_map/ppermute | solution.py:389
  63.9 0.0 collective-permute-done.2.edge_ref
  63.9 0.0 copy-done.1
  63.9 0.0 copy-done.3
  63.9 0.0 copy-start.4
  63.9 1.3 %copy-done.4 = f32[768,384]{1,0:T(8,128)S(1)} copy-done((f32[768,384]{1,0:T(8,128)S(1)}, f32[768,384]{1,0:T(8,128)}, u32[]{:S(2)}) %copy-start.4) | copy-done | bytes 1179672
  65.1 0.0 copy-start
  65.1 3.6 %medium.1.mix_ref = f32[768,512]{1,0:T(8,128)S(1)} custom-call(bf16[512,768]{1,0:T(8,128)(2,1)S(1)} %get-tuple-element.19.q_hbm, f32[36,512]{1,0:T(8,128)S(1)} %get-tuple-element.20.gate_hbm, f32[768,384]{1,0:T(8,128)S(1)} %copy-done.4, bf16[512,1536]{1,0:T(8,128)(2,1)} %get-tuple-element.15.kv_hbm, bf16[32,1536]{1,0:T(8,128)(2,1)S(1)} %collective-permute-done.far3_ref, ...), custom_call_target="tpu_custom_call" | custom-call | flops 4000000000 | bytes 4000000 | tf_op jit(solution)/shard_map/medium/pallas_call | solution.py:475
  68.7 0.0 collective-permute-done.6.refs_4_
  68.7 0.0 collective-permute-done.7.refs_5_
  68.8 0.0 collective-permute-done.8.refs_6_
  68.8 0.0 collective-permute-done.9.refs_7_
  68.8 0.0 copy-done
  68.8 6.1 %far.1 = bf16[512,768]{1,0:T(8,128)(2,1)} custom-call(bf16[512,768]{1,0:T(8,128)(2,1)S(1)} %get-tuple-element.19.q_hbm, f32[36,512]{1,0:T(8,128)S(1)} %get-tuple-element.20.gate_hbm, f32[768,512]{1,0:T(8,128)S(1)} %medium.1.mix_ref, bf16[768,768]{1,0:T(8,128)(2,1)S(1)} %copy-done, bf16[384,128]{1,0:T(8,128)(2,1)S(1)} %bitcast.10, ...), custom_call_target="tpu_custom_call" | custom-call | flops 4000000000 | bytes 4000000 | tf_op jit(solution)/shard_map/far/pallas_call | solution.py:493
Async XLA Ops:
  0.0 40.4 %copy-start.2 = (bf16[768,36]{0,1:T(8,128)(2,1)S(1)}, bf16[768,36]{0,1:T(8,128)(2,1)}, u32[]{:S(2)}) copy-start(bf16[768,36]{0,1:T(8,128)(2,1)} %param.9) | copy-start | bytes 165892
  5.1 51.1 %collective-permute-start = (bf16[32,1536]{1,0:T(8,128)(2,1)}, bf16[32,1536]{1,0:T(8,128)(2,1)S(1)}, u32[]{:S(2)}, u32[]{:S(2)}) collective-permute-start(bf16[32,1536]{1,0:T(8,128)(2,1)} %get-tuple-element.22.med_ref), channel_id=1, source_target_pairs={{0,3},{1,4},{2,5},{3,6},{4,7},{5,8},{6,9},{7,10},{8,11},{9,12},{10... | collective-permute-start | bytes 294920 | tf_op jit(solution)/shard_map/ppermute | solution.py:384
  13.0 44.2 %collective-permute-start.1 = (bf16[32,1536]{1,0:T(8,128)(2,1)}, bf16[32,1536]{1,0:T(8,128)(2,1)S(1)}, u32[]{:S(2)}, u32[]{:S(2)}) collective-permute-start(bf16[32,1536]{1,0:T(8,128)(2,1)} %get-tuple-element.22.med_ref), channel_id=1, source_target_pairs={{0,2},{1,3},{2,4},{3,5},{4,6},{5,7},{6,8},{7,9},{8,10},{9,11},{10,... | collective-permute-start | bytes 294920 | tf_op jit(solution)/shard_map/ppermute | solution.py:384
  17.5 46.4 %collective-permute-start.2 = (bf16[160,1536]{1,0:T(8,128)(2,1)}, bf16[160,1536]{1,0:T(8,128)(2,1)S(1)}, u32[]{:S(2)}, u32[]{:S(2)}) collective-permute-start(bf16[160,1536]{1,0:T(8,128)(2,1)} %get-tuple-element.23), channel_id=1, source_target_pairs={{0,1},{1,2},{2,3},{3,4},{4,5},{5,6},{6,7},{7,8},{8,9},{9,10},{10,1... | collective-permute-start | bytes 1474568 | tf_op jit(solution)/shard_map/ppermute | solution.py:384
  19.8 32.3 %all-to-all-start = ((bf16[16,24,128]{2,1,0:T(8,128)(2,1)}), bf16[16,24,128]{2,1,0:T(8,128)(2,1)S(1)}, u32[]{:S(2)}, u32[]{:S(2)}) async-start(bf16[16,24,128]{2,1,0:T(8,128)(2,1)} %bitcast.14), calls=%async_computation | async-start | bytes 196608 | tf_op jit(solution)/shard_map/all_to_all | solution.py:470
  52.1 8.7 %collective-permute-start.3 = (bf16[384,128]{1,0:T(8,128)(2,1)S(1)}, bf16[384,128]{1,0:T(8,128)(2,1)S(1)}, u32[]{:S(2)}, u32[]{:S(2)}) collective-permute-start(bf16[384,128]{1,0:T(8,128)(2,1)S(1)} %bitcast.6), channel_id=1, source_target_pairs={{0,32},{32,64},{64,96},{96,0},{1,33},{33,65},{65,97},{97,1},{2,34}... | collective-permute-start | bytes 294920 | tf_op jit(solution)/shard_map/ppermute | solution.py:389
  53.4 7.5 %collective-permute-start.4 = (bf16[384,128]{1,0:T(8,128)(2,1)S(1)}, bf16[384,128]{1,0:T(8,128)(2,1)S(1)}, u32[]{:S(2)}, u32[]{:S(2)}) collective-permute-start(bf16[384,128]{1,0:T(8,128)(2,1)S(1)} %bitcast.7), channel_id=1, source_target_pairs={{0,64},{32,96},{64,0},{96,32},{1,65},{33,97},{65,1},{97,33},{2,66}... | collective-permute-start | bytes 294920 | tf_op jit(solution)/shard_map/ppermute | solution.py:389
  56.2 6.7 %collective-permute-start.5 = (bf16[384,128]{1,0:T(8,128)(2,1)S(1)}, bf16[384,128]{1,0:T(8,128)(2,1)S(1)}, u32[]{:S(2)}, u32[]{:S(2)}) collective-permute-start(bf16[384,128]{1,0:T(8,128)(2,1)S(1)} %bitcast.8), channel_id=1, source_target_pairs={{0,96},{32,0},{64,32},{96,64},{1,97},{33,1},{65,33},{97,65},{2,98}... | collective-permute-start | bytes 294920 | tf_op jit(solution)/shard_map/ppermute | solution.py:389
  57.2 6.7 %copy-start.1 = (bf16[32,1536]{1,0:T(8,128)(2,1)S(1)}, bf16[32,1536]{1,0:T(8,128)(2,1)}, u32[]{:S(2)}) copy-start(bf16[32,1536]{1,0:T(8,128)(2,1)} %get-tuple-element.22.med_ref) | copy-start | bytes 294916
  57.2 6.7 %copy-start.3 = (s32[4096]{0:T(1024)S(1)}, s32[4096]{0:T(1024)}, u32[]{:S(2)}) copy-start(s32[4096]{0:T(1024)} %param.13) | copy-start | bytes 49156
  57.3 11.5 %collective-permute-start.6 = (bf16[384,128]{1,0:T(8,128)(2,1)S(1)}, bf16[384,128]{1,0:T(8,128)(2,1)S(1)}, u32[]{:S(2)}, u32[]{:S(2)}) collective-permute-start(bf16[384,128]{1,0:T(8,128)(2,1)S(1)} %bitcast.9), channel_id=1, source_target_pairs={{0,1},{1,0},{2,3},{3,2},{4,5},{5,4},{6,7},{7,6},{8,9},{9,8},{10,11... | collective-permute-start | bytes 294920 | tf_op jit(solution)/shard_map/ppermute | solution.py:389
  60.8 8.0 %collective-permute-start.7 = (bf16[384,128]{1,0:T(8,128)(2,1)S(1)}, bf16[384,128]{1,0:T(8,128)(2,1)S(1)}, u32[]{:S(2)}, u32[]{:S(2)}) collective-permute-start(bf16[384,128]{1,0:T(8,128)(2,1)S(1)} %collective-permute-done.3.refs_1_), channel_id=1, source_target_pairs={{0,1},{1,0},{2,3},{3,2},{4,5},{5,4},{6,7},{7,6},{8,9},{9,8},{10,11... | collective-permute-start | bytes 294920 | tf_op jit(solution)/shard_map/ppermute | solution.py:389
  61.0 7.8 %collective-permute-start.8 = (bf16[384,128]{1,0:T(8,128)(2,1)S(1)}, bf16[384,128]{1,0:T(8,128)(2,1)S(1)}, u32[]{:S(2)}, u32[]{:S(2)}) collective-permute-start(bf16[384,128]{1,0:T(8,128)(2,1)S(1)} %collective-permute-done.4.refs_2_), channel_id=1, source_target_pairs={{0,1},{1,0},{2,3},{3,2},{4,5},{5,4},{6,7},{7,6},{8,9},{9,8},{10,11... | collective-permute-start | bytes 294920 | tf_op jit(solution)/shard_map/ppermute | solution.py:389
  62.9 5.9 %collective-permute-start.9 = (bf16[384,128]{1,0:T(8,128)(2,1)S(1)}, bf16[384,128]{1,0:T(8,128)(2,1)S(1)}, u32[]{:S(2)}, u32[]{:S(2)}) collective-permute-start(bf16[384,128]{1,0:T(8,128)(2,1)S(1)} %collective-permute-done.5.refs_3_), channel_id=1, source_target_pairs={{0,1},{1,0},{2,3},{3,2},{4,5},{5,4},{6,7},{7,6},{8,9},{9,8},{10,11... | collective-permute-start | bytes 294920 | tf_op jit(solution)/shard_map/ppermute | solution.py:389
  63.9 1.3 %copy-start.4 = (f32[768,384]{1,0:T(8,128)S(1)}, f32[768,384]{1,0:T(8,128)}, u32[]{:S(2)}) copy-start(f32[768,384]{1,0:T(8,128)} %get-tuple-element.21.old_hbm) | copy-start | bytes 3538948
  65.1 3.6 %copy-start = (bf16[768,768]{1,0:T(8,128)(2,1)S(1)}, bf16[768,768]{1,0:T(8,128)(2,1)}, u32[]{:S(2)}) copy-start(bf16[768,768]{1,0:T(8,128)(2,1)} %w_hbm.7) | copy-start | bytes 3538948
